TPU v7x, 32 devices: a whole 2x2x4 slice. The times are simulated.
32 devices in a mesh: zero: 4 (over x, core), width: 8 (over z, y).
Axes of the slice: x: 2, y: 2, z: 4, core: 2. Of those that a mesh axis runs over, the one named last changes fastest.
Arguments:
- weight_query: float32 [8192, 8192], P('zero', 'width'), may hold values from -0.09375 to 0.09375
- smooth_query: float32 [8192, 8192], P('zero', 'width'), may hold values from -0.0625 to 0.0625
- weight_key: float32 [8192, 512], P('zero', 'width'), may hold values from -0.09375 to 0.09375
- smooth_key: float32 [8192, 512], P('zero', 'width'), may hold values from -0.0625 to 0.0625
- weight_value: float32 [8192, 512], P('zero', 'width'), may hold values from -0.09375 to 0.09375
- smooth_value: float32 [8192, 512], P('zero', 'width'), may hold values from -0.0625 to 0.0625
- norm_train: float32 [8192], P(('zero', 'width')), may hold values from 0.25 to 1.75
- norm_step: float32 [8192], P(('zero', 'width')), may hold values from -0.3 to 0.3
Outputs:
- final_query: bfloat16 [8192, 8192], P(None, 'width')
- final_key: bfloat16 [8192, 512], P(None, 'width')
- final_value: bfloat16 [8192, 512], P(None, 'width')
- factor_query: float32 [8192], P('width')
- factor_key: float32 [512], P('width')
- factor_value: float32 [512], P('width')
- serve_norm: bfloat16 [8192], replicated
- result_query: float32 [8192, 8192], P('zero', 'width')
- result_key: float32 [8192, 512], P('zero', 'width')
- result_value: float32 [8192, 512], P('zero', 'width')
All inputs are finite; a program needn't handle non-finite values. Where the computation divides by a largest or mean magnitude, that divisor is 1e-20 or more.
Results may differ from a plain program's by a relative error of at most 0.001.
Values may be sent and summed in bfloat16 or wider, within the bound.
No kernel may reach another device: no remote copies, remote signals or barrier semaphores. Data moves between devices by JAX's collectives and lax.ppermute only.
A program may use at most 128 MiB of HBM per device.

v0:
```python
import functools

import jax
import jax.numpy as jnp
from jax import lax
from jax.experimental import pallas as pl
from jax.experimental.pallas import tpu as pltpu
from jax.sharding import PartitionSpec as P


KEEP = 0.7
LANES = 128

VMEM = pl.BlockSpec(memory_space=pltpu.VMEM)
SMEM = pl.BlockSpec(memory_space=pltpu.SMEM)
HBM = pl.BlockSpec(memory_space=pl.ANY)


def cost(flops, bytes_accessed):
    return pl.CostEstimate(flops=flops, bytes_accessed=bytes_accessed, transcendentals=0)


def round_up(value, step):
    return -(-value // step) * step


def average(smooth, weight):
    return KEEP * smooth + (1.0 - KEEP) * weight


def lane_sum(block):
    total = block[:, :LANES]
    for at in range(LANES, block.shape[1], LANES):
        total = total + block[:, at : at + LANES]
    return total


def row_sum(block):
    return jnp.sum(block.reshape(block.shape[0] // 8, 8, block.shape[1]), axis=0)


def narrow_kernel(places, wq, sq, wk, sk, wv, sv, nt, ns, rk, rv, message, sum_q, sum_kv):
    step, steps = pl.program_id(0), pl.num_programs(0)
    heads = wk.shape[0]

    @pl.when(step == 0)
    def _():
        sum_q[...] = jnp.zeros_like(sum_q)
        sum_kv[...] = jnp.zeros_like(sum_kv)

    sum_q[...] += row_sum(jnp.abs(average(sq[...], wq[...])))
    for at, (w, s, r) in enumerate(((wk, sk, rk), (wv, sv, rv))):
        new = average(s[...], w[...])
        r[...] = new
        sum_kv[at * heads : (at + 1) * heads, :] += lane_sum(jnp.abs(new))

    @pl.when(step == steps - 1)
    def _():
        place_kv, place_norm = places
        message[...] = jnp.zeros_like(message)
        message[:, : sum_q.shape[1]] = jnp.sum(sum_q[...], axis=0, keepdims=True)
        message[:, place_kv : place_kv + 2 * heads] = jnp.sum(
            sum_kv[...].T, axis=0, keepdims=True
        )
        gain = (nt[...] + ns[...]).astype(jnp.bfloat16)
        message[:, place_norm : place_norm + gain.shape[1]] = gain.astype(jnp.float32)


def tree(pieces):
    while len(pieces) > 1:
        pieces = [a + b for a, b in zip(pieces[::2], pieces[1::2])]
    return pieces[0]


def first_kernel(places, columns, gain, count, me, rk, rv, *refs):
    n = len(refs) - 5
    messages, (own, inv_q, factor_k, factor_v, norms) = refs[:n], refs[n:]
    place_kv, place_norm = places
    heads = rk.shape[0]
    pieces = [m[...] for m in messages]
    for distance, piece in enumerate(pieces):
        norms[pl.ds(me[0] ^ distance, 1), :] = piece[:, place_norm : place_norm + gain]
    total = tree(pieces) / count
    inv_q[...] = 1.0 / total[:, :columns]
    of_kv = total[:, place_kv : place_kv + 2 * heads]
    factor_k[...] = of_kv[:, :heads]
    factor_v[...] = of_kv[:, heads:]
    inv = jnp.broadcast_to(1.0 / of_kv, (LANES, 2 * heads)).T
    for at, r in enumerate((rk, rv)):
        scale = inv[at * heads : (at + 1) * heads, :]
        for lane in range(0, rk.shape[1], LANES):
            own[at * heads : (at + 1) * heads, lane : lane + LANES] = (
                r[:, lane : lane + LANES] * scale
            ).astype(jnp.bfloat16)


def second_kernel(wq, sq, inv, *owns):
    first = 0
    for own in owns:
        rows = pl.ds(first, own.shape[0])
        own[...] = (average(sq[rows, :], wq[rows, :]) * inv[...]).astype(jnp.bfloat16)
        first += own.shape[0]


def average_kernel(wq, sq, rq, message, sum_q):
    step, steps = pl.program_id(0), pl.num_programs(0)

    @pl.when(step == 0)
    def _():
        sum_q[...] = jnp.zeros_like(sum_q)

    new = average(sq[...], wq[...])
    rq[...] = new
    sum_q[...] += row_sum(jnp.abs(new))

    @pl.when(step == steps - 1)
    def _():
        message[...] = jnp.sum(sum_q[...], axis=0, keepdims=True)


def third_kernel(columns, count, rq, *refs):
    messages, (own, inv, factor) = refs[:-3], refs[-3:]
    total = tree([m[...] for m in messages]) / count
    factor[...] = total
    scale = 1.0 / total[:, columns:]
    inv[...] = scale
    own[...] = (rq[:, columns:] * scale).astype(jnp.bfloat16)


def fourth_kernel(inv, *refs):
    half = len(refs) // 2
    for source, own in zip(refs[:half], refs[half:]):
        columns = source.shape[1] - own.shape[1]
        own[...] = (source[:, columns:] * inv[...]).astype(jnp.bfloat16)


def place_kernel(plan, rows, kv, whole, me, *refs):
    pieces, refs = refs[: len(plan)], refs[len(plan) :]
    kv_pieces, refs = refs[:kv], refs[kv + (1 if whole else 0) :]
    out, kv_outs, sems = refs[0], refs[1:-1], refs[-1]
    copies = []

    def move(source, target):
        copies.append(pltpu.make_async_copy(source, target, sems.at[len(copies)]))
        copies[-1].start()

    for piece, (distance, first, column) in zip(pieces, plan):
        start = pl.multiple_of((me[0] ^ distance) * rows + first, 16)
        move(piece, out.at[pl.ds(start, piece.shape[0]), pl.ds(column, piece.shape[1])])
    for distance, piece in enumerate(kv_pieces):
        heads = piece.shape[0] // 2
        start = pl.multiple_of((me[0] ^ distance) * rows, LANES)
        for at, target in enumerate(kv_outs):
            move(
                piece.at[at * heads : (at + 1) * heads, :],
                target.at[:, pl.ds(start, rows)],
            )
    for copy in copies:
        copy.wait()


CUTS = (4,) * 7 + (2, 1, 1)


def on_device(n, groups, wq, sq, wk, sk, wv, sv, norm_train, norm_step):
    rows, width = wq.shape
    heads = wk.shape[1]
    gain = norm_train.shape[0]
    f32, bf16 = jnp.float32, jnp.bfloat16
    shaped = jax.ShapeDtypeStruct
    me = lax.axis_index("zero").astype(jnp.int32).reshape(1)

    def swap(array, distance, axis="zero", size=n):
        return lax.ppermute(array, axis, [(i, i ^ distance) for i in range(size)])

    def gather(piece):
        found = [piece, swap(piece, 1)]
        for distance in range(2, n, 2):
            far = swap(piece, distance)
            found += [far, swap(far, 1)]
        return found

    def exchange(piece):
        found = [piece]
        for distance in range(1, n):
            found.append(swap(piece, distance))
        return found

    once = lambda shape: pl.BlockSpec(shape, lambda i: (0, 0))
    full = lambda a: once(a.shape)

    columns = max(LANES, width // 8)
    place_kv = columns
    place_norm = place_kv + round_up(2 * heads, LANES)
    places = (place_kv, place_norm)
    length = place_norm + round_up(gain, LANES)
    block = rows // 4
    of_q = pl.BlockSpec((block, columns), lambda i: (i, 0))
    of_kv = pl.BlockSpec((heads, block), lambda i: (0, i))
    rk, rv, message = pl.pallas_call(
        functools.partial(narrow_kernel, places),
        grid=(rows // block,),
        out_shape=(
            shaped((heads, rows), f32),
            shaped((heads, rows), f32),
            shaped((1, length), f32),
        ),
        in_specs=[of_q] * 2 + [of_kv] * 4 + [once((1, gain))] * 2,
        out_specs=[of_kv, of_kv, once((1, length))],
        scratch_shapes=[pltpu.VMEM((8, columns), f32), pltpu.VMEM((2 * heads, LANES), f32)],
        cost_estimate=cost(rows * 2 * heads * 8, rows * 2 * heads * 16),
        name="narrow",
    )(wq, sq, wk.T, sk.T, wv.T, sv.T, norm_train[None], norm_step[None])
    messages = exchange(message)
    own_kv, inv_a, factor_k, factor_v, norms = pl.pallas_call(
        functools.partial(first_kernel, places, columns, gain, n * rows),
        grid=(1,),
        out_shape=(
            shaped((2 * heads, rows), bf16),
            shaped((1, columns), f32),
            shaped((1, heads), f32),
            shaped((1, heads), f32),
            shaped((n, gain), f32),
        ),
        in_specs=[SMEM] + [full(rk)] * 2 + [full(message)] * n,
        out_specs=[
            once((2 * heads, rows)),
            once((1, columns)),
            once((1, heads)),
            once((1, heads)),
            once((n, gain)),
        ],
        cost_estimate=cost(rows * heads * 8, rows * heads * 12),
        name="first",
    )(me, rk, rv, *messages)
    part = shaped((rows // 2, columns), bf16)
    own_a = pl.pallas_call(
        second_kernel,
        grid=(1,),
        out_shape=(part,) * 2,
        in_specs=[once((rows, columns))] * 2 + [full(inv_a)],
        out_specs=[full(part)] * 2,
        cost_estimate=cost(rows * columns * 8, rows * columns * 10),
        name="second",
    )(wq, sq, inv_a)
    found_kv = gather(own_kv)
    found_a = [gather(piece) for piece in own_a]

    block = min(rows, 256)
    of_q = pl.BlockSpec((block, width), lambda i: (i, 0))
    rq, message_q = pl.pallas_call(
        average_kernel,
        grid=(rows // block,),
        out_shape=(shaped((rows, width), f32), shaped((1, width), f32)),
        in_specs=[of_q] * 2,
        out_specs=[of_q, once((1, width))],
        scratch_shapes=[pltpu.VMEM((8, width), f32)],
        cost_estimate=cost(rows * width * 8, rows * width * 12),
        name="average",
    )(wq, sq)
    messages_q = exchange(message_q)

    unit = rows // sum(CUTS)
    firsts = [sum(CUTS[:at]) for at in range(len(CUTS))]
    rest = width - columns
    rows_of = lambda at: pl.BlockSpec(
        (CUTS[at] * unit, width), lambda i: (firsts[at] // CUTS[at], 0)
    )
    narrow = [shaped((c * unit, rest), bf16) for c in CUTS]
    own0, inv, factor_q = pl.pallas_call(
        functools.partial(third_kernel, columns, n * rows),
        grid=(1,),
        out_shape=(narrow[0], shaped((1, rest), f32), shaped((1, width), f32)),
        in_specs=[rows_of(0)] + [full(message_q)] * n,
        out_specs=[full(narrow[0]), once((1, rest)), once((1, width))],
        cost_estimate=cost(narrow[0].size * 8, narrow[0].size * 6),
        name="third",
    )(rq, *messages_q)
    others = range(1, len(CUTS))
    owns = pl.pallas_call(
        fourth_kernel,
        grid=(1,),
        out_shape=narrow[1:],
        in_specs=[full(inv)] + [rows_of(at) for at in others],
        out_specs=[full(narrow[at]) for at in others],
        cost_estimate=cost(rows * rest * 8, rows * rest * 6),
        name="fourth",
    )(inv, *[rq for _ in others])
    found = [gather(piece) for piece in [own0, *owns]]

    whole = shaped((n * rows, width), bf16)
    whole_kv = shaped((heads, n * rows), bf16)

    def place(jobs, kv=(), final=None):
        pieces = [job[0] for job in jobs]
        operands = [*pieces, *kv]
        moved = sum(p.size for p in operands) * 2
        return pl.pallas_call(
            functools.partial(
                place_kernel, [job[1:] for job in jobs], rows, len(kv), final is not None
            ),
            grid=(1,),
            out_shape=[whole] + [whole_kv] * (2 if kv else 0),
            in_specs=[SMEM]
            + [full(p) for p in operands]
            + ([HBM] if final is not None else []),
            out_specs=[HBM] * (3 if kv else 1),
            scratch_shapes=[pltpu.SemaphoreType.DMA((len(jobs) + 2 * len(kv),))],
            input_output_aliases={} if final is None else {1 + len(operands): 0},
            cost_estimate=cost(moved * 4, 2 * moved),
        )(me, *operands, *(() if final is None else (final,)))

    def jobs(chunks, distances):
        return [
            (found[at][d], d, firsts[at] * unit, columns) for at in chunks for d in distances
        ]

    near, far = range(2), range(2, n)
    final_q, final_k, final_v = place(
        [(found_a[at][d], d, at * rows // 2, 0) for at in range(2) for d in range(n)], found_kv
    )
    for chunks, distances in (
        (range(len(CUTS)), near),
        ((0, 1, 2), far),
        ((3, 4), far),
        ((5,), far),
        ((6,), far),
        ((7,), far),
        ((8, 9), far),
    ):
        (final_q,) = place(jobs(chunks, distances), (), final_q)

    gains = norms.astype(jnp.bfloat16).reshape(n, 1, gain)
    spot = lax.axis_index("width")
    bit = 1
    while bit < groups:
        other = swap(gains, bit, "width", groups)
        low = (spot & bit) == 0
        gains = jnp.concatenate(
            [jnp.where(low, gains, other), jnp.where(low, other, gains)], axis=1
        )
        bit *= 2

    return (
        final_q,
        final_k.T,
        final_v.T,
        factor_q.reshape(width),
        factor_k.reshape(heads),
        factor_v.reshape(heads),
        gains.reshape(n * groups * gain),
        rq,
        rk.T,
        rv.T,
    )


def solution(mesh):
    split, columns, lone = P("zero", "width"), P(None, "width"), P("width")
    vector = P(("zero", "width"))
    n = mesh.shape["zero"]

    def body(*args):
        return on_device(n, mesh.shape["width"], *args)

    return jax.shard_map(
        body,
        mesh=mesh,
        in_specs=(split,) * 6 + (vector,) * 2,
        out_specs=(columns,) * 3 + (lone,) * 3 + (P(),) + (split,) * 3,
        check_vma=False,
    )
```

profile of v0, /device:TPU:0, one launch (start us, length us, event | category | flops | bytes accessed | tf_op | source)
XLA Modules:
  0.0 183.3 jit_solution(10420480193965807324)
XLA Ops:
  0.6 4.3 %narrow.1 = (f32[64,2048]{1,0:T(8,128)}, f32[64,2048]{1,0:T(8,128)}, f32[1,512]{1,0:T(1,128)}) custom-call(f32[2048,1024]{1,0:T(8,128)} %wq.5, f32[2048,1024]{1,0:T(8,128)} %sq.5, f32[64,2048]{1,0:T(8,128)} %bitcast.22, f32[64,2048]{1,0:T(8,128)} %bitcast.23, f32[64,2048]{1,0:T(8,128)} %bitcast.24, f32[64,2048]{1,0:T(8,128)} %bitcast.25, f32[1,256]{1,0:T(1,128)} %bitcast.30, ...), custom_call_target="tpu_custom_call" | custom-call | flops 2097152 | bytes 4194304 | tf_op jit(solution)/shard_map/narrow/pallas_call | solution.py:200
  5.5 2.6 %collective-permute-start.34 = (f32[1,512]{1,0:T(1,128)}, f32[1,512]{1,0:T(1,128)S(1)}, u32[]{:S(2)}, u32[]{:S(2)}) collective-permute-start(f32[1,512]{1,0:T(1,128)} %get-tuple-element.52.refs_0_), channel_id=1, source_target_pairs={{0,16},{8,24},{16,0},{24,8},{1,17},{9,25},{17,1},{25,9},{2,18},{10... | collective-permute-start | bytes 6152 | tf_op jit(solution)/shard_map/ppermute | solution.py:174
  8.1 1.7 collective-permute-done.34.refs_2_
  9.8 1.4 collective-permute-done.35.refs_3_
  11.8 2.2 %first.1 = (bf16[128,2048]{1,0:T(8,128)(2,1)}, f32[1,128]{1,0:T(1,128)}, f32[1,64]{1,0:T(1,128)}, f32[1,64]{1,0:T(1,128)}, f32[4,256]{1,0:T(4,128)}) custom-call(s32[1]{0:T(128)} %bitcast.me, f32[64,2048]{1,0:T(8,128)} %get-tuple-element.50.rk, f32[64,2048]{1,0:T(8,128)} %get-tuple-element.51.rv, f32[1,512]{1,0:T(1,128)} %get-tuple-element.52.refs_0_, ...), custom_call_target="tpu_custom_call" | custom-call | flops 1048576 | bytes 1572864 | tf_op jit(solution)/shard_map/first/pallas_call | solution.py:215
  14.0 0.8 convert_bitcast_fusion
  14.8 1.5 collective-permute-start.45
  16.3 11.2 %average.1 = (f32[2048,1024]{1,0:T(8,128)}, f32[1,1024]{1,0:T(1,128)}) custom-call(f32[2048,1024]{1,0:T(8,128)} %wq.5, f32[2048,1024]{1,0:T(8,128)} %sq.5), custom_call_target="tpu_custom_call" | custom-call | flops 16777216 | bytes 25165824 | tf_op jit(solution)/shard_map/average/pallas_call | solution.py:251
  28.1 1.2 collective-permute-start.2
  29.4 1.6 collective-permute-start.46
  32.0 2.1 %third.1 = (bf16[256,896]{1,0:T(8,128)(2,1)}, f32[1,896]{1,0:T(1,128)}, f32[1,1024]{1,0:T(1,128)}) custom-call(f32[2048,1024]{1,0:T(8,128)} %get-tuple-element.34.rq.refs_0_.refs_1_.refs_2_.refs_3_.refs_4_.refs_5_.refs_6_.refs_7_.refs_8_, f32[1,1024]{1,0:T(1,128)} %get-tuple-element.38.refs_0_, f32[1,1024]{1,0:T(1,128)} %copy-done.34, f32[1,1024]{1,0:T(1,128)} %copy-done.35, ...), custom_call_target="tpu_custom_call" | custom-call | flops 1835008 | bytes 1376256 | tf_op jit(solution)/shard_map/third/pallas_call | solution.py:270
  34.1 4.8 %fourth.1 = (bf16[256,896]{1,0:T(8,128)(2,1)}, bf16[256,896]{1,0:T(8,128)(2,1)}, bf16[256,896]{1,0:T(8,128)(2,1)}, bf16[256,896]{1,0:T(8,128)(2,1)}, bf16[256,89...) custom-call(f32[1,896]{1,0:T(1,128)} %get-tuple-element.39.inv, ...), custom_call_target="tpu_custom_call" | custom-call | flops 14680064 | bytes 11010048 | tf_op jit(solution)/shard_map/fourth/pallas_call | solution.py:280
  39.2 1.4 collective-permute-start.7
  41.2 2.7 %collective-permute-start.47 = (bf16[4,4,256]{2,0,1:T(4,128)(2,1)S(1)}, bf16[4,4,256]{2,0,1:T(4,128)(2,1)S(1)}, u32[]{:S(2)}, u32[]{:S(2)}) collective-permute-start(bf16[4,4,256]{2,0,1:T(4,128)(2,1)S(1)} %pad_maximum_fusion.1), channel_id=1, source_target_pairs={{0,4},{1,5},{2,6},{3,7},{4,0},{5,1},{6,2},{7,3},{8,12},{9,13},{10,... | collective-permute-start | bytes 24584 | tf_op jit(solution)/shard_map/ppermute | solution.py:174
  43.8 2.0 %collective-permute-done.47 = bf16[4,4,256]{2,0,1:T(4,128)(2,1)S(1)} collective-permute-done((bf16[4,4,256]{2,0,1:T(4,128)(2,1)S(1)}, bf16[4,4,256]{2,0,1:T(4,128)(2,1)S(1)}, u32[]{:S(2)}, u32[]{:S(2)}) %collective-permute-start.47) | collective-permute-done | bytes 8224 | tf_op jit(solution)/shard_map/ppermute | solution.py:174
  46.4 1.4 collective-permute-start.5
  47.8 0.6 copy-done.32
  48.5 2.5 %second.1 = (bf16[1024,128]{1,0:T(8,128)(2,1)}, bf16[1024,128]{1,0:T(8,128)(2,1)}) custom-call(f32[2048,1024]{1,0:T(8,128)} %wq.5, f32[2048,1024]{1,0:T(8,128)} %sq.5, f32[1,128]{1,0:T(1,128)} %get-tuple-element.53.inv), custom_call_target="tpu_custom_call" | custom-call | flops 2097152 | bytes 2621440 | tf_op jit(solution)/shard_map/second/pallas_call | solution.py:237
  51.3 1.2 collective-permute-start.37
  52.5 1.2 collective-permute-start.40
  54.2 6.5 %collective-permute-done.37.refs_2_ = bf16[1024,128]{1,0:T(8,128)(2,1)S(1)} collective-permute-done((bf16[1024,128]{1,0:T(8,128)(2,1)}, bf16[1024,128]{1,0:T(8,128)(2,1)S(1)}, u32[]{:S(2)}, u32[]{:S(2)}) %collective-permute-start.37) | collective-permute-done | bytes 262176 | tf_op jit(solution)/shard_map/ppermute | solution.py:174
  60.7 4.9 %collective-permute-done.40.refs_6_ = bf16[1024,128]{1,0:T(8,128)(2,1)S(1)} collective-permute-done((bf16[1024,128]{1,0:T(8,128)(2,1)}, bf16[1024,128]{1,0:T(8,128)(2,1)S(1)}, u32[]{:S(2)}, u32[]{:S(2)}) %collective-permute-start.40) | collective-permute-done | bytes 262176 | tf_op jit(solution)/shard_map/ppermute | solution.py:174
  65.6 0.7 copy-done.25
  66.7 0.7 copy-done.26
  68.1 0.7 collective-permute-start.19
  68.8 1.4 collective-permute-start.21
  70.2 0.6 collective-permute-start.17
  70.9 1.4 collective-permute-start.13
  72.3 0.6 collective-permute-start.15
  72.9 8.7 %collective-permute-done.19.refs_2_ = bf16[256,896]{1,0:T(8,128)(2,1)S(1)} collective-permute-done((bf16[256,896]{1,0:T(8,128)(2,1)S(1)}, bf16[256,896]{1,0:T(8,128)(2,1)S(1)}, u32[]{:S(2)}, u32[]{:S(2)}) %collective-permute-start.19) | collective-permute-done | bytes 458784 | tf_op jit(solution)/shard_map/ppermute | solution.py:174
  82.2 9.2 %collective-permute-done.21.refs_4_ = bf16[256,896]{1,0:T(8,128)(2,1)S(1)} collective-permute-done((bf16[256,896]{1,0:T(8,128)(2,1)S(1)}, bf16[256,896]{1,0:T(8,128)(2,1)S(1)}, u32[]{:S(2)}, u32[]{:S(2)}) %collective-permute-start.21) | collective-permute-done | bytes 458784 | tf_op jit(solution)/shard_map/ppermute | solution.py:174
  91.4 0.6 collective-permute-start.43
  92.1 9.2 %collective-permute-done.17.refs_0_ = bf16[256,896]{1,0:T(8,128)(2,1)S(1)} collective-permute-done((bf16[256,896]{1,0:T(8,128)(2,1)S(1)}, bf16[256,896]{1,0:T(8,128)(2,1)S(1)}, u32[]{:S(2)}, u32[]{:S(2)}) %collective-permute-start.17) | collective-permute-done | bytes 458784 | tf_op jit(solution)/shard_map/ppermute | solution.py:174
  101.3 9.9 %collective-permute-done.13.refs_0_ = bf16[256,896]{1,0:T(8,128)(2,1)} collective-permute-done((bf16[256,896]{1,0:T(8,128)(2,1)S(1)}, bf16[256,896]{1,0:T(8,128)(2,1)}, u32[]{:S(2)}, u32[]{:S(2)}) %collective-permute-start.13) | collective-permute-done | bytes 458784 | tf_op jit(solution)/shard_map/ppermute | solution.py:174
  111.2 0.6 collective-permute-start.9
  111.8 9.2 %collective-permute-done.15.refs_2_ = bf16[256,896]{1,0:T(8,128)(2,1)} collective-permute-done((bf16[256,896]{1,0:T(8,128)(2,1)}, bf16[256,896]{1,0:T(8,128)(2,1)}, u32[]{:S(2)}, u32[]{:S(2)}) %collective-permute-start.15) | collective-permute-done | bytes 458784 | tf_op jit(solution)/shard_map/ppermute | solution.py:174
  121.0 9.8 %collective-permute-done.11.refs_0_ = bf16[256,896]{1,0:T(8,128)(2,1)} collective-permute-done((bf16[256,896]{1,0:T(8,128)(2,1)}, bf16[256,896]{1,0:T(8,128)(2,1)}, u32[]{:S(2)}, u32[]{:S(2)}) %collective-permute-start.11) | collective-permute-done | bytes 458784 | tf_op jit(solution)/shard_map/ppermute | solution.py:174
  130.9 20.5 %collective-permute-done.9.refs_0_ = bf16[256,896]{1,0:T(8,128)(2,1)S(1)} collective-permute-done((bf16[256,896]{1,0:T(8,128)(2,1)S(1)}, bf16[256,896]{1,0:T(8,128)(2,1)S(1)}, u32[]{:S(2)}, u32[]{:S(2)}) %collective-permute-start.9) | collective-permute-done | bytes 458784 | tf_op jit(solution)/shard_map/ppermute | solution.py:174
  152.4 1.8 collective-permute-done.41.refs_7_
  155.1 0.8 copy-done.22
  158.0 4.3 %shard_map.159 = (bf16[8192,1024]{1,0:T(8,128)(2,1)}, bf16[64,8192]{1,0:T(8,128)(2,1)}, bf16[64,8192]{1,0:T(8,128)(2,1)}) custom-call(s32[1]{0:T(128)} %bitcast.me, bf16[1024,128]{1,0:T(8,128)(2,1)} %get-tuple-element.54.refs_0_, bf16[1024,128]{1,0:T(8,128)(2,1)} %copy-done.25, bf16[1024,128]{1,0:T(8,128)(2,1)} %copy-done.23, bf16[1024,128]{1,0:T(8,128)(2,1)} %copy-done.27, ...), custom_call_target="tpu_custom_call" | custom-call | flops 16777216 | bytes 8388608 | tf_op jit(solution)/shard_map/pallas_call | solution.py:298
  162.3 6.3 %shard_map.160.refs_6_ = bf16[8192,1024]{1,0:T(8,128)(2,1)} custom-call(s32[1]{0:T(128)} %bitcast.me, bf16[256,896]{1,0:T(8,128)(2,1)} %get-tuple-element.47.refs_0_, bf16[256,896]{1,0:T(8,128)(2,1)} %copy-done.15, bf16[256,896]{1,0:T(8,128)(2,1)} %get-tuple-element.48.refs_2_, bf16[256,896]{1,0:T(8,128)(2,1)} %copy-done.9, ...), custom_call_target="tpu_custom_call", output_to_operand_aliasing={{}: (21, {})} | custom-call | flops 29360128 | bytes 14680064 | tf_op jit(solution)/shard_map/pallas_call | solution.py:298
  168.7 3.3 %shard_map.161.refs_4_ = bf16[8192,1024]{1,0:T(8,128)(2,1)} custom-call(s32[1]{0:T(128)} %bitcast.me, bf16[256,896]{1,0:T(8,128)(2,1)} %copy-done.18, bf16[256,896]{1,0:T(8,128)(2,1)} %copy-done.22, bf16[256,896]{1,0:T(8,128)(2,1)} %copy-done.16, bf16[256,896]{1,0:T(8,128)(2,1)} %copy-done.20, ...), custom_call_target="tpu_custom_call", output_to_operand_aliasing={{}: (7, {})} | custom-call | flops 11010048 | bytes 5505024 | tf_op jit(solution)/shard_map/pallas_call | solution.py:298
  172.0 2.7 %shard_map.162.refs_2_ = bf16[8192,1024]{1,0:T(8,128)(2,1)} custom-call(s32[1]{0:T(128)} %bitcast.me, bf16[256,896]{1,0:T(8,128)(2,1)} %collective-permute-done.13.refs_0_, bf16[256,896]{1,0:T(8,128)(2,1)} %collective-permute-done.14.refs_1_, bf16[256,896]{1,0:T(8,128)(2,1)} %collective-permute-done.15.refs_2_, ...), custom_call_target="tpu_custom_call", output_to_operand_aliasing={{}: (5, {})} | custom-call | flops 7340032 | bytes 3670016 | tf_op jit(solution)/shard_map/pallas_call | solution.py:298
  174.7 2.1 %shard_map.163.refs_2_ = bf16[8192,1024]{1,0:T(8,128)(2,1)} custom-call(s32[1]{0:T(128)} %bitcast.me, bf16[256,896]{1,0:T(8,128)(2,1)} %collective-permute-done.11.refs_0_, bf16[256,896]{1,0:T(8,128)(2,1)} %collective-permute-done.12.refs_1_, bf16[8192,1024]{1,0:T(8,128)(2,1)} %shard_map.162.refs_2_), custom_call_target="tpu_custom_call", output_to_operand_aliasing={{}: (3, {})} | custom-call | flops 3670016 | bytes 1835008 | tf_op jit(solution)/shard_map/pallas_call | solution.py:298
  176.8 2.1 %shard_map.164.refs_2_ = bf16[8192,1024]{1,0:T(8,128)(2,1)} custom-call(s32[1]{0:T(128)} %bitcast.me, bf16[256,896]{1,0:T(8,128)(2,1)} %copy-done.19, bf16[256,896]{1,0:T(8,128)(2,1)} %collective-permute-done.10.refs_1_, bf16[8192,1024]{1,0:T(8,128)(2,1)} %shard_map.163.refs_2_), custom_call_target="tpu_custom_call", output_to_operand_aliasing={{}: (3, {})} | custom-call | flops 3670016 | bytes 1835008 | tf_op jit(solution)/shard_map/pallas_call | solution.py:298
  178.9 1.8 shard_map.165.refs_4_
  181.4 1.9 %shard_map.166 = bf16[8192,1024]{1,0:T(8,128)(2,1)} custom-call(s32[1]{0:T(128)} %bitcast.me, bf16[64,896]{1,0:T(8,128)(2,1)} %collective-permute-done.3.refs_0_, bf16[64,896]{1,0:T(8,128)(2,1)} %copy-done.30, bf16[64,896]{1,0:T(8,128)(2,1)} %collective-permute-done.5.refs_2_, ...), custom_call_target="tpu_custom_call", output_to_operand_aliasing={{}: (5, {})} | custom-call | flops 1835008 | bytes 917504 | tf_op jit(solution)/shard_map/pallas_call | solution.py:298
  (151 shorter events, 11.5 us)
Async XLA Ops:
  4.9 3.1 %collective-permute-start.33 = (f32[1,512]{1,0:T(1,128)}, f32[1,512]{1,0:T(1,128)S(1)}, u32[]{:S(2)}, u32[]{:S(2)}) collective-permute-start(f32[1,512]{1,0:T(1,128)} %get-tuple-element.52.refs_0_), channel_id=1, source_target_pairs={{0,8},{8,0},{16,24},{24,16},{1,9},{9,1},{17,25},{25,17},{2,10},{10... | collective-permute-start | bytes 6152 | tf_op jit(solution)/shard_map/ppermute | solution.py:174
  5.5 4.3 %collective-permute-start.34 = (f32[1,512]{1,0:T(1,128)}, f32[1,512]{1,0:T(1,128)S(1)}, u32[]{:S(2)}, u32[]{:S(2)}) collective-permute-start(f32[1,512]{1,0:T(1,128)} %get-tuple-element.52.refs_0_), channel_id=1, source_target_pairs={{0,16},{8,24},{16,0},{24,8},{1,17},{9,25},{17,1},{25,9},{2,18},{10... | collective-permute-start | bytes 6152 | tf_op jit(solution)/shard_map/ppermute | solution.py:174
  8.0 3.2 %collective-permute-start.35 = (f32[1,512]{1,0:T(1,128)}, f32[1,512]{1,0:T(1,128)S(1)}, u32[]{:S(2)}, u32[]{:S(2)}) collective-permute-start(f32[1,512]{1,0:T(1,128)} %get-tuple-element.52.refs_0_), channel_id=1, source_target_pairs={{0,24},{8,16},{16,8},{24,0},{1,25},{9,17},{17,9},{25,1},{2,26},{10... | collective-permute-start | bytes 6152 | tf_op jit(solution)/shard_map/ppermute | solution.py:174
  14.8 14.6 %collective-permute-start.45 = (bf16[4,1,256]{2,0,1:T(4,128)(2,1)S(1)}, bf16[4,1,256]{2,0,1:T(4,128)(2,1)S(1)}, u32[]{:S(2)}, u32[]{:S(2)}) collective-permute-start(bf16[4,1,256]{2,0,1:T(4,128)(2,1)S(1)} %convert_bitcast_fusion), channel_id=1, source_target_pairs={{0,1},{1,0},{2,3},{3,2},{4,5},{5,4},{6,7},{7,6},{8,9},{9,8},{10,11... | collective-permute-start | bytes 6152 | tf_op jit(solution)/shard_map/ppermute | solution.py:174
  27.5 3.5 %collective-permute-start = (f32[1,1024]{1,0:T(1,128)}, f32[1,1024]{1,0:T(1,128)S(1)}, u32[]{:S(2)}, u32[]{:S(2)}) collective-permute-start(f32[1,1024]{1,0:T(1,128)} %get-tuple-element.38.refs_0_), channel_id=1, source_target_pairs={{0,8},{8,0},{16,24},{24,16},{1,9},{9,1},{17,25},{25,17},{2,10},{10... | collective-permute-start | bytes 12296 | tf_op jit(solution)/shard_map/ppermute | solution.py:174
  27.5 3.9 %collective-permute-start.1 = (f32[1,1024]{1,0:T(1,128)}, f32[1,1024]{1,0:T(1,128)S(1)}, u32[]{:S(2)}, u32[]{:S(2)}) collective-permute-start(f32[1,1024]{1,0:T(1,128)} %get-tuple-element.38.refs_0_), channel_id=1, source_target_pairs={{0,16},{8,24},{16,0},{24,8},{1,17},{9,25},{17,1},{25,9},{2,18},{10... | collective-permute-start | bytes 12296 | tf_op jit(solution)/shard_map/ppermute | solution.py:174
  28.1 3.3 %collective-permute-start.2 = (f32[1,1024]{1,0:T(1,128)}, f32[1,1024]{1,0:T(1,128)S(1)}, u32[]{:S(2)}, u32[]{:S(2)}) collective-permute-start(f32[1,1024]{1,0:T(1,128)} %get-tuple-element.38.refs_0_), channel_id=1, source_target_pairs={{0,24},{8,16},{16,8},{24,0},{1,25},{9,17},{17,9},{25,1},{2,26},{10... | collective-permute-start | bytes 12296 | tf_op jit(solution)/shard_map/ppermute | solution.py:174
  29.4 11.7 %collective-permute-start.46 = (bf16[4,2,256]{2,0,1:T(4,128)(2,1)S(1)}, bf16[4,2,256]{2,0,1:T(4,128)(2,1)S(1)}, u32[]{:S(2)}, u32[]{:S(2)}) collective-permute-start(bf16[4,2,256]{2,0,1:T(4,128)(2,1)S(1)} %pad_maximum_fusion.2), channel_id=1, source_target_pairs={{0,2},{1,3},{2,0},{3,1},{4,6},{5,7},{6,4},{7,5},{8,10},{9,11},{10,... | collective-permute-start | bytes 12296 | tf_op jit(solution)/shard_map/ppermute | solution.py:174
  39.0 14.7 %collective-permute-start.30 = (bf16[128,896]{1,0:T(8,128)(2,1)}, bf16[128,896]{1,0:T(8,128)(2,1)}, u32[]{:S(2)}, u32[]{:S(2)}) collective-permute-start(bf16[128,896]{1,0:T(8,128)(2,1)} %get-tuple-element.42.refs_14_), channel_id=1, source_target_pairs={{0,8},{8,0},{16,24},{24,16},{1,9},{9,1},{17,25},{25,17},{2,10},{10... | collective-permute-start | bytes 688136 | tf_op jit(solution)/shard_map/ppermute | solution.py:174
  39.2 14.5 %collective-permute-start.7 = (bf16[128,896]{1,0:T(8,128)(2,1)}, bf16[128,896]{1,0:T(8,128)(2,1)S(1)}, u32[]{:S(2)}, u32[]{:S(2)}) collective-permute-start(bf16[128,896]{1,0:T(8,128)(2,1)} %get-tuple-element.42.refs_14_), channel_id=1, source_target_pairs={{0,16},{8,24},{16,0},{24,8},{1,17},{9,25},{17,1},{25,9},{2,18},{10... | collective-permute-start | bytes 688136 | tf_op jit(solution)/shard_map/ppermute | solution.py:174
  40.6 5.7 %collective-permute-start.31 = (bf16[64,896]{1,0:T(8,128)(2,1)}, bf16[64,896]{1,0:T(8,128)(2,1)S(1)}, u32[]{:S(2)}, u32[]{:S(2)}) collective-permute-start(bf16[64,896]{1,0:T(8,128)(2,1)} %get-tuple-element.40.refs_16_), channel_id=1, source_target_pairs={{0,8},{8,0},{16,24},{24,16},{1,9},{9,1},{17,25},{25,17},{2,10},{10... | collective-permute-start | bytes 344072 | tf_op jit(solution)/shard_map/ppermute | solution.py:174
  40.7 7.2 %collective-permute-start.32 = (bf16[64,896]{1,0:T(8,128)(2,1)}, bf16[64,896]{1,0:T(8,128)(2,1)S(1)}, u32[]{:S(2)}, u32[]{:S(2)}) collective-permute-start(bf16[64,896]{1,0:T(8,128)(2,1)} %get-tuple-element.41.refs_18_), channel_id=1, source_target_pairs={{0,8},{8,0},{16,24},{24,16},{1,9},{9,1},{17,25},{25,17},{2,10},{10... | collective-permute-start | bytes 344072 | tf_op jit(solution)/shard_map/ppermute | solution.py:174
  41.2 4.6 %collective-permute-start.47 = (bf16[4,4,256]{2,0,1:T(4,128)(2,1)S(1)}, bf16[4,4,256]{2,0,1:T(4,128)(2,1)S(1)}, u32[]{:S(2)}, u32[]{:S(2)}) collective-permute-start(bf16[4,4,256]{2,0,1:T(4,128)(2,1)S(1)} %pad_maximum_fusion.1), channel_id=1, source_target_pairs={{0,4},{1,5},{2,6},{3,7},{4,0},{5,1},{6,2},{7,3},{8,12},{9,13},{10,... | collective-permute-start | bytes 24584 | tf_op jit(solution)/shard_map/ppermute | solution.py:174
  45.8 5.5 %collective-permute-start.3 = (bf16[64,896]{1,0:T(8,128)(2,1)}, bf16[64,896]{1,0:T(8,128)(2,1)}, u32[]{:S(2)}, u32[]{:S(2)}) collective-permute-start(bf16[64,896]{1,0:T(8,128)(2,1)} %get-tuple-element.40.refs_16_), channel_id=1, source_target_pairs={{0,16},{8,24},{16,0},{24,8},{1,17},{9,25},{17,1},{25,9},{2,18},{10... | collective-permute-start | bytes 344072 | tf_op jit(solution)/shard_map/ppermute | solution.py:174
  46.4 6.1 %collective-permute-start.5 = (bf16[64,896]{1,0:T(8,128)(2,1)}, bf16[64,896]{1,0:T(8,128)(2,1)}, u32[]{:S(2)}, u32[]{:S(2)}) collective-permute-start(bf16[64,896]{1,0:T(8,128)(2,1)} %get-tuple-element.41.refs_18_), channel_id=1, source_target_pairs={{0,16},{8,24},{16,0},{24,8},{1,17},{9,25},{17,1},{25,9},{2,18},{10... | collective-permute-start | bytes 344072 | tf_op jit(solution)/shard_map/ppermute | solution.py:174
  48.5 19.0 %collective-permute-start.24 = (bf16[256,896]{1,0:T(8,128)(2,1)}, bf16[256,896]{1,0:T(8,128)(2,1)S(1)}, u32[]{:S(2)}, u32[]{:S(2)}) collective-permute-start(bf16[256,896]{1,0:T(8,128)(2,1)} %get-tuple-element.48.refs_2_), channel_id=1, source_target_pairs={{0,8},{8,0},{16,24},{24,16},{1,9},{9,1},{17,25},{25,17},{2,10},{10... | collective-permute-start | bytes 1376264 | tf_op jit(solution)/shard_map/ppermute | solution.py:174
  51.3 9.4 %collective-permute-start.37 = (bf16[1024,128]{1,0:T(8,128)(2,1)}, bf16[1024,128]{1,0:T(8,128)(2,1)S(1)}, u32[]{:S(2)}, u32[]{:S(2)}) collective-permute-start(bf16[1024,128]{1,0:T(8,128)(2,1)} %get-tuple-element.54.refs_0_), channel_id=1, source_target_pairs={{0,16},{8,24},{16,0},{24,8},{1,17},{9,25},{17,1},{25,9},{2,18},{10... | collective-permute-start | bytes 786440 | tf_op jit(solution)/shard_map/ppermute | solution.py:174
  52.5 13.0 %collective-permute-start.40 = (bf16[1024,128]{1,0:T(8,128)(2,1)}, bf16[1024,128]{1,0:T(8,128)(2,1)S(1)}, u32[]{:S(2)}, u32[]{:S(2)}) collective-permute-start(bf16[1024,128]{1,0:T(8,128)(2,1)} %get-tuple-element.55.refs_4_), channel_id=1, source_target_pairs={{0,16},{8,24},{16,0},{24,8},{1,17},{9,25},{17,1},{25,9},{2,18},{10... | collective-permute-start | bytes 786440 | tf_op jit(solution)/shard_map/ppermute | solution.py:174
  53.7 11.9 %collective-permute-start.36 = (bf16[1024,128]{1,0:T(8,128)(2,1)}, bf16[1024,128]{1,0:T(8,128)(2,1)S(1)}, u32[]{:S(2)}, u32[]{:S(2)}) collective-permute-start(bf16[1024,128]{1,0:T(8,128)(2,1)} %get-tuple-element.54.refs_0_), channel_id=1, source_target_pairs={{0,8},{8,0},{16,24},{24,16},{1,9},{9,1},{17,25},{25,17},{2,10},{10... | collective-permute-start | bytes 786440 | tf_op jit(solution)/shard_map/ppermute | solution.py:174
  53.7 13.0 %collective-permute-start.39 = (bf16[1024,128]{1,0:T(8,128)(2,1)}, bf16[1024,128]{1,0:T(8,128)(2,1)S(1)}, u32[]{:S(2)}, u32[]{:S(2)}) collective-permute-start(bf16[1024,128]{1,0:T(8,128)(2,1)} %get-tuple-element.55.refs_4_), channel_id=1, source_target_pairs={{0,8},{8,0},{16,24},{24,16},{1,9},{9,1},{17,25},{25,17},{2,10},{10... | collective-permute-start | bytes 786440 | tf_op jit(solution)/shard_map/ppermute | solution.py:174
  60.7 7.4 %collective-permute-start.25 = (bf16[256,896]{1,0:T(8,128)(2,1)S(1)}, bf16[256,896]{1,0:T(8,128)(2,1)S(1)}, u32[]{:S(2)}, u32[]{:S(2)}) collective-permute-start(bf16[256,896]{1,0:T(8,128)(2,1)S(1)} %copy-done.6), channel_id=1, source_target_pairs={{0,8},{8,0},{16,24},{24,16},{1,9},{9,1},{17,25},{25,17},{2,10},{10... | collective-permute-start | bytes 1376264 | tf_op jit(solution)/shard_map/ppermute | solution.py:174
  65.5 2.6 %collective-permute-start.26 = (bf16[256,896]{1,0:T(8,128)(2,1)S(1)}, bf16[256,896]{1,0:T(8,128)(2,1)S(1)}, u32[]{:S(2)}, u32[]{:S(2)}) collective-permute-start(bf16[256,896]{1,0:T(8,128)(2,1)S(1)} %copy-done.7), channel_id=1, source_target_pairs={{0,8},{8,0},{16,24},{24,16},{1,9},{9,1},{17,25},{25,17},{2,10},{10... | collective-permute-start | bytes 1376264 | tf_op jit(solution)/shard_map/ppermute | solution.py:174
  66.3 2.6 %collective-permute-start.27 = (bf16[256,896]{1,0:T(8,128)(2,1)}, bf16[256,896]{1,0:T(8,128)(2,1)S(1)}, u32[]{:S(2)}, u32[]{:S(2)}) collective-permute-start(bf16[256,896]{1,0:T(8,128)(2,1)} %get-tuple-element.46.refs_8_), channel_id=1, source_target_pairs={{0,8},{8,0},{16,24},{24,16},{1,9},{9,1},{17,25},{25,17},{2,10},{10... | collective-permute-start | bytes 1376264 | tf_op jit(solution)/shard_map/ppermute | solution.py:174
  67.4 2.8 %collective-permute-start.28 = (bf16[256,896]{1,0:T(8,128)(2,1)}, bf16[256,896]{1,0:T(8,128)(2,1)S(1)}, u32[]{:S(2)}, u32[]{:S(2)}) collective-permute-start(bf16[256,896]{1,0:T(8,128)(2,1)} %get-tuple-element.44.refs_10_), channel_id=1, source_target_pairs={{0,8},{8,0},{16,24},{24,16},{1,9},{9,1},{17,25},{25,17},{2,10},{10... | collective-permute-start | bytes 1376264 | tf_op jit(solution)/shard_map/ppermute | solution.py:174
  67.5 3.4 %collective-permute-start.29 = (bf16[256,896]{1,0:T(8,128)(2,1)S(1)}, bf16[256,896]{1,0:T(8,128)(2,1)S(1)}, u32[]{:S(2)}, u32[]{:S(2)}) collective-permute-start(bf16[256,896]{1,0:T(8,128)(2,1)S(1)} %copy-done.8), channel_id=1, source_target_pairs={{0,8},{8,0},{16,24},{24,16},{1,9},{9,1},{17,25},{25,17},{2,10},{10... | collective-permute-start | bytes 1376264 | tf_op jit(solution)/shard_map/ppermute | solution.py:174
  68.0 4.3 %collective-permute-start.23 = (bf16[256,896]{1,0:T(8,128)(2,1)S(1)}, bf16[256,896]{1,0:T(8,128)(2,1)S(1)}, u32[]{:S(2)}, u32[]{:S(2)}) collective-permute-start(bf16[256,896]{1,0:T(8,128)(2,1)S(1)} %copy-done.4), channel_id=1, source_target_pairs={{0,8},{8,0},{16,24},{24,16},{1,9},{9,1},{17,25},{25,17},{2,10},{10... | collective-permute-start | bytes 1376264 | tf_op jit(solution)/shard_map/ppermute | solution.py:174
  68.1 13.5 %collective-permute-start.19 = (bf16[256,896]{1,0:T(8,128)(2,1)S(1)}, bf16[256,896]{1,0:T(8,128)(2,1)S(1)}, u32[]{:S(2)}, u32[]{:S(2)}) collective-permute-start(bf16[256,896]{1,0:T(8,128)(2,1)S(1)} %copy-done.5), channel_id=1, source_target_pairs={{0,16},{8,24},{16,0},{24,8},{1,17},{9,25},{17,1},{25,9},{2,18},{10... | collective-permute-start | bytes 1376264 | tf_op jit(solution)/shard_map/ppermute | solution.py:174
  68.8 22.6 %collective-permute-start.21 = (bf16[256,896]{1,0:T(8,128)(2,1)S(1)}, bf16[256,896]{1,0:T(8,128)(2,1)S(1)}, u32[]{:S(2)}, u32[]{:S(2)}) collective-permute-start(bf16[256,896]{1,0:T(8,128)(2,1)S(1)} %copy-done.6), channel_id=1, source_target_pairs={{0,16},{8,24},{16,0},{24,8},{1,17},{9,25},{17,1},{25,9},{2,18},{10... | collective-permute-start | bytes 1376264 | tf_op jit(solution)/shard_map/ppermute | solution.py:174
  70.2 31.0 %collective-permute-start.17 = (bf16[256,896]{1,0:T(8,128)(2,1)S(1)}, bf16[256,896]{1,0:T(8,128)(2,1)S(1)}, u32[]{:S(2)}, u32[]{:S(2)}) collective-permute-start(bf16[256,896]{1,0:T(8,128)(2,1)S(1)} %copy-done.4), channel_id=1, source_target_pairs={{0,16},{8,24},{16,0},{24,8},{1,17},{9,25},{17,1},{25,9},{2,18},{10... | collective-permute-start | bytes 1376264 | tf_op jit(solution)/shard_map/ppermute | solution.py:174
  70.9 40.3 %collective-permute-start.13 = (bf16[256,896]{1,0:T(8,128)(2,1)S(1)}, bf16[256,896]{1,0:T(8,128)(2,1)}, u32[]{:S(2)}, u32[]{:S(2)}) collective-permute-start(bf16[256,896]{1,0:T(8,128)(2,1)S(1)} %copy-done.7), channel_id=1, source_target_pairs={{0,16},{8,24},{16,0},{24,8},{1,17},{9,25},{17,1},{25,9},{2,18},{10... | collective-permute-start | bytes 1376264 | tf_op jit(solution)/shard_map/ppermute | solution.py:174
  72.3 48.7 %collective-permute-start.15 = (bf16[256,896]{1,0:T(8,128)(2,1)}, bf16[256,896]{1,0:T(8,128)(2,1)}, u32[]{:S(2)}, u32[]{:S(2)}) collective-permute-start(bf16[256,896]{1,0:T(8,128)(2,1)} %get-tuple-element.46.refs_8_), channel_id=1, source_target_pairs={{0,16},{8,24},{16,0},{24,8},{1,17},{9,25},{17,1},{25,9},{2,18},{10... | collective-permute-start | bytes 1376264 | tf_op jit(solution)/shard_map/ppermute | solution.py:174
  81.6 49.3 %collective-permute-start.11 = (bf16[256,896]{1,0:T(8,128)(2,1)}, bf16[256,896]{1,0:T(8,128)(2,1)}, u32[]{:S(2)}, u32[]{:S(2)}) collective-permute-start(bf16[256,896]{1,0:T(8,128)(2,1)} %get-tuple-element.44.refs_10_), channel_id=1, source_target_pairs={{0,16},{8,24},{16,0},{24,8},{1,17},{9,25},{17,1},{25,9},{2,18},{10... | collective-permute-start | bytes 1376264 | tf_op jit(solution)/shard_map/ppermute | solution.py:174
  91.4 59.9 %collective-permute-start.43 = (bf16[128,2048]{1,0:T(8,128)(2,1)S(1)}, bf16[128,2048]{1,0:T(8,128)(2,1)S(1)}, u32[]{:S(2)}, u32[]{:S(2)}) collective-permute-start(bf16[128,2048]{1,0:T(8,128)(2,1)S(1)} %copy-done), channel_id=1, source_target_pairs={{0,16},{8,24},{16,0},{24,8},{1,17},{9,25},{17,1},{25,9},{2,18},{10... | collective-permute-start | bytes 1572872 | tf_op jit(solution)/shard_map/ppermute | solution.py:174
  101.3 50.6 %collective-permute-start.42 = (bf16[128,2048]{1,0:T(8,128)(2,1)S(1)}, bf16[128,2048]{1,0:T(8,128)(2,1)S(1)}, u32[]{:S(2)}, u32[]{:S(2)}) collective-permute-start(bf16[128,2048]{1,0:T(8,128)(2,1)S(1)} %copy-done), channel_id=1, source_target_pairs={{0,8},{8,0},{16,24},{24,16},{1,9},{9,1},{17,25},{25,17},{2,10},{10... | collective-permute-start | bytes 1572872 | tf_op jit(solution)/shard_map/ppermute | solution.py:174
  111.2 40.1 %collective-permute-start.9 = (bf16[256,896]{1,0:T(8,128)(2,1)S(1)}, bf16[256,896]{1,0:T(8,128)(2,1)S(1)}, u32[]{:S(2)}, u32[]{:S(2)}) collective-permute-start(bf16[256,896]{1,0:T(8,128)(2,1)S(1)} %copy-done.8), channel_id=1, source_target_pairs={{0,16},{8,24},{16,0},{24,8},{1,17},{9,25},{17,1},{25,9},{2,18},{10... | collective-permute-start | bytes 1376264 | tf_op jit(solution)/shard_map/ppermute | solution.py:174
  121.0 30.9 %collective-permute-start.38 = (bf16[1024,128]{1,0:T(8,128)(2,1)S(1)}, bf16[1024,128]{1,0:T(8,128)(2,1)S(1)}, u32[]{:S(2)}, u32[]{:S(2)}) collective-permute-start(bf16[1024,128]{1,0:T(8,128)(2,1)S(1)} %collective-permute-done.37.refs_2_), channel_id=1, source_target_pairs={{0,8},{8,0},{16,24},{24,16},{1,9},{9,1},{17,25},{25,17},{2,10},{10... | collective-permute-start | bytes 786440 | tf_op jit(solution)/shard_map/ppermute | solution.py:174
  130.9 23.5 %collective-permute-start.20 = (bf16[256,896]{1,0:T(8,128)(2,1)S(1)}, bf16[256,896]{1,0:T(8,128)(2,1)S(1)}, u32[]{:S(2)}, u32[]{:S(2)}) collective-permute-start(bf16[256,896]{1,0:T(8,128)(2,1)S(1)} %collective-permute-done.19.refs_2_), channel_id=1, source_target_pairs={{0,8},{8,0},{16,24},{24,16},{1,9},{9,1},{17,25},{25,17},{2,10},{10... | collective-permute-start | bytes 1376264 | tf_op jit(solution)/shard_map/ppermute | solution.py:174
  151.3 3.5 %collective-permute-start.22 = (bf16[256,896]{1,0:T(8,128)(2,1)S(1)}, bf16[256,896]{1,0:T(8,128)(2,1)S(1)}, u32[]{:S(2)}, u32[]{:S(2)}) collective-permute-start(bf16[256,896]{1,0:T(8,128)(2,1)S(1)} %collective-permute-done.21.refs_4_), channel_id=1, source_target_pairs={{0,8},{8,0},{16,24},{24,16},{1,9},{9,1},{17,25},{25,17},{2,10},{10... | collective-permute-start | bytes 1376264 | tf_op jit(solution)/shard_map/ppermute | solution.py:174
  151.3 3.7 %collective-permute-start.18 = (bf16[256,896]{1,0:T(8,128)(2,1)S(1)}, bf16[256,896]{1,0:T(8,128)(2,1)S(1)}, u32[]{:S(2)}, u32[]{:S(2)}) collective-permute-start(bf16[256,896]{1,0:T(8,128)(2,1)S(1)} %collective-permute-done.17.refs_0_), channel_id=1, source_target_pairs={{0,8},{8,0},{16,24},{24,16},{1,9},{9,1},{17,25},{25,17},{2,10},{10... | collective-permute-start | bytes 1376264 | tf_op jit(solution)/shard_map/ppermute | solution.py:174
  151.8 2.3 %collective-permute-start.41 = (bf16[1024,128]{1,0:T(8,128)(2,1)S(1)}, bf16[1024,128]{1,0:T(8,128)(2,1)S(1)}, u32[]{:S(2)}, u32[]{:S(2)}) collective-permute-start(bf16[1024,128]{1,0:T(8,128)(2,1)S(1)} %collective-permute-done.40.refs_6_), channel_id=1, source_target_pairs={{0,8},{8,0},{16,24},{24,16},{1,9},{9,1},{17,25},{25,17},{2,10},{10... | collective-permute-start | bytes 786440 | tf_op jit(solution)/shard_map/ppermute | solution.py:174
  151.9 4.3 %collective-permute-start.14 = (bf16[256,896]{1,0:T(8,128)(2,1)}, bf16[256,896]{1,0:T(8,128)(2,1)}, u32[]{:S(2)}, u32[]{:S(2)}) collective-permute-start(bf16[256,896]{1,0:T(8,128)(2,1)} %collective-permute-done.13.refs_0_), channel_id=1, source_target_pairs={{0,8},{8,0},{16,24},{24,16},{1,9},{9,1},{17,25},{25,17},{2,10},{10... | collective-permute-start | bytes 1376264 | tf_op jit(solution)/shard_map/ppermute | solution.py:174
  154.2 2.8 %collective-permute-start.44 = (bf16[128,2048]{1,0:T(8,128)(2,1)S(1)}, bf16[128,2048]{1,0:T(8,128)(2,1)S(1)}, u32[]{:S(2)}, u32[]{:S(2)}) collective-permute-start(bf16[128,2048]{1,0:T(8,128)(2,1)S(1)} %collective-permute-done.43.refs_10_), channel_id=1, source_target_pairs={{0,8},{8,0},{16,24},{24,16},{1,9},{9,1},{17,25},{25,17},{2,10},{10... | collective-permute-start | bytes 1572872 | tf_op jit(solution)/shard_map/ppermute | solution.py:174
  154.3 2.5 %collective-permute-start.16 = (bf16[256,896]{1,0:T(8,128)(2,1)}, bf16[256,896]{1,0:T(8,128)(2,1)}, u32[]{:S(2)}, u32[]{:S(2)}) collective-permute-start(bf16[256,896]{1,0:T(8,128)(2,1)} %collective-permute-done.15.refs_2_), channel_id=1, source_target_pairs={{0,8},{8,0},{16,24},{24,16},{1,9},{9,1},{17,25},{25,17},{2,10},{10... | collective-permute-start | bytes 1376264 | tf_op jit(solution)/shard_map/ppermute | solution.py:174
  154.8 19.9 %collective-permute-start.12 = (bf16[256,896]{1,0:T(8,128)(2,1)}, bf16[256,896]{1,0:T(8,128)(2,1)}, u32[]{:S(2)}, u32[]{:S(2)}) collective-permute-start(bf16[256,896]{1,0:T(8,128)(2,1)} %collective-permute-done.11.refs_0_), channel_id=1, source_target_pairs={{0,8},{8,0},{16,24},{24,16},{1,9},{9,1},{17,25},{25,17},{2,10},{10... | collective-permute-start | bytes 1376264 | tf_op jit(solution)/shard_map/ppermute | solution.py:174
  155.8 21.0 %collective-permute-start.10 = (bf16[256,896]{1,0:T(8,128)(2,1)S(1)}, bf16[256,896]{1,0:T(8,128)(2,1)}, u32[]{:S(2)}, u32[]{:S(2)}) collective-permute-start(bf16[256,896]{1,0:T(8,128)(2,1)S(1)} %collective-permute-done.9.refs_0_), channel_id=1, source_target_pairs={{0,8},{8,0},{16,24},{24,16},{1,9},{9,1},{17,25},{25,17},{2,10},{10... | collective-permute-start | bytes 1376264 | tf_op jit(solution)/shard_map/ppermute | solution.py:174
  156.2 22.7 %collective-permute-start.8 = (bf16[128,896]{1,0:T(8,128)(2,1)}, bf16[128,896]{1,0:T(8,128)(2,1)}, u32[]{:S(2)}, u32[]{:S(2)}) collective-permute-start(bf16[128,896]{1,0:T(8,128)(2,1)} %copy-done.29), channel_id=1, source_target_pairs={{0,8},{8,0},{16,24},{24,16},{1,9},{9,1},{17,25},{25,17},{2,10},{10... | collective-permute-start | bytes 688136 | tf_op jit(solution)/shard_map/ppermute | solution.py:174
  156.9 23.9 %collective-permute-start.4 = (bf16[64,896]{1,0:T(8,128)(2,1)}, bf16[64,896]{1,0:T(8,128)(2,1)S(1)}, u32[]{:S(2)}, u32[]{:S(2)}) collective-permute-start(bf16[64,896]{1,0:T(8,128)(2,1)} %collective-permute-done.3.refs_0_), channel_id=1, source_target_pairs={{0,8},{8,0},{16,24},{24,16},{1,9},{9,1},{17,25},{25,17},{2,10},{10... | collective-permute-start | bytes 344072 | tf_op jit(solution)/shard_map/ppermute | solution.py:174
  157.0 23.8 %collective-permute-start.6 = (bf16[64,896]{1,0:T(8,128)(2,1)}, bf16[64,896]{1,0:T(8,128)(2,1)}, u32[]{:S(2)}, u32[]{:S(2)}) collective-permute-start(bf16[64,896]{1,0:T(8,128)(2,1)} %collective-permute-done.5.refs_2_), channel_id=1, source_target_pairs={{0,8},{8,0},{16,24},{24,16},{1,9},{9,1},{17,25},{25,17},{2,10},{10... | collective-permute-start | bytes 344072 | tf_op jit(solution)/shard_map/ppermute | solution.py:174
  (40 other events, 1298.6 us)
where the time goes:
time: 184 us; the launch traced here: 183 us
  waiting for transfers between devices  96 us (52%)
  Pallas kernels  51.6 us (28%)
  starting transfers between devices  28.5 us (15%)
  local copies, waits for them, and re-layouts  5.38 us (3%)
    ppermute x48, waiting for transfers between devices, swap(): return lax.ppermute(array, axis, [(i, i ^ distance) for i in range(size)])  96 us
    ppermute x48, starting transfers between devices, swap(): return lax.ppermute(array, axis, [(i, i ^ distance) for i in range(size)])  28.5 us
    pallas_call x8, Pallas kernels, place(): pl.pallas_call(functools.partial(place_kernel, [job[1:] for job in jobs],...  24.5 us
    pallas_call x1, Pallas kernels, on_device(): pl.pallas_call(average_kernel, grid=(rows // block,), out_shape=(shaped((...  11.2 us
    unnamed x81, local copies, waits for them, and re-layouts  5.37 us
    pallas_call x1, Pallas kernels, on_device(): pl.pallas_call(fourth_kernel, grid=(1,), out_shape=narrow[1:], in_specs=[...  4.8 us
    pallas_call x1, Pallas kernels, on_device(): pl.pallas_call(functools.partial(narrow_kernel, places), grid=(rows // bl...  4.29 us
  transfers between devices with their start and end apart: 48, of which 16 were waited for; matrix products, arithmetic and copies ran while one was open for 0% of the time, Pallas kernels for 24%

commit v1 on v0

v1 whole, which is shorter than its diff:
```python
import functools

import jax
import jax.numpy as jnp
from jax import lax
from jax.experimental import pallas as pl
from jax.experimental.pallas import tpu as pltpu
from jax.sharding import PartitionSpec as P


KEEP = 0.7
LANES = 128
GRANT_KIB = 60 * 1024

VMEM = pl.BlockSpec(memory_space=pltpu.VMEM)
SMEM = pl.BlockSpec(memory_space=pltpu.SMEM)
HBM = pl.BlockSpec(memory_space=pl.ANY)


def cost(flops, bytes_accessed):
    return pl.CostEstimate(flops=flops, bytes_accessed=bytes_accessed, transcendentals=0)


def leaving(kibibytes):
    return pltpu.CompilerParams(vmem_limit_bytes=(GRANT_KIB - kibibytes) << 10)


def round_up(value, step):
    return -(-value // step) * step


def average(smooth, weight):
    return KEEP * smooth + (1.0 - KEEP) * weight


def lane_sum(block):
    total = block[:, :LANES]
    for at in range(LANES, block.shape[1], LANES):
        total = total + block[:, at : at + LANES]
    return total


def row_sum(block):
    return jnp.sum(block.reshape(block.shape[0] // 8, 8, block.shape[1]), axis=0)


def load(sources, buffers, parts, sems):
    copies = []
    for at in range(parts):
        copies.append([])
        for source, buffer in zip(sources, buffers):
            step = buffer.shape[0] // parts
            rows = pl.ds(at * step, step)
            slot = sems.at[at * len(sources) + len(copies[-1])]
            copies[-1].append(
                pltpu.make_async_copy(
                    source.at[rows, pl.ds(0, buffer.shape[1])], buffer.at[rows, :], slot
                )
            )
            copies[-1][-1].start()

    def wait(at):
        for copy in copies[at]:
            copy.wait()

    return wait


PARTS = 4


def narrow_kernel(places, wq, sq, wk, sk, wv, sv, nt, ns, rk, rv, early, message, *refs):
    *buffers, gain_a, gain_b, note, sum_kv, in_kv, in_q, in_gain, outs = refs
    of_kv, of_q = buffers[:4], buffers[4:]
    place_kv, place_norm = places
    heads, rows = of_kv[0].shape
    wait_kv = load((wk, sk, wv, sv), of_kv, PARTS, in_kv)
    wait_gain = load((nt, ns), (gain_a, gain_b), 1, in_gain)
    wait_q = load((wq, sq), of_q, PARTS, in_q)
    step = heads // PARTS
    writes = []

    def write(source, target):
        writes.append(pltpu.make_async_copy(source, target, outs.at[len(writes)]))
        writes[-1].start()

    for part in range(PARTS):
        wait_kv(part)
        at = pl.ds(part * step, step)
        for which, (w, s, r) in enumerate(((of_kv[0], of_kv[1], rk), (of_kv[2], of_kv[3], rv))):
            new = average(s[at, :], w[at, :])
            sum_kv[which * heads + part * step : which * heads + (part + 1) * step, :] = (
                lane_sum(jnp.abs(new))
            )
            s[at, :] = new
            write(s.at[at, :], r.at[at, :])
            if which == 0:
                write(s.at[at, pl.ds(0, early.shape[1])], early.at[at, :])
    total = jnp.zeros((8, of_q[0].shape[1]), jnp.float32)
    step = rows // PARTS
    for part in range(PARTS):
        wait_q(part)
        at = pl.ds(part * step, step)
        total = total + row_sum(jnp.abs(average(of_q[1][at, :], of_q[0][at, :])))
    note[...] = jnp.zeros_like(note)
    note[:, : total.shape[1]] = jnp.sum(total, axis=0, keepdims=True)
    note[:, place_kv : place_kv + 2 * heads] = jnp.sum(
        sum_kv[...].T, axis=0, keepdims=True
    )
    wait_gain(0)
    gain = (gain_a[...] + gain_b[...]).astype(jnp.bfloat16)
    note[:, place_norm : place_norm + gain.shape[1]] = gain.astype(jnp.float32)
    write(note, message)
    for copy in writes:
        copy.wait()


def tree(pieces):
    while len(pieces) > 1:
        pieces = [a + b for a, b in zip(pieces[::2], pieces[1::2])]
    return pieces[0]


def first_kernel(places, gain, count, me, rk, rv, wq, sq, *refs):
    n = len(refs) - 7
    messages, (own, own_a, own_b, inv_k, factor_k, factor_v, norms) = refs[:n], refs[n:]
    place_kv, place_norm = places
    heads, rows = rk.shape
    pieces = [m[...] for m in messages]
    for distance, piece in enumerate(pieces):
        norms[pl.ds(me[0] ^ distance, 1), :] = piece[:, place_norm : place_norm + gain]
    total = tree(pieces) / count
    first = 0
    for part in (own_a, own_b):
        at = pl.ds(first, part.shape[0])
        first += part.shape[0]
        part[...] = (average(sq[at, :], wq[at, :]) / total[:, : part.shape[1]]).astype(
            jnp.bfloat16
        )
    of_kv = total[:, place_kv : place_kv + 2 * heads]
    factor_k[...] = of_kv[:, :heads]
    factor_v[...] = of_kv[:, heads:]
    inv = jnp.broadcast_to(1.0 / of_kv, (LANES, 2 * heads)).T
    inv_k[...] = inv[:heads, :]
    late = 2 * rows - own.shape[1]
    scale_lanes(rk, inv[:heads, :], own, late, 0, rows - late)
    scale_lanes(rv, inv[heads:, :], own, 0, rows - late, rows)


def scale_lanes(source, scale, target, first, to, count):
    for at in range(0, count, LANES):
        target[:, to + at : to + at + LANES] = (
            source[:, first + at : first + at + LANES] * scale
        ).astype(jnp.bfloat16)


def average_kernel(wq, sq, rq, message, w, s, note, in_w, in_s, outs, sent):
    parts = in_w.shape[0]
    step = w.shape[0] // parts

    def copies(at):
        rows = pl.ds(pl.multiple_of(at * step, step), step)
        return (
            pltpu.make_async_copy(wq.at[rows, :], w.at[rows, :], in_w.at[at]),
            pltpu.make_async_copy(sq.at[rows, :], s.at[rows, :], in_s.at[at]),
            pltpu.make_async_copy(s.at[rows, :], rq.at[rows, :], outs.at[at]),
        )

    @pl.loop(0, parts)
    def _(at):
        one, two, _ = copies(at)
        one.start()
        two.start()

    def body(at, total):
        one, two, out = copies(at)
        one.wait()
        two.wait()
        rows = pl.ds(pl.multiple_of(at * step, step), step)
        new = average(s[rows, :], w[rows, :])
        s[rows, :] = new
        out.start()
        return total + row_sum(jnp.abs(new))

    total = lax.fori_loop(0, parts, body, jnp.zeros((8, w.shape[1]), jnp.float32))
    note[...] = jnp.sum(total, axis=0, keepdims=True)
    send = pltpu.make_async_copy(note, message, sent)
    send.start()

    @pl.loop(0, parts)
    def _(at):
        copies(at)[2].wait()

    send.wait()


def third_kernel(columns, count, rq, *refs):
    messages, (own, inv, factor) = refs[:-3], refs[-3:]
    total = tree([m[...] for m in messages]) / count
    factor[...] = total
    scale = 1.0 / total[:, columns:]
    inv[...] = scale
    own[...] = (rq[:, columns:] * scale).astype(jnp.bfloat16)


def fourth_kernel(inv, *refs):
    half = len(refs) // 2
    for source, own in zip(refs[:half], refs[half:]):
        columns = source.shape[1] - own.shape[1]
        own[...] = (source[:, columns:] * inv[...]).astype(jnp.bfloat16)


def place_kernel(plan, rows, unread, me, *refs):
    pieces, refs = refs[: len(plan)], refs[len(plan) + unread :]
    out, sems = refs
    copies = []
    for piece, (distance, first, column) in zip(pieces, plan):
        start = pl.multiple_of((me[0] ^ distance) * rows + first, 16)
        target = out.at[pl.ds(start, piece.shape[0]), pl.ds(column, piece.shape[1])]
        copies.append(pltpu.make_async_copy(piece, target, sems.at[len(copies)]))
        copies[-1].start()
    for copy in copies:
        copy.wait()


def place_kv_kernel(n, me, inv, *refs):
    early, pieces, (out_k, out_v, scaled, sems) = refs[:n], refs[n : 2 * n], refs[2 * n :]
    part = early[0].shape[1]
    rows = (pieces[0].shape[1] + part) // 2
    copies = []

    def move(source, target):
        copies.append(pltpu.make_async_copy(source, target, sems.at[len(copies)]))
        copies[-1].start()

    starts = [pl.multiple_of((me[0] ^ distance) * rows, LANES) for distance in range(n)]
    for start, piece in zip(starts, pieces):
        late = rows - part
        move(piece.at[:, pl.ds(0, late)], out_k.at[:, pl.ds(start + part, late)])
        move(piece.at[:, pl.ds(late, rows)], out_v.at[:, pl.ds(start, rows)])
    for distance, start in enumerate(starts):
        scale_lanes(early[distance], inv[...], scaled.at[distance], 0, 0, part)
        move(scaled.at[distance], out_k.at[:, pl.ds(start, part)])
    for copy in copies:
        copy.wait()


CUTS = (4, 4, 8, 8, 4, 2, 1, 1)


def on_device(n, groups, wq, sq, wk, sk, wv, sv, norm_train, norm_step):
    rows, width = wq.shape
    heads = wk.shape[1]
    gain = norm_train.shape[0]
    f32, bf16 = jnp.float32, jnp.bfloat16
    shaped = jax.ShapeDtypeStruct
    me = lax.axis_index("zero").astype(jnp.int32).reshape(1)

    def swap(array, distance, axis="zero", size=n):
        return lax.ppermute(array, axis, [(i, i ^ distance) for i in range(size)])

    def gather(piece):
        found = [piece, swap(piece, 1)]
        for distance in range(2, n, 2):
            far = swap(piece, distance)
            found += [far, swap(far, 1)]
        return found

    once = lambda shape: pl.BlockSpec(shape, lambda i: (0, 0))
    full = lambda a: once(a.shape)

    columns = max(LANES, width // 8)
    place_kv = columns
    place_norm = place_kv + round_up(2 * heads, LANES)
    places = (place_kv, place_norm)
    length = place_norm + round_up(gain, LANES)
    ahead = rows * 11 // 16 // LANES * LANES
    rk, rv, early, message = pl.pallas_call(
        functools.partial(narrow_kernel, places),
        out_shape=(
            shaped((heads, rows), f32),
            shaped((heads, rows), f32),
            shaped((heads, ahead), f32),
            shaped((1, length), f32),
        ),
        in_specs=[HBM] * 8,
        out_specs=[HBM] * 4,
        scratch_shapes=[pltpu.VMEM((heads, rows), f32)] * 4
        + [pltpu.VMEM((rows, columns), f32)] * 2
        + [
            pltpu.VMEM((1, gain), f32),
            pltpu.VMEM((1, gain), f32),
            pltpu.VMEM((1, length), f32),
            pltpu.VMEM((2 * heads, LANES), f32),
            pltpu.SemaphoreType.DMA((4 * PARTS,)),
            pltpu.SemaphoreType.DMA((2 * PARTS,)),
            pltpu.SemaphoreType.DMA((2,)),
            pltpu.SemaphoreType.DMA((3 * PARTS + 1,)),
        ],
        cost_estimate=cost(rows * 2 * heads * 8, rows * 2 * heads * 16),
        name="narrow",
    )(wq, sq, wk.T, sk.T, wv.T, sv.T, norm_train[None], norm_step[None])
    messages = gather(message)
    found_early = gather(early)
    cut_a = rows * 3 // 8
    late = (heads, 2 * rows - ahead)
    own_kv, *own_a, inv_k, factor_k, factor_v, norms = pl.pallas_call(
        functools.partial(first_kernel, places, gain, n * rows),
        grid=(1,),
        out_shape=(
            shaped(late, bf16),
            shaped((cut_a, columns), bf16),
            shaped((rows - cut_a, columns), bf16),
            shaped((heads, LANES), f32),
            shaped((1, heads), f32),
            shaped((1, heads), f32),
            shaped((n, gain), f32),
        ),
        in_specs=[SMEM]
        + [full(rk)] * 2
        + [once((rows, columns))] * 2
        + [full(message)] * n,
        out_specs=[
            once(late),
            once((cut_a, columns)),
            once((rows - cut_a, columns)),
            once((heads, LANES)),
            once((1, heads)),
            once((1, heads)),
            once((n, gain)),
        ],
        cost_estimate=cost(rows * heads * 8, rows * heads * 12),
        name="first",
    )(me, rk, rv, wq, sq, *messages)
    found_kv = gather(own_kv)
    found_a = [gather(piece) for piece in own_a]

    parts = 16
    rq, message_q = pl.pallas_call(
        average_kernel,
        out_shape=(shaped((rows, width), f32), shaped((1, width), f32)),
        in_specs=[HBM] * 2,
        out_specs=[HBM] * 2,
        scratch_shapes=[pltpu.VMEM((rows, width), f32)] * 2
        + [pltpu.VMEM((1, width), f32)]
        + [pltpu.SemaphoreType.DMA((parts,))] * 3
        + [pltpu.SemaphoreType.DMA],
        cost_estimate=cost(rows * width * 8, rows * width * 12),
        name="average",
    )(wq, sq)
    messages_q = gather(message_q)

    unit = rows // sum(CUTS)
    firsts = [sum(CUTS[:at]) for at in range(len(CUTS))]
    rest = width - columns
    rows_of = lambda at: pl.BlockSpec(
        (CUTS[at] * unit, width), lambda i: (firsts[at] // CUTS[at], 0)
    )
    narrow = [shaped((c * unit, rest), bf16) for c in CUTS]
    own0, inv, factor_q = pl.pallas_call(
        functools.partial(third_kernel, columns, n * rows),
        grid=(1,),
        out_shape=(narrow[0], shaped((1, rest), f32), shaped((1, width), f32)),
        in_specs=[rows_of(0)] + [full(message_q)] * n,
        out_specs=[full(narrow[0]), once((1, rest)), once((1, width))],
        cost_estimate=cost(narrow[0].size * 8, narrow[0].size * 6),
        name="third",
    )(rq, *messages_q)
    others = range(1, len(CUTS))
    owns = pl.pallas_call(
        fourth_kernel,
        grid=(1,),
        out_shape=narrow[1:],
        in_specs=[full(inv)] + [rows_of(at) for at in others],
        out_specs=[full(narrow[at]) for at in others],
        cost_estimate=cost(rows * rest * 8, rows * rest * 6),
        name="fourth",
    )(inv, *[rq for _ in others])
    found = [gather(piece) for piece in [own0, *owns]]

    whole = shaped((n * rows, width), bf16)
    whole_kv = shaped((heads, n * rows), bf16)

    def place(jobs, final=None, extra=(), spec=None):
        pieces = [job[0] for job in jobs]
        moved = sum(p.size for p in pieces) * 2
        return pl.pallas_call(
            functools.partial(
                place_kernel,
                [job[1:] for job in jobs],
                rows,
                len(extra) + (final is not None),
            ),
            out_shape=whole,
            in_specs=[SMEM]
            + [spec or VMEM] * len(pieces)
            + [HBM] * (len(extra) + (final is not None)),
            out_specs=HBM,
            scratch_shapes=[pltpu.SemaphoreType.DMA((len(jobs),))],
            input_output_aliases={} if final is None else {1 + len(pieces): 0},
            compiler_params=leaving(54000) if spec else None,
            cost_estimate=cost(moved * 4, 2 * moved),
        )(me, *pieces, *(() if final is None else (final,)), *extra)

    def jobs(chunks, distances):
        return [
            (found[at][d], d, firsts[at] * unit, columns) for at in chunks for d in distances
        ]

    gains = norms.astype(jnp.bfloat16).reshape(n, 1, gain)
    spot = lax.axis_index("width")
    bit = 1
    while bit < groups:
        other = swap(gains, bit, "width", groups)
        low = (spot & bit) == 0
        gains = jnp.concatenate(
            [jnp.where(low, gains, other), jnp.where(low, other, gains)], axis=1
        )
        bit *= 2
    serve = gains.reshape(n * groups * gain)

    near, far = range(2), range(2, n)
    final_q = place(
        [(found_a[at][d], d, at * cut_a, 0) for at in range(2) for d in range(n)],
    )
    moved = n * own_kv.size * 2
    final_k, final_v = pl.pallas_call(
        functools.partial(place_kv_kernel, n),
        grid=(1,),
        out_shape=[whole_kv] * 2,
        in_specs=[SMEM, full(inv_k)] + [full(early)] * n + [full(own_kv)] * n,
        out_specs=[HBM] * 2,
        scratch_shapes=[
            pltpu.VMEM((n, heads, ahead), bf16),
            pltpu.SemaphoreType.DMA((3 * n,)),
        ],
        cost_estimate=cost(moved * 4, 2 * moved),
        name="place_kv",
    )(me, inv_k, *found_early, *found_kv)
    for name, chunks, distances in (
        ("place_near", range(len(CUTS)), near),
        ("place1", (0, 1), far),
        ("place2", (2,), far),
        ("place3", (3,), far),
        ("place4", (4,), far),
        ("place5", (5,), far),
        ("place6", (6, 7), far),
    ):
        extra = (serve,) if name == "place1" else ()
        spec = HBM if name in ("place5", "place6") else None
        final_q = place(jobs(chunks, distances), final_q, extra, spec)

    return (
        final_q,
        final_k.T,
        final_v.T,
        factor_q.reshape(width),
        factor_k.reshape(heads),
        factor_v.reshape(heads),
        serve,
        rq,
        rk.T,
        rv.T,
    )


def solution(mesh):
    split, columns, lone = P("zero", "width"), P(None, "width"), P("width")
    vector = P(("zero", "width"))
    n = mesh.shape["zero"]

    def body(*args):
        return on_device(n, mesh.shape["width"], *args)

    return jax.shard_map(
        body,
        mesh=mesh,
        in_specs=(split,) * 6 + (vector,) * 2,
        out_specs=(columns,) * 3 + (lone,) * 3 + (P(),) + (split,) * 3,
        check_vma=False,
    )
```

time: 184 us -> 182 us (0.989)
  Pallas kernels: 51.6 us -> 47.5 us
  waiting for transfers between devices: 96 us -> 98.2 us
    pallas_call x8, Pallas kernels: 24.5 us -> 20.9 us  [place(): pl.pallas_call(functools.partial(place_kernel, [job[1:] for job in jobs],...]
    ppermute x48 -> x45, waiting for transfers between devices: 96 us -> 98.2 us  [swap(): return lax.ppermute(array, axis, [(i, i ^ distance) for i in range(size)])]
    ppermute x48 -> x45, starting transfers between devices: 28.5 us -> 26.9 us  [swap(): return lax.ppermute(array, axis, [(i, i ^ distance) for i in range(size)])]
    unnamed x81 -> x63, local copies, waits for them, and re-layouts: 5.37 us -> 6.12 us
  transfers between devices with their start and end apart: 48 -> 45, of which waited for: 16 -> 14; matrix products, arithmetic and copies ran while one was open for 0% -> 1% of each run, Pallas kernels for 24% -> 24%
where the time goes in v1:
time: 182 us; the launch traced here: 181 us
  waiting for transfers between devices  98.2 us (54%)
  Pallas kernels  47.5 us (26%)
  starting transfers between devices  26.9 us (15%)
  local copies, waits for them, and re-layouts  6.13 us (3%)
    ppermute x45, waiting for transfers between devices, swap(): return lax.ppermute(array, axis, [(i, i ^ distance) for i in range(size)])  98.2 us
    ppermute x45, starting transfers between devices, swap(): return lax.ppermute(array, axis, [(i, i ^ distance) for i in range(size)])  26.9 us
    pallas_call x8, Pallas kernels, place(): pl.pallas_call(functools.partial(place_kernel, [job[1:] for job in jobs],...  20.9 us
    pallas_call x1, Pallas kernels, on_device(): pl.pallas_call(average_kernel, out_shape=(shaped((rows, width), f32), sha...  9.5 us
    unnamed x63, local copies, waits for them, and re-layouts  6.12 us
    pallas_call x1, Pallas kernels, on_device(): pl.pallas_call(fourth_kernel, grid=(1,), out_shape=narrow[1:], in_specs=[...  4.97 us
    pallas_call x1, Pallas kernels, on_device(): pl.pallas_call(functools.partial(narrow_kernel, places), out_shape=(shape...  3.77 us
  transfers between devices with their start and end apart: 45, of which 14 were waited for; matrix products, arithmetic and copies ran while one was open for 1% of the time, Pallas kernels for 24%

profile of v1, /device:TPU:0, one launch (start us, length us, event | category | flops | bytes accessed | tf_op | source)
XLA Modules:
  0.0 181.2 jit_solution(13518477193324798235)
XLA Ops:
  0.6 3.8 %narrow.1 = (f32[64,2048]{1,0:T(8,128)}, f32[64,2048]{1,0:T(8,128)}, f32[64,1408]{1,0:T(8,128)}, f32[1,512]{1,0:T(1,128)}) custom-call(f32[2048,1024]{1,0:T(8,128)} %wq.5, f32[2048,1024]{1,0:T(8,128)} %sq.5, f32[64,2048]{1,0:T(8,128)} %bitcast.22, f32[64,2048]{1,0:T(8,128)} %bitcast.23, f32[64,2048]{1,0:T(8,128)} %bitcast.24, f32[64,2048]{1,0:T(8,128)} %bitcast.25, ...), custom_call_target="tpu_custom_call" | custom-call | flops 2097152 | bytes 4194304 | tf_op jit(solution)/shard_map/narrow/pallas_call | solution.py:278
  4.4 3.0 %collective-permute-start.28 = (f32[1,512]{1,0:T(1,128)}, f32[1,512]{1,0:T(1,128)S(1)}, u32[]{:S(2)}, u32[]{:S(2)}) collective-permute-start(f32[1,512]{1,0:T(1,128)} %get-tuple-element.48.refs_0_), channel_id=1, source_target_pairs={{0,16},{8,24},{16,0},{24,8},{1,17},{9,25},{17,1},{25,9},{2,18},{10... | collective-permute-start | bytes 6152 | tf_op jit(solution)/shard_map/ppermute | solution.py:260
  7.5 1.8 collective-permute-done.28.refs_2_
  9.2 9.5 %average.1 = (f32[2048,1024]{1,0:T(8,128)}, f32[1,1024]{1,0:T(1,128)}) custom-call(f32[2048,1024]{1,0:T(8,128)} %wq.5, f32[2048,1024]{1,0:T(8,128)} %sq.5), custom_call_target="tpu_custom_call" | custom-call | flops 16777216 | bytes 25165824 | tf_op jit(solution)/shard_map/average/pallas_call | solution.py:339
  18.7 2.1 %collective-permute-start.1 = (f32[1,1024]{1,0:T(1,128)}, f32[1,1024]{1,0:T(1,128)S(1)}, u32[]{:S(2)}, u32[]{:S(2)}) collective-permute-start(f32[1,1024]{1,0:T(1,128)} %get-tuple-element.36.refs_0_), channel_id=1, source_target_pairs={{0,16},{8,24},{16,0},{24,8},{1,17},{9,25},{17,1},{25,9},{2,18},{10... | collective-permute-start | bytes 12296 | tf_op jit(solution)/shard_map/ppermute | solution.py:260
  21.4 3.1 %first.1 = (bf16[64,2688]{1,0:T(8,128)(2,1)}, bf16[768,128]{1,0:T(8,128)(2,1)}, bf16[1280,128]{1,0:T(8,128)(2,1)}, f32[64,128]{1,0:T(8,128)}, f32[1,64]{1,0:T(1,...) custom-call(s32[1]{0:T(128)} %bitcast.me, f32[64,2048]{1,0:T(8,128)} %get-tuple-element.46.rk, f32[64,2048]{1,0:T(8,128)} %get-tuple-element.47.rv, ...), custom_call_target="tpu_custom_call" | custom-call | flops 1048576 | bytes 1572864 | tf_op jit(solution)/shard_map/first/pallas_call | solution.py:307
  24.5 0.7 convert_bitcast_fusion
  25.2 1.5 collective-permute-start.36
  27.2 1.5 collective-permute-done.36
  28.8 0.7 broadcast_select_fusion.5
  29.5 1.6 collective-permute-start.37
  31.7 0.6 copy-done.26
  32.3 2.1 %third.1 = (bf16[256,896]{1,0:T(8,128)(2,1)}, f32[1,896]{1,0:T(1,128)}, f32[1,1024]{1,0:T(1,128)}) custom-call(f32[2048,1024]{1,0:T(8,128)} %get-tuple-element.32.rq.refs_0_.refs_1_.refs_2_.refs_3_.refs_4_.refs_5_.refs_6_, f32[1,1024]{1,0:T(1,128)} %get-tuple-element.36.refs_0_, f32[1,1024]{1,0:T(1,128)} %copy-done.26, f32[1,1024]{1,0:T(1,128)} %copy-done.25, ...), custom_call_target="tpu_custom_call" | custom-call | flops 1835008 | bytes 1376256 | tf_op jit(solution)/shard_map/third/pallas_call | solution.py:360
  34.4 5.0 %fourth.1 = (bf16[256,896]{1,0:T(8,128)(2,1)}, bf16[512,896]{1,0:T(8,128)(2,1)}, bf16[512,896]{1,0:T(8,128)(2,1)}, bf16[256,896]{1,0:T(8,128)(2,1)}, bf16[128,89...) custom-call(f32[1,896]{1,0:T(1,128)} %get-tuple-element.37.inv, ...), custom_call_target="tpu_custom_call" | custom-call | flops 14680064 | bytes 11010048 | tf_op jit(solution)/shard_map/fourth/pallas_call | solution.py:370
  39.4 1.5 collective-permute-start.3
  41.2 2.7 %collective-permute-start.38 = (bf16[4,4,256]{2,0,1:T(4,128)(2,1)S(1)}, bf16[4,4,256]{2,0,1:T(4,128)(2,1)S(1)}, u32[]{:S(2)}, u32[]{:S(2)}) collective-permute-start(bf16[4,4,256]{2,0,1:T(4,128)(2,1)S(1)} %pad_maximum_fusion.1), channel_id=1, source_target_pairs={{0,4},{1,5},{2,6},{3,7},{4,0},{5,1},{6,2},{7,3},{8,12},{9,13},{10,... | collective-permute-start | bytes 24584 | tf_op jit(solution)/shard_map/ppermute | solution.py:260
  43.8 2.0 %collective-permute-done.38 = bf16[4,4,256]{2,0,1:T(4,128)(2,1)S(1)} collective-permute-done((bf16[4,4,256]{2,0,1:T(4,128)(2,1)S(1)}, bf16[4,4,256]{2,0,1:T(4,128)(2,1)S(1)}, u32[]{:S(2)}, u32[]{:S(2)}) %collective-permute-start.38) | collective-permute-done | bytes 8224 | tf_op jit(solution)/shard_map/ppermute | solution.py:260
  45.8 0.6 collective-permute-start.5
  46.6 1.5 collective-permute-start.34
  48.1 4.0 %collective-permute-done.5.refs_2_ = bf16[64,896]{1,0:T(8,128)(2,1)S(1)} collective-permute-done((bf16[64,896]{1,0:T(8,128)(2,1)}, bf16[64,896]{1,0:T(8,128)(2,1)S(1)}, u32[]{:S(2)}, u32[]{:S(2)}) %collective-permute-start.5) | collective-permute-done | bytes 114720 | tf_op jit(solution)/shard_map/ppermute | solution.py:260
  52.6 1.5 collective-permute-start.7
  54.7 16.2 %collective-permute-done.7.refs_0_ = bf16[128,896]{1,0:T(8,128)(2,1)S(1)} collective-permute-done((bf16[128,896]{1,0:T(8,128)(2,1)}, bf16[128,896]{1,0:T(8,128)(2,1)S(1)}, u32[]{:S(2)}, u32[]{:S(2)}) %collective-permute-start.7) | collective-permute-done | bytes 229408 | tf_op jit(solution)/shard_map/ppermute | solution.py:260
  71.4 0.8 copy-done.17
  72.7 0.8 copy-done.13
  73.9 6.9 %collective-permute-done.40.refs_2_ = f32[64,1408]{1,0:T(8,128)S(1)} collective-permute-done((f32[64,1408]{1,0:T(8,128)S(1)}, f32[64,1408]{1,0:T(8,128)S(1)}, u32[]{:S(2)}, u32[]{:S(2)}) %collective-permute-start.40) | collective-permute-done | bytes 360480 | tf_op jit(solution)/shard_map/ppermute | solution.py:260
  81.3 1.6 collective-permute-done.32.refs_3_
  83.0 1.5 collective-permute-start.15
  85.2 0.8 copy-done.4
  86.0 1.3 collective-permute-start.13
  87.3 0.8 copy-done.5
  88.0 0.8 collective-permute-start.11
  88.8 5.7 %collective-permute-done.17.refs_2_ = bf16[256,896]{1,0:T(8,128)(2,1)} collective-permute-done((bf16[256,896]{1,0:T(8,128)(2,1)}, bf16[256,896]{1,0:T(8,128)(2,1)}, u32[]{:S(2)}, u32[]{:S(2)}) %collective-permute-start.17) | collective-permute-done | bytes 458784 | tf_op jit(solution)/shard_map/ppermute | solution.py:260
  94.5 9.8 %collective-permute-done.15.refs_0_ = bf16[256,896]{1,0:T(8,128)(2,1)} collective-permute-done((bf16[256,896]{1,0:T(8,128)(2,1)S(1)}, bf16[256,896]{1,0:T(8,128)(2,1)}, u32[]{:S(2)}, u32[]{:S(2)}) %collective-permute-start.15) | collective-permute-done | bytes 458784 | tf_op jit(solution)/shard_map/ppermute | solution.py:260
  104.3 9.8 %collective-permute-done.9.refs_0_ = bf16[256,896]{1,0:T(8,128)(2,1)} collective-permute-done((bf16[256,896]{1,0:T(8,128)(2,1)}, bf16[256,896]{1,0:T(8,128)(2,1)}, u32[]{:S(2)}, u32[]{:S(2)}) %collective-permute-start.9) | collective-permute-done | bytes 458784 | tf_op jit(solution)/shard_map/ppermute | solution.py:260
  114.8 18.9 %collective-permute-done.13.refs_0_ = bf16[512,896]{1,0:T(8,128)(2,1)S(1)} collective-permute-done((bf16[512,896]{1,0:T(8,128)(2,1)}, bf16[512,896]{1,0:T(8,128)(2,1)S(1)}, u32[]{:S(2)}, u32[]{:S(2)}) %collective-permute-start.13) | collective-permute-done | bytes 917536 | tf_op jit(solution)/shard_map/ppermute | solution.py:260
  133.7 17.4 %collective-permute-done.11.refs_0_ = bf16[512,896]{1,0:T(8,128)(2,1)S(1)} collective-permute-done((bf16[512,896]{1,0:T(8,128)(2,1)}, bf16[512,896]{1,0:T(8,128)(2,1)S(1)}, u32[]{:S(2)}, u32[]{:S(2)}) %collective-permute-start.11) | collective-permute-done | bytes 917536 | tf_op jit(solution)/shard_map/ppermute | solution.py:260
  152.4 2.0 %collective-permute-done.18.refs_3_ = bf16[256,896]{1,0:T(8,128)(2,1)} collective-permute-done((bf16[256,896]{1,0:T(8,128)(2,1)}, bf16[256,896]{1,0:T(8,128)(2,1)}, u32[]{:S(2)}, u32[]{:S(2)}) %collective-permute-start.18) | collective-permute-done | bytes 458784 | tf_op jit(solution)/shard_map/ppermute | solution.py:260
  155.6 0.6 copy.26
  156.2 3.0 %shard_map.159.refs_16_ = bf16[8192,1024]{1,0:T(8,128)(2,1)} custom-call(s32[1]{0:T(128)} %bitcast.me, bf16[768,128]{1,0:T(8,128)(2,1)} %get-tuple-element.49.refs_0_, bf16[768,128]{1,0:T(8,128)(2,1)} %copy-done.21, bf16[768,128]{1,0:T(8,128)(2,1)} %collective-permute-done.31.refs_2_, bf16[768,128]{1,0:T(8,128)(2,1)} %copy-done.22, ...), custom_call_target="tpu_custom_call" | custom-call | flops 8388608 | bytes 4194304 | tf_op jit(solution)/shard_map/pallas_call | solution.py:387
  159.2 3.2 %place_kv.1 = (bf16[64,8192]{1,0:T(8,128)(2,1)}, bf16[64,8192]{1,0:T(8,128)(2,1)}) custom-call(s32[1]{0:T(128)} %bitcast.me, f32[64,128]{1,0:T(8,128)} %get-tuple-element.52.inv, f32[64,1408]{1,0:T(8,128)} %get-tuple-element.53.refs_0_, f32[64,1408]{1,0:T(8,128)} %copy-done.9, f32[64,1408]{1,0:T(8,128)} %copy-done.8, f32[64,1408]{1,0:T(8,128)} %copy-done.10, ...), custom_call_target="tpu_custom_call" | custom-call | flops 5505024 | bytes 2752512 | tf_op jit(solution)/shard_map/place_kv/pallas_call | solution.py:427
  162.3 6.1 %shard_map.160.refs_4_ = bf16[8192,1024]{1,0:T(8,128)(2,1)} custom-call(s32[1]{0:T(128)} %bitcast.me, bf16[256,896]{1,0:T(8,128)(2,1)} %get-tuple-element.44.refs_0_, bf16[256,896]{1,0:T(8,128)(2,1)} %copy-done.5, bf16[256,896]{1,0:T(8,128)(2,1)} %get-tuple-element.45.refs_2_, bf16[256,896]{1,0:T(8,128)(2,1)} %copy-done.3, ...), custom_call_target="tpu_custom_call", output_to_operand_aliasing={{}: (17, {})} | custom-call | flops 29360128 | bytes 14680064 | tf_op jit(solution)/shard_map/pallas_call | solution.py:387
  168.5 2.7 %shard_map.161.refs_2_ = bf16[8192,1024]{1,0:T(8,128)(2,1)} custom-call(s32[1]{0:T(128)} %bitcast.me, bf16[256,896]{1,0:T(8,128)(2,1)} %collective-permute-done.15.refs_0_, bf16[256,896]{1,0:T(8,128)(2,1)} %collective-permute-done.16.refs_1_, bf16[256,896]{1,0:T(8,128)(2,1)} %collective-permute-done.17.refs_2_, ...), custom_call_target="tpu_custom_call", output_to_operand_aliasing={{}: (5, {})} | custom-call | flops 7340032 | bytes 3670016 | tf_op jit(solution)/shard_map/pallas_call | solution.py:387
  171.2 2.7 %shard_map.162.refs_2_ = bf16[8192,1024]{1,0:T(8,128)(2,1)} custom-call(s32[1]{0:T(128)} %bitcast.me, bf16[512,896]{1,0:T(8,128)(2,1)} %copy-done, bf16[512,896]{1,0:T(8,128)(2,1)} %collective-permute-done.14.refs_1_, bf16[8192,1024]{1,0:T(8,128)(2,1)} %shard_map.161.refs_2_), custom_call_target="tpu_custom_call", output_to_operand_aliasing={{}: (3, {})} | custom-call | flops 7340032 | bytes 3670016 | tf_op jit(solution)/shard_map/pallas_call | solution.py:387
  173.9 2.7 %shard_map.163.refs_2_ = bf16[8192,1024]{1,0:T(8,128)(2,1)} custom-call(s32[1]{0:T(128)} %bitcast.me, bf16[512,896]{1,0:T(8,128)(2,1)} %copy-done.1, bf16[512,896]{1,0:T(8,128)(2,1)} %collective-permute-done.12.refs_1_, bf16[8192,1024]{1,0:T(8,128)(2,1)} %shard_map.162.refs_2_), custom_call_target="tpu_custom_call", output_to_operand_aliasing={{}: (3, {})} | custom-call | flops 7340032 | bytes 3670016 | tf_op jit(solution)/shard_map/pallas_call | solution.py:387
  176.7 0.8 copy-done.6
  177.5 2.1 %shard_map.164.refs_2_ = bf16[8192,1024]{1,0:T(8,128)(2,1)} custom-call(s32[1]{0:T(128)} %bitcast.me, bf16[256,896]{1,0:T(8,128)(2,1)} %collective-permute-done.9.refs_0_, bf16[256,896]{1,0:T(8,128)(2,1)} %copy-done.6, bf16[8192,1024]{1,0:T(8,128)(2,1)} %shard_map.163.refs_2_), custom_call_target="tpu_custom_call", output_to_operand_aliasing={{}: (3, {})} | custom-call | flops 3670016 | bytes 1835008 | tf_op jit(solution)/shard_map/pallas_call | solution.py:387
  179.6 0.8 shard_map.165.refs_4_
  180.4 0.8 shard_map.166
  (127 shorter events, 9.1 us)
Async XLA Ops:
  4.4 4.8 %collective-permute-start.28 = (f32[1,512]{1,0:T(1,128)}, f32[1,512]{1,0:T(1,128)S(1)}, u32[]{:S(2)}, u32[]{:S(2)}) collective-permute-start(f32[1,512]{1,0:T(1,128)} %get-tuple-element.48.refs_0_), channel_id=1, source_target_pairs={{0,16},{8,24},{16,0},{24,8},{1,17},{9,25},{17,1},{25,9},{2,18},{10... | collective-permute-start | bytes 6152 | tf_op jit(solution)/shard_map/ppermute | solution.py:260
  7.5 13.4 %collective-permute-start.27 = (f32[1,512]{1,0:T(1,128)}, f32[1,512]{1,0:T(1,128)S(1)}, u32[]{:S(2)}, u32[]{:S(2)}) collective-permute-start(f32[1,512]{1,0:T(1,128)} %get-tuple-element.48.refs_0_), channel_id=1, source_target_pairs={{0,8},{8,0},{16,24},{24,16},{1,9},{9,1},{17,25},{25,17},{2,10},{10... | collective-permute-start | bytes 6152 | tf_op jit(solution)/shard_map/ppermute | solution.py:260
  9.2 11.6 %collective-permute-start.29 = (f32[1,512]{1,0:T(1,128)S(1)}, f32[1,512]{1,0:T(1,128)S(1)}, u32[]{:S(2)}, u32[]{:S(2)}) collective-permute-start(f32[1,512]{1,0:T(1,128)S(1)} %collective-permute-done.28.refs_2_), channel_id=1, source_target_pairs={{0,8},{8,0},{16,24},{24,16},{1,9},{9,1},{17,25},{25,17},{2,10},{10... | collective-permute-start | bytes 6152 | tf_op jit(solution)/shard_map/ppermute | solution.py:260
  18.7 8.0 %collective-permute-start.1 = (f32[1,1024]{1,0:T(1,128)}, f32[1,1024]{1,0:T(1,128)S(1)}, u32[]{:S(2)}, u32[]{:S(2)}) collective-permute-start(f32[1,1024]{1,0:T(1,128)} %get-tuple-element.36.refs_0_), channel_id=1, source_target_pairs={{0,16},{8,24},{16,0},{24,8},{1,17},{9,25},{17,1},{25,9},{2,18},{10... | collective-permute-start | bytes 12296 | tf_op jit(solution)/shard_map/ppermute | solution.py:260
  25.2 3.6 %collective-permute-start.36 = (bf16[4,1,256]{2,0,1:T(4,128)(2,1)S(1)}, bf16[4,1,256]{2,0,1:T(4,128)(2,1)S(1)}, u32[]{:S(2)}, u32[]{:S(2)}) collective-permute-start(bf16[4,1,256]{2,0,1:T(4,128)(2,1)S(1)} %convert_bitcast_fusion), channel_id=1, source_target_pairs={{0,1},{1,0},{2,3},{3,2},{4,5},{5,4},{6,7},{7,6},{8,9},{9,8},{10,11... | collective-permute-start | bytes 6152 | tf_op jit(solution)/shard_map/ppermute | solution.py:260
  26.7 4.9 %collective-permute-start = (f32[1,1024]{1,0:T(1,128)S(1)}, f32[1,1024]{1,0:T(1,128)S(1)}, u32[]{:S(2)}, u32[]{:S(2)}) collective-permute-start(f32[1,1024]{1,0:T(1,128)S(1)} %copy-done.24), channel_id=1, source_target_pairs={{0,8},{8,0},{16,24},{24,16},{1,9},{9,1},{17,25},{25,17},{2,10},{10... | collective-permute-start | bytes 12296 | tf_op jit(solution)/shard_map/ppermute | solution.py:260
  26.7 4.9 %collective-permute-start.2 = (f32[1,1024]{1,0:T(1,128)S(1)}, f32[1,1024]{1,0:T(1,128)S(1)}, u32[]{:S(2)}, u32[]{:S(2)}) collective-permute-start(f32[1,1024]{1,0:T(1,128)S(1)} %collective-permute-done.1.refs_2_), channel_id=1, source_target_pairs={{0,8},{8,0},{16,24},{24,16},{1,9},{9,1},{17,25},{25,17},{2,10},{10... | collective-permute-start | bytes 12296 | tf_op jit(solution)/shard_map/ppermute | solution.py:260
  29.5 11.6 %collective-permute-start.37 = (bf16[4,2,256]{2,0,1:T(4,128)(2,1)S(1)}, bf16[4,2,256]{2,0,1:T(4,128)(2,1)S(1)}, u32[]{:S(2)}, u32[]{:S(2)}) collective-permute-start(bf16[4,2,256]{2,0,1:T(4,128)(2,1)S(1)} %pad_maximum_fusion.2), channel_id=1, source_target_pairs={{0,2},{1,3},{2,0},{3,1},{4,6},{5,7},{6,4},{7,5},{8,10},{9,11},{10,... | collective-permute-start | bytes 12296 | tf_op jit(solution)/shard_map/ppermute | solution.py:260
  31.1 21.5 %collective-permute-start.31 = (bf16[768,128]{1,0:T(8,128)(2,1)}, bf16[768,128]{1,0:T(8,128)(2,1)}, u32[]{:S(2)}, u32[]{:S(2)}) collective-permute-start(bf16[768,128]{1,0:T(8,128)(2,1)} %get-tuple-element.49.refs_0_), channel_id=1, source_target_pairs={{0,16},{8,24},{16,0},{24,8},{1,17},{9,25},{17,1},{25,9},{2,18},{10... | collective-permute-start | bytes 589832 | tf_op jit(solution)/shard_map/ppermute | solution.py:260
  39.4 6.4 %collective-permute-start.25 = (bf16[64,896]{1,0:T(8,128)(2,1)}, bf16[64,896]{1,0:T(8,128)(2,1)}, u32[]{:S(2)}, u32[]{:S(2)}) collective-permute-start(bf16[64,896]{1,0:T(8,128)(2,1)} %get-tuple-element.38.refs_12_), channel_id=1, source_target_pairs={{0,8},{8,0},{16,24},{24,16},{1,9},{9,1},{17,25},{25,17},{2,10},{10... | collective-permute-start | bytes 344072 | tf_op jit(solution)/shard_map/ppermute | solution.py:260
  39.4 7.2 %collective-permute-start.3 = (bf16[64,896]{1,0:T(8,128)(2,1)}, bf16[64,896]{1,0:T(8,128)(2,1)S(1)}, u32[]{:S(2)}, u32[]{:S(2)}) collective-permute-start(bf16[64,896]{1,0:T(8,128)(2,1)} %get-tuple-element.38.refs_12_), channel_id=1, source_target_pairs={{0,16},{8,24},{16,0},{24,8},{1,17},{9,25},{17,1},{25,9},{2,18},{10... | collective-permute-start | bytes 344072 | tf_op jit(solution)/shard_map/ppermute | solution.py:260
  40.9 5.4 %collective-permute-start.26 = (bf16[64,896]{1,0:T(8,128)(2,1)}, bf16[64,896]{1,0:T(8,128)(2,1)S(1)}, u32[]{:S(2)}, u32[]{:S(2)}) collective-permute-start(bf16[64,896]{1,0:T(8,128)(2,1)} %get-tuple-element.39.refs_14_), channel_id=1, source_target_pairs={{0,8},{8,0},{16,24},{24,16},{1,9},{9,1},{17,25},{25,17},{2,10},{10... | collective-permute-start | bytes 344072 | tf_op jit(solution)/shard_map/ppermute | solution.py:260
  41.2 4.6 %collective-permute-start.38 = (bf16[4,4,256]{2,0,1:T(4,128)(2,1)S(1)}, bf16[4,4,256]{2,0,1:T(4,128)(2,1)S(1)}, u32[]{:S(2)}, u32[]{:S(2)}) collective-permute-start(bf16[4,4,256]{2,0,1:T(4,128)(2,1)S(1)} %pad_maximum_fusion.1), channel_id=1, source_target_pairs={{0,4},{1,5},{2,6},{3,7},{4,0},{5,1},{6,2},{7,3},{8,12},{9,13},{10,... | collective-permute-start | bytes 24584 | tf_op jit(solution)/shard_map/ppermute | solution.py:260
  45.8 8.3 %collective-permute-start.30 = (bf16[768,128]{1,0:T(8,128)(2,1)S(1)}, bf16[768,128]{1,0:T(8,128)(2,1)S(1)}, u32[]{:S(2)}, u32[]{:S(2)}) collective-permute-start(bf16[768,128]{1,0:T(8,128)(2,1)S(1)} %copy-done.20), channel_id=1, source_target_pairs={{0,8},{8,0},{16,24},{24,16},{1,9},{9,1},{17,25},{25,17},{2,10},{10... | collective-permute-start | bytes 589832 | tf_op jit(solution)/shard_map/ppermute | solution.py:260
  45.8 6.3 %collective-permute-start.5 = (bf16[64,896]{1,0:T(8,128)(2,1)}, bf16[64,896]{1,0:T(8,128)(2,1)S(1)}, u32[]{:S(2)}, u32[]{:S(2)}) collective-permute-start(bf16[64,896]{1,0:T(8,128)(2,1)} %get-tuple-element.39.refs_14_), channel_id=1, source_target_pairs={{0,16},{8,24},{16,0},{24,8},{1,17},{9,25},{17,1},{25,9},{2,18},{10... | collective-permute-start | bytes 344072 | tf_op jit(solution)/shard_map/ppermute | solution.py:260
  46.4 7.8 %collective-permute-start.24 = (bf16[128,896]{1,0:T(8,128)(2,1)}, bf16[128,896]{1,0:T(8,128)(2,1)S(1)}, u32[]{:S(2)}, u32[]{:S(2)}) collective-permute-start(bf16[128,896]{1,0:T(8,128)(2,1)} %get-tuple-element.40.refs_10_), channel_id=1, source_target_pairs={{0,8},{8,0},{16,24},{24,16},{1,9},{9,1},{17,25},{25,17},{2,10},{10... | collective-permute-start | bytes 688136 | tf_op jit(solution)/shard_map/ppermute | solution.py:260
  46.6 24.9 %collective-permute-start.34 = (bf16[1280,128]{1,0:T(8,128)(2,1)S(1)}, bf16[1280,128]{1,0:T(8,128)(2,1)S(1)}, u32[]{:S(2)}, u32[]{:S(2)}) collective-permute-start(bf16[1280,128]{1,0:T(8,128)(2,1)S(1)} %copy-done.15), channel_id=1, source_target_pairs={{0,16},{8,24},{16,0},{24,8},{1,17},{9,25},{17,1},{25,9},{2,18},{10... | collective-permute-start | bytes 983048 | tf_op jit(solution)/shard_map/ppermute | solution.py:260
  52.1 20.6 %collective-permute-start.43 = (bf16[64,2688]{1,0:T(8,128)(2,1)S(1)}, bf16[64,2688]{1,0:T(8,128)(2,1)S(1)}, u32[]{:S(2)}, u32[]{:S(2)}) collective-permute-start(bf16[64,2688]{1,0:T(8,128)(2,1)S(1)} %copy-done.11), channel_id=1, source_target_pairs={{0,16},{8,24},{16,0},{24,8},{1,17},{9,25},{17,1},{25,9},{2,18},{10... | collective-permute-start | bytes 1032200 | tf_op jit(solution)/shard_map/ppermute | solution.py:260
  52.6 18.2 %collective-permute-start.7 = (bf16[128,896]{1,0:T(8,128)(2,1)}, bf16[128,896]{1,0:T(8,128)(2,1)S(1)}, u32[]{:S(2)}, u32[]{:S(2)}) collective-permute-start(bf16[128,896]{1,0:T(8,128)(2,1)} %get-tuple-element.40.refs_10_), channel_id=1, source_target_pairs={{0,16},{8,24},{16,0},{24,8},{1,17},{9,25},{17,1},{25,9},{2,18},{10... | collective-permute-start | bytes 688136 | tf_op jit(solution)/shard_map/ppermute | solution.py:260
  54.1 17.3 %collective-permute-start.33 = (bf16[1280,128]{1,0:T(8,128)(2,1)S(1)}, bf16[1280,128]{1,0:T(8,128)(2,1)S(1)}, u32[]{:S(2)}, u32[]{:S(2)}) collective-permute-start(bf16[1280,128]{1,0:T(8,128)(2,1)S(1)} %copy-done.15), channel_id=1, source_target_pairs={{0,8},{8,0},{16,24},{24,16},{1,9},{9,1},{17,25},{25,17},{2,10},{10... | collective-permute-start | bytes 983048 | tf_op jit(solution)/shard_map/ppermute | solution.py:260
  54.2 98.2 %copy-start.19 = (bf16[128,896]{1,0:T(8,128)(2,1)}, bf16[128,896]{1,0:T(8,128)(2,1)S(1)}, u32[]{:S(2)}) copy-start(bf16[128,896]{1,0:T(8,128)(2,1)S(1)} %collective-permute-done.24.refs_11_) | copy-start | bytes 688132
  54.2 18.5 %collective-permute-start.42 = (bf16[64,2688]{1,0:T(8,128)(2,1)S(1)}, bf16[64,2688]{1,0:T(8,128)(2,1)S(1)}, u32[]{:S(2)}, u32[]{:S(2)}) collective-permute-start(bf16[64,2688]{1,0:T(8,128)(2,1)S(1)} %copy-done.11), channel_id=1, source_target_pairs={{0,8},{8,0},{16,24},{24,16},{1,9},{9,1},{17,25},{25,17},{2,10},{10... | collective-permute-start | bytes 1032200 | tf_op jit(solution)/shard_map/ppermute | solution.py:260
  70.9 9.9 %collective-permute-start.40 = (f32[64,1408]{1,0:T(8,128)S(1)}, f32[64,1408]{1,0:T(8,128)S(1)}, u32[]{:S(2)}, u32[]{:S(2)}) collective-permute-start(f32[64,1408]{1,0:T(8,128)S(1)} %copy-done.7), channel_id=1, source_target_pairs={{0,16},{8,24},{16,0},{24,8},{1,17},{9,25},{17,1},{25,9},{2,18},{10... | collective-permute-start | bytes 1081352 | tf_op jit(solution)/shard_map/ppermute | solution.py:260
  71.4 9.9 %collective-permute-start.39 = (f32[64,1408]{1,0:T(8,128)S(1)}, f32[64,1408]{1,0:T(8,128)S(1)}, u32[]{:S(2)}, u32[]{:S(2)}) collective-permute-start(f32[64,1408]{1,0:T(8,128)S(1)} %copy-done.7), channel_id=1, source_target_pairs={{0,8},{8,0},{16,24},{24,16},{1,9},{9,1},{17,25},{25,17},{2,10},{10... | collective-permute-start | bytes 1081352 | tf_op jit(solution)/shard_map/ppermute | solution.py:260
  72.2 12.3 %collective-permute-start.20 = (bf16[256,896]{1,0:T(8,128)(2,1)}, bf16[256,896]{1,0:T(8,128)(2,1)S(1)}, u32[]{:S(2)}, u32[]{:S(2)}) collective-permute-start(bf16[256,896]{1,0:T(8,128)(2,1)} %get-tuple-element.45.refs_2_), channel_id=1, source_target_pairs={{0,8},{8,0},{16,24},{24,16},{1,9},{9,1},{17,25},{25,17},{2,10},{10... | collective-permute-start | bytes 1376264 | tf_op jit(solution)/shard_map/ppermute | solution.py:260
  72.7 12.3 %collective-permute-start.23 = (bf16[256,896]{1,0:T(8,128)(2,1)}, bf16[256,896]{1,0:T(8,128)(2,1)S(1)}, u32[]{:S(2)}, u32[]{:S(2)}) collective-permute-start(bf16[256,896]{1,0:T(8,128)(2,1)} %get-tuple-element.41.refs_8_), channel_id=1, source_target_pairs={{0,8},{8,0},{16,24},{24,16},{1,9},{9,1},{17,25},{25,17},{2,10},{10... | collective-permute-start | bytes 1376264 | tf_op jit(solution)/shard_map/ppermute | solution.py:260
  73.5 13.8 %collective-permute-start.19 = (bf16[256,896]{1,0:T(8,128)(2,1)S(1)}, bf16[256,896]{1,0:T(8,128)(2,1)S(1)}, u32[]{:S(2)}, u32[]{:S(2)}) collective-permute-start(bf16[256,896]{1,0:T(8,128)(2,1)S(1)} %copy-done.2), channel_id=1, source_target_pairs={{0,8},{8,0},{16,24},{24,16},{1,9},{9,1},{17,25},{25,17},{2,10},{10... | collective-permute-start | bytes 1376264 | tf_op jit(solution)/shard_map/ppermute | solution.py:260
  80.8 71.0 %copy-start.8 = (f32[64,1408]{1,0:T(8,128)}, f32[64,1408]{1,0:T(8,128)S(1)}, u32[]{:S(2)}) copy-start(f32[64,1408]{1,0:T(8,128)S(1)} %collective-permute-done.40.refs_2_) | copy-start | bytes 1081348
  80.8 13.7 %collective-permute-start.17 = (bf16[256,896]{1,0:T(8,128)(2,1)}, bf16[256,896]{1,0:T(8,128)(2,1)}, u32[]{:S(2)}, u32[]{:S(2)}) collective-permute-start(bf16[256,896]{1,0:T(8,128)(2,1)} %get-tuple-element.45.refs_2_), channel_id=1, source_target_pairs={{0,16},{8,24},{16,0},{24,8},{1,17},{9,25},{17,1},{25,9},{2,18},{10... | collective-permute-start | bytes 1376264 | tf_op jit(solution)/shard_map/ppermute | solution.py:260
  81.3 70.4 %copy-start.9 = (f32[64,1408]{1,0:T(8,128)}, f32[64,1408]{1,0:T(8,128)S(1)}, u32[]{:S(2)}) copy-start(f32[64,1408]{1,0:T(8,128)S(1)} %collective-permute-done.39.refs_1_) | copy-start | bytes 1081348
  81.3 1.7 collective-permute-start.32
  83.0 21.3 %collective-permute-start.15 = (bf16[256,896]{1,0:T(8,128)(2,1)S(1)}, bf16[256,896]{1,0:T(8,128)(2,1)}, u32[]{:S(2)}, u32[]{:S(2)}) collective-permute-start(bf16[256,896]{1,0:T(8,128)(2,1)S(1)} %copy-done.2), channel_id=1, source_target_pairs={{0,16},{8,24},{16,0},{24,8},{1,17},{9,25},{17,1},{25,9},{2,18},{10... | collective-permute-start | bytes 1376264 | tf_op jit(solution)/shard_map/ppermute | solution.py:260
  84.5 29.7 %collective-permute-start.9 = (bf16[256,896]{1,0:T(8,128)(2,1)}, bf16[256,896]{1,0:T(8,128)(2,1)}, u32[]{:S(2)}, u32[]{:S(2)}) collective-permute-start(bf16[256,896]{1,0:T(8,128)(2,1)} %get-tuple-element.41.refs_8_), channel_id=1, source_target_pairs={{0,16},{8,24},{16,0},{24,8},{1,17},{9,25},{17,1},{25,9},{2,18},{10... | collective-permute-start | bytes 1376264 | tf_op jit(solution)/shard_map/ppermute | solution.py:260
  86.0 47.7 %collective-permute-start.13 = (bf16[512,896]{1,0:T(8,128)(2,1)}, bf16[512,896]{1,0:T(8,128)(2,1)S(1)}, u32[]{:S(2)}, u32[]{:S(2)}) collective-permute-start(bf16[512,896]{1,0:T(8,128)(2,1)} %get-tuple-element.43.refs_4_), channel_id=1, source_target_pairs={{0,16},{8,24},{16,0},{24,8},{1,17},{9,25},{17,1},{25,9},{2,18},{10... | collective-permute-start | bytes 2752520 | tf_op jit(solution)/shard_map/ppermute | solution.py:260
  88.0 63.1 %collective-permute-start.11 = (bf16[512,896]{1,0:T(8,128)(2,1)}, bf16[512,896]{1,0:T(8,128)(2,1)S(1)}, u32[]{:S(2)}, u32[]{:S(2)}) collective-permute-start(bf16[512,896]{1,0:T(8,128)(2,1)} %get-tuple-element.42.refs_6_), channel_id=1, source_target_pairs={{0,16},{8,24},{16,0},{24,8},{1,17},{9,25},{17,1},{25,9},{2,18},{10... | collective-permute-start | bytes 2752520 | tf_op jit(solution)/shard_map/ppermute | solution.py:260
  94.5 19.7 %collective-permute-start.35 = (bf16[1280,128]{1,0:T(8,128)(2,1)S(1)}, bf16[1280,128]{1,0:T(8,128)(2,1)S(1)}, u32[]{:S(2)}, u32[]{:S(2)}) collective-permute-start(bf16[1280,128]{1,0:T(8,128)(2,1)S(1)} %collective-permute-done.34.refs_6_), channel_id=1, source_target_pairs={{0,8},{8,0},{16,24},{24,16},{1,9},{9,1},{17,25},{25,17},{2,10},{10... | collective-permute-start | bytes 983048 | tf_op jit(solution)/shard_map/ppermute | solution.py:260
  104.3 10.4 %collective-permute-start.44 = (bf16[64,2688]{1,0:T(8,128)(2,1)S(1)}, bf16[64,2688]{1,0:T(8,128)(2,1)S(1)}, u32[]{:S(2)}, u32[]{:S(2)}) collective-permute-start(bf16[64,2688]{1,0:T(8,128)(2,1)S(1)} %collective-permute-done.43.refs_6_), channel_id=1, source_target_pairs={{0,8},{8,0},{16,24},{24,16},{1,9},{9,1},{17,25},{25,17},{2,10},{10... | collective-permute-start | bytes 1032200 | tf_op jit(solution)/shard_map/ppermute | solution.py:260
  114.1 37.5 %collective-permute-start.21 = (bf16[512,896]{1,0:T(8,128)(2,1)}, bf16[512,896]{1,0:T(8,128)(2,1)}, u32[]{:S(2)}, u32[]{:S(2)}) collective-permute-start(bf16[512,896]{1,0:T(8,128)(2,1)} %get-tuple-element.43.refs_4_), channel_id=1, source_target_pairs={{0,8},{8,0},{16,24},{24,16},{1,9},{9,1},{17,25},{25,17},{2,10},{10... | collective-permute-start | bytes 2752520 | tf_op jit(solution)/shard_map/ppermute | solution.py:260
  114.2 37.6 %collective-permute-start.22 = (bf16[512,896]{1,0:T(8,128)(2,1)}, bf16[512,896]{1,0:T(8,128)(2,1)}, u32[]{:S(2)}, u32[]{:S(2)}) collective-permute-start(bf16[512,896]{1,0:T(8,128)(2,1)} %get-tuple-element.42.refs_6_), channel_id=1, source_target_pairs={{0,8},{8,0},{16,24},{24,16},{1,9},{9,1},{17,25},{25,17},{2,10},{10... | collective-permute-start | bytes 2752520 | tf_op jit(solution)/shard_map/ppermute | solution.py:260
  114.7 36.5 %collective-permute-start.41 = (f32[64,1408]{1,0:T(8,128)S(1)}, f32[64,1408]{1,0:T(8,128)S(1)}, u32[]{:S(2)}, u32[]{:S(2)}) collective-permute-start(f32[64,1408]{1,0:T(8,128)S(1)} %collective-permute-done.40.refs_2_), channel_id=1, source_target_pairs={{0,8},{8,0},{16,24},{24,16},{1,9},{9,1},{17,25},{25,17},{2,10},{10... | collective-permute-start | bytes 1081352 | tf_op jit(solution)/shard_map/ppermute | solution.py:260
  133.7 21.5 %collective-permute-start.14 = (bf16[512,896]{1,0:T(8,128)(2,1)S(1)}, bf16[512,896]{1,0:T(8,128)(2,1)}, u32[]{:S(2)}, u32[]{:S(2)}) collective-permute-start(bf16[512,896]{1,0:T(8,128)(2,1)S(1)} %collective-permute-done.13.refs_0_), channel_id=1, source_target_pairs={{0,8},{8,0},{16,24},{24,16},{1,9},{9,1},{17,25},{25,17},{2,10},{10... | collective-permute-start | bytes 2752520 | tf_op jit(solution)/shard_map/ppermute | solution.py:260
  151.1 22.8 %collective-permute-start.12 = (bf16[512,896]{1,0:T(8,128)(2,1)S(1)}, bf16[512,896]{1,0:T(8,128)(2,1)}, u32[]{:S(2)}, u32[]{:S(2)}) collective-permute-start(bf16[512,896]{1,0:T(8,128)(2,1)S(1)} %collective-permute-done.11.refs_0_), channel_id=1, source_target_pairs={{0,8},{8,0},{16,24},{24,16},{1,9},{9,1},{17,25},{25,17},{2,10},{10... | collective-permute-start | bytes 2752520 | tf_op jit(solution)/shard_map/ppermute | solution.py:260
  151.1 3.2 %collective-permute-start.18 = (bf16[256,896]{1,0:T(8,128)(2,1)}, bf16[256,896]{1,0:T(8,128)(2,1)}, u32[]{:S(2)}, u32[]{:S(2)}) collective-permute-start(bf16[256,896]{1,0:T(8,128)(2,1)} %collective-permute-done.17.refs_2_), channel_id=1, source_target_pairs={{0,8},{8,0},{16,24},{24,16},{1,9},{9,1},{17,25},{25,17},{2,10},{10... | collective-permute-start | bytes 1376264 | tf_op jit(solution)/shard_map/ppermute | solution.py:260
  151.6 3.4 %collective-permute-start.16 = (bf16[256,896]{1,0:T(8,128)(2,1)}, bf16[256,896]{1,0:T(8,128)(2,1)}, u32[]{:S(2)}, u32[]{:S(2)}) collective-permute-start(bf16[256,896]{1,0:T(8,128)(2,1)} %collective-permute-done.15.refs_0_), channel_id=1, source_target_pairs={{0,8},{8,0},{16,24},{24,16},{1,9},{9,1},{17,25},{25,17},{2,10},{10... | collective-permute-start | bytes 1376264 | tf_op jit(solution)/shard_map/ppermute | solution.py:260
  151.9 24.7 %collective-permute-start.10 = (bf16[256,896]{1,0:T(8,128)(2,1)}, bf16[256,896]{1,0:T(8,128)(2,1)S(1)}, u32[]{:S(2)}, u32[]{:S(2)}) collective-permute-start(bf16[256,896]{1,0:T(8,128)(2,1)} %collective-permute-done.9.refs_0_), channel_id=1, source_target_pairs={{0,8},{8,0},{16,24},{24,16},{1,9},{9,1},{17,25},{25,17},{2,10},{10... | collective-permute-start | bytes 1376264 | tf_op jit(solution)/shard_map/ppermute | solution.py:260
  154.4 25.2 %collective-permute-start.8 = (bf16[128,896]{1,0:T(8,128)(2,1)S(1)}, bf16[128,896]{1,0:T(8,128)(2,1)S(1)}, u32[]{:S(2)}, u32[]{:S(2)}) collective-permute-start(bf16[128,896]{1,0:T(8,128)(2,1)S(1)} %collective-permute-done.7.refs_0_), channel_id=1, source_target_pairs={{0,8},{8,0},{16,24},{24,16},{1,9},{9,1},{17,25},{25,17},{2,10},{10... | collective-permute-start | bytes 688136 | tf_op jit(solution)/shard_map/ppermute | solution.py:260
  155.0 25.3 %collective-permute-start.4 = (bf16[64,896]{1,0:T(8,128)(2,1)S(1)}, bf16[64,896]{1,0:T(8,128)(2,1)S(1)}, u32[]{:S(2)}, u32[]{:S(2)}) collective-permute-start(bf16[64,896]{1,0:T(8,128)(2,1)S(1)} %collective-permute-done.3.refs_0_), channel_id=1, source_target_pairs={{0,8},{8,0},{16,24},{24,16},{1,9},{9,1},{17,25},{25,17},{2,10},{10... | collective-permute-start | bytes 344072 | tf_op jit(solution)/shard_map/ppermute | solution.py:260
  155.2 25.2 %collective-permute-start.6 = (bf16[64,896]{1,0:T(8,128)(2,1)S(1)}, bf16[64,896]{1,0:T(8,128)(2,1)S(1)}, u32[]{:S(2)}, u32[]{:S(2)}) collective-permute-start(bf16[64,896]{1,0:T(8,128)(2,1)S(1)} %collective-permute-done.5.refs_2_), channel_id=1, source_target_pairs={{0,8},{8,0},{16,24},{24,16},{1,9},{9,1},{17,25},{25,17},{2,10},{10... | collective-permute-start | bytes 344072 | tf_op jit(solution)/shard_map/ppermute | solution.py:260
  (28 other events, 395.2 us)

commit v2 on v1

--- a/solution.py
+++ b/solution.py
@@ -66,7 +66,8 @@
     return wait
 
 
-PARTS = 4
+PARTS = 1
+PARTS_Q = 2
 
 
 def narrow_kernel(places, wq, sq, wk, sk, wv, sv, nt, ns, rk, rv, early, message, *refs):
@@ -76,7 +77,7 @@
     heads, rows = of_kv[0].shape
     wait_kv = load((wk, sk, wv, sv), of_kv, PARTS, in_kv)
     wait_gain = load((nt, ns), (gain_a, gain_b), 1, in_gain)
-    wait_q = load((wq, sq), of_q, PARTS, in_q)
+    wait_q = load((wq, sq), of_q, PARTS_Q, in_q)
     step = heads // PARTS
     writes = []
 
@@ -97,8 +98,8 @@
             if which == 0:
                 write(s.at[at, pl.ds(0, early.shape[1])], early.at[at, :])
     total = jnp.zeros((8, of_q[0].shape[1]), jnp.float32)
-    step = rows // PARTS
-    for part in range(PARTS):
+    step = rows // PARTS_Q
+    for part in range(PARTS_Q):
         wait_q(part)
         at = pl.ds(part * step, step)
         total = total + row_sum(jnp.abs(average(of_q[1][at, :], of_q[0][at, :])))
@@ -121,30 +122,27 @@
     return pieces[0]
 
 
-def first_kernel(places, gain, count, me, rk, rv, wq, sq, *refs):
+def first_kernel(places, heads, gain, count, me, rk, wq, sq, *refs):
     n = len(refs) - 7
-    messages, (own, own_a, own_b, inv_k, factor_k, factor_v, norms) = refs[:n], refs[n:]
+    messages, (own_k, own_a, own_b, inv_k, factor_k, factor_v, norms) = refs[:n], refs[n:]
     place_kv, place_norm = places
-    heads, rows = rk.shape
     pieces = [m[...] for m in messages]
     for distance, piece in enumerate(pieces):
         norms[pl.ds(me[0] ^ distance, 1), :] = piece[:, place_norm : place_norm + gain]
     total = tree(pieces) / count
+    scale = 1.0 / total[:, : own_a.shape[1]]
     first = 0
     for part in (own_a, own_b):
         at = pl.ds(first, part.shape[0])
         first += part.shape[0]
-        part[...] = (average(sq[at, :], wq[at, :]) / total[:, : part.shape[1]]).astype(
-            jnp.bfloat16
-        )
+        part[...] = (average(sq[at, :], wq[at, :]) * scale).astype(jnp.bfloat16)
     of_kv = total[:, place_kv : place_kv + 2 * heads]
     factor_k[...] = of_kv[:, :heads]
     factor_v[...] = of_kv[:, heads:]
-    inv = jnp.broadcast_to(1.0 / of_kv, (LANES, 2 * heads)).T
-    inv_k[...] = inv[:heads, :]
-    late = 2 * rows - own.shape[1]
-    scale_lanes(rk, inv[:heads, :], own, late, 0, rows - late)
-    scale_lanes(rv, inv[heads:, :], own, 0, rows - late, rows)
+    inv = jnp.broadcast_to(1.0 / of_kv[:, :heads], (LANES, heads)).T
+    inv_k[...] = inv
+    late = own_k.shape[1]
+    scale_lanes(rk, inv, own_k, rk.shape[1] - late, 0, late)
 
 
 def scale_lanes(source, scale, target, first, to, count):
@@ -154,60 +152,92 @@
         ).astype(jnp.bfloat16)
 
 
-def average_kernel(wq, sq, rq, message, w, s, note, in_w, in_s, outs, sent):
-    parts = in_w.shape[0]
+def sizes_kernel(wq, sq, message, w, s, note, ins, sent):
+    parts = ins.shape[0] // 2
     step = w.shape[0] // parts
 
     def copies(at):
         rows = pl.ds(pl.multiple_of(at * step, step), step)
         return (
-            pltpu.make_async_copy(wq.at[rows, :], w.at[rows, :], in_w.at[at]),
-            pltpu.make_async_copy(sq.at[rows, :], s.at[rows, :], in_s.at[at]),
-            pltpu.make_async_copy(s.at[rows, :], rq.at[rows, :], outs.at[at]),
+            pltpu.make_async_copy(wq.at[rows, :], w.at[rows, :], ins.at[2 * at]),
+            pltpu.make_async_copy(sq.at[rows, :], s.at[rows, :], ins.at[2 * at + 1]),
         )
 
     @pl.loop(0, parts)
     def _(at):
-        one, two, _ = copies(at)
-        one.start()
-        two.start()
+        for copy in copies(at):
+            copy.start()
 
     def body(at, total):
-        one, two, out = copies(at)
-        one.wait()
-        two.wait()
+        for copy in copies(at):
+            copy.wait()
         rows = pl.ds(pl.multiple_of(at * step, step), step)
-        new = average(s[rows, :], w[rows, :])
-        s[rows, :] = new
-        out.start()
-        return total + row_sum(jnp.abs(new))
+        return total + row_sum(jnp.abs(average(s[rows, :], w[rows, :])))
 
     total = lax.fori_loop(0, parts, body, jnp.zeros((8, w.shape[1]), jnp.float32))
     note[...] = jnp.sum(total, axis=0, keepdims=True)
     send = pltpu.make_async_copy(note, message, sent)
     send.start()
-
-    @pl.loop(0, parts)
-    def _(at):
-        copies(at)[2].wait()
-
     send.wait()
 
 
-def third_kernel(columns, count, rq, *refs):
+def third_kernel(columns, count, wq, sq, *refs):
     messages, (own, inv, factor) = refs[:-3], refs[-3:]
     total = tree([m[...] for m in messages]) / count
     factor[...] = total
     scale = 1.0 / total[:, columns:]
     inv[...] = scale
-    own[...] = (rq[:, columns:] * scale).astype(jnp.bfloat16)
-
-
-def fourth_kernel(inv, *refs):
-    half = len(refs) // 2
-    for source, own in zip(refs[:half], refs[half:]):
-        columns = source.shape[1] - own.shape[1]
-        own[...] = (source[:, columns:] * inv[...]).astype(jnp.bfloat16)
+    new = average(sq[:, columns:], wq[:, columns:])
+    own[...] = (new * scale).astype(jnp.bfloat16)
+
+
+def next_kernel(wq, sq, inv, own):
+    columns = wq.shape[1] - own.shape[1]
+    new = average(sq[:, columns:], wq[:, columns:])
+    own[...] = (new * inv[...]).astype(jnp.bfloat16)
+
+
+def fourth_kernel(sizes, wq, sq, inv, rq, *refs):
+    owns, (w, s, scale, narrow, ins, outs) = refs[: len(sizes) - 2], refs[len(sizes) - 2 :]
+    columns = w.shape[1] - narrow.shape[1]
+    pieces, first = [], 0
+    for chunk, size in enumerate(sizes):
+        step = min(size, sizes[0] // 2)
+        for at in range(0, size, step):
+            pieces.append((chunk, at, first + at, step))
+        first += size
+    pieces = [p for p in pieces if p[0] > 1] + [p for p in pieces if p[0] < 2]
+    loads, writes = [], []
+    known = pltpu.make_async_copy(inv, scale, ins.at[0])
+    known.start()
+    for at, (_, _, row, step) in enumerate(pieces):
+        rows = pl.ds(row, step)
+        loads.append(
+            (
+                pltpu.make_async_copy(wq.at[rows, :], w.at[rows, :], ins.at[2 * at + 1]),
+                pltpu.make_async_copy(sq.at[rows, :], s.at[rows, :], ins.at[2 * at + 2]),
+            )
+        )
+        for copy in loads[-1]:
+            copy.start()
+
+    def write(source, target):
+        writes.append(pltpu.make_async_copy(source, target, outs.at[len(writes)]))
+        writes[-1].start()
+
+    known.wait()
+    for (chunk, at, row, step), copies in zip(pieces, loads):
+        for copy in copies:
+            copy.wait()
+        rows = pl.ds(row, step)
+        new = average(s[rows, :], w[rows, :])
+        s[rows, :] = new
+        write(s.at[rows, :], rq.at[rows, :])
+        if chunk > 1:
+            narrow[rows, :] = (new[:, columns:] * scale[...]).astype(jnp.bfloat16)
+            write(narrow.at[rows, :], owns[chunk - 2].at[pl.ds(at, step), :])
+    for copy in writes:
+        copy.wait()
 
 
 def place_kernel(plan, rows, unread, me, *refs):
@@ -224,9 +254,10 @@
 
 
 def place_kv_kernel(n, me, inv, *refs):
-    early, pieces, (out_k, out_v, scaled, sems) = refs[:n], refs[n : 2 * n], refs[2 * n :]
+    early, keys, values = refs[:n], refs[n : 2 * n], refs[2 * n : 3 * n]
+    out_k, out_v, scaled, sems = refs[3 * n :]
     part = early[0].shape[1]
-    rows = (pieces[0].shape[1] + part) // 2
+    rows = values[0].shape[1]
     copies = []
 
     def move(source, target):
@@ -234,10 +265,9 @@
         copies[-1].start()
 
     starts = [pl.multiple_of((me[0] ^ distance) * rows, LANES) for distance in range(n)]
-    for start, piece in zip(starts, pieces):
-        late = rows - part
-        move(piece.at[:, pl.ds(0, late)], out_k.at[:, pl.ds(start + part, late)])
-        move(piece.at[:, pl.ds(late, rows)], out_v.at[:, pl.ds(start, rows)])
+    for start, key, value in zip(starts, keys, values):
+        move(key, out_k.at[:, pl.ds(start + part, rows - part)])
+        move(value, out_v.at[:, pl.ds(start, rows)])
     for distance, start in enumerate(starts):
         scale_lanes(early[distance], inv[...], scaled.at[distance], 0, 0, part)
         move(scaled.at[distance], out_k.at[:, pl.ds(start, part)])
@@ -246,6 +276,7 @@
 
 
 CUTS = (4, 4, 8, 8, 4, 2, 1, 1)
+CUT_A = 6
 
 
 def on_device(n, groups, wq, sq, wk, sk, wv, sv, norm_train, norm_step):
@@ -269,12 +300,12 @@
     once = lambda shape: pl.BlockSpec(shape, lambda i: (0, 0))
     full = lambda a: once(a.shape)
 
-    columns = max(LANES, width // 8)
+    columns = max(LANES, width // 4)
     place_kv = columns
     place_norm = place_kv + round_up(2 * heads, LANES)
     places = (place_kv, place_norm)
     length = place_norm + round_up(gain, LANES)
-    ahead = rows * 11 // 16 // LANES * LANES
+    ahead = rows * 9 // 16 // LANES * LANES
     rk, rv, early, message = pl.pallas_call(
         functools.partial(narrow_kernel, places),
         out_shape=(
@@ -293,7 +324,7 @@
             pltpu.VMEM((1, length), f32),
             pltpu.VMEM((2 * heads, LANES), f32),
             pltpu.SemaphoreType.DMA((4 * PARTS,)),
-            pltpu.SemaphoreType.DMA((2 * PARTS,)),
+            pltpu.SemaphoreType.DMA((2 * PARTS_Q,)),
             pltpu.SemaphoreType.DMA((2,)),
             pltpu.SemaphoreType.DMA((3 * PARTS + 1,)),
         ],
@@ -302,13 +333,15 @@
     )(wq, sq, wk.T, sk.T, wv.T, sv.T, norm_train[None], norm_step[None])
     messages = gather(message)
     found_early = gather(early)
-    cut_a = rows * 3 // 8
-    late = (heads, 2 * rows - ahead)
-    own_kv, *own_a, inv_k, factor_k, factor_v, norms = pl.pallas_call(
-        functools.partial(first_kernel, places, gain, n * rows),
+    total = tree(list(messages)) / (n * rows)
+    of_v = total[0, place_kv + heads : place_kv + 2 * heads, None]
+    own_v = (rv / of_v).astype(bf16)
+    cut_a = rows * CUT_A // 16
+    own_k, *own_a, inv_k, factor_k, factor_v, norms = pl.pallas_call(
+        functools.partial(first_kernel, places, heads, gain, n * rows),
         grid=(1,),
         out_shape=(
-            shaped(late, bf16),
+            shaped((heads, rows - ahead), bf16),
             shaped((cut_a, columns), bf16),
             shaped((rows - cut_a, columns), bf16),
             shaped((heads, LANES), f32),
@@ -316,12 +349,9 @@
             shaped((1, heads), f32),
             shaped((n, gain), f32),
         ),
-        in_specs=[SMEM]
-        + [full(rk)] * 2
-        + [once((rows, columns))] * 2
-        + [full(message)] * n,
+        in_specs=[SMEM, full(rk)] + [once((rows, columns))] * 2 + [full(message)] * n,
         out_specs=[
-            once(late),
+            once((heads, rows - ahead)),
             once((cut_a, columns)),
             once((rows - cut_a, columns)),
             once((heads, LANES)),
@@ -329,24 +359,23 @@
             once((1, heads)),
             once((n, gain)),
         ],
-        cost_estimate=cost(rows * heads * 8, rows * heads * 12),
+        cost_estimate=cost(rows * columns * 8, rows * columns * 12),
         name="first",
-    )(me, rk, rv, wq, sq, *messages)
-    found_kv = gather(own_kv)
+    )(me, rk, wq, sq, *messages)
+    found_v, found_k = gather(own_v), gather(own_k)
     found_a = [gather(piece) for piece in own_a]
 
-    parts = 16
-    rq, message_q = pl.pallas_call(
-        average_kernel,
-        out_shape=(shaped((rows, width), f32), shaped((1, width), f32)),
+    parts = 8
+    message_q = pl.pallas_call(
+        sizes_kernel,
+        out_shape=shaped((1, width), f32),
         in_specs=[HBM] * 2,
-        out_specs=[HBM] * 2,
+        out_specs=HBM,
         scratch_shapes=[pltpu.VMEM((rows, width), f32)] * 2
         + [pltpu.VMEM((1, width), f32)]
-        + [pltpu.SemaphoreType.DMA((parts,))] * 3
-        + [pltpu.SemaphoreType.DMA],
-        cost_estimate=cost(rows * width * 8, rows * width * 12),
-        name="average",
+        + [pltpu.SemaphoreType.DMA((2 * parts,)), pltpu.SemaphoreType.DMA],
+        cost_estimate=cost(rows * width * 8, rows * width * 8),
+        name="sizes",
     )(wq, sq)
     messages_q = gather(message_q)
 
@@ -361,22 +390,32 @@
         functools.partial(third_kernel, columns, n * rows),
         grid=(1,),
         out_shape=(narrow[0], shaped((1, rest), f32), shaped((1, width), f32)),
-        in_specs=[rows_of(0)] + [full(message_q)] * n,
+        in_specs=[rows_of(0)] * 2 + [full(message_q)] * n,
         out_specs=[full(narrow[0]), once((1, rest)), once((1, width))],
-        cost_estimate=cost(narrow[0].size * 8, narrow[0].size * 6),
+        cost_estimate=cost(narrow[0].size * 8, narrow[0].size * 10),
         name="third",
-    )(rq, *messages_q)
-    others = range(1, len(CUTS))
-    owns = pl.pallas_call(
-        fourth_kernel,
+    )(wq, sq, *messages_q)
+    own1 = pl.pallas_call(
+        next_kernel,
         grid=(1,),
-        out_shape=narrow[1:],
-        in_specs=[full(inv)] + [rows_of(at) for at in others],
-        out_specs=[full(narrow[at]) for at in others],
-        cost_estimate=cost(rows * rest * 8, rows * rest * 6),
+        out_shape=narrow[1],
+        in_specs=[rows_of(1)] * 2 + [full(inv)],
+        out_specs=full(narrow[1]),
+        cost_estimate=cost(narrow[1].size * 8, narrow[1].size * 10),
+        name="next",
+    )(wq, sq, inv)
+    rq, *owns = pl.pallas_call(
+        functools.partial(fourth_kernel, [c * unit for c in CUTS]),
+        out_shape=[shaped((rows, width), f32)] + narrow[2:],
+        in_specs=[HBM] * 3,
+        out_specs=[HBM] * (len(CUTS) - 1),
+        scratch_shapes=[pltpu.VMEM((rows, width), f32)] * 2
+        + [pltpu.VMEM((1, rest), f32), pltpu.VMEM((rows, rest), bf16)]
+        + [pltpu.SemaphoreType.DMA((65,)), pltpu.SemaphoreType.DMA((64,))],
+        cost_estimate=cost(rows * width * 8, rows * width * 14),
         name="fourth",
-    )(inv, *[rq for _ in others])
-    found = [gather(piece) for piece in [own0, *owns]]
+    )(wq, sq, inv)
+    found = [gather(piece) for piece in [own0, own1, *owns]]
 
     whole = shaped((n * rows, width), bf16)
     whole_kv = shaped((heads, n * rows), bf16)
@@ -420,15 +459,16 @@
     serve = gains.reshape(n * groups * gain)
 
     near, far = range(2), range(2, n)
-    final_q = place(
-        [(found_a[at][d], d, at * cut_a, 0) for at in range(2) for d in range(n)],
-    )
-    moved = n * own_kv.size * 2
+    final_q = place([(found_a[at][d], d, at * cut_a, 0) for at in range(2) for d in range(n)])
+    moved = n * own_v.size * 4
     final_k, final_v = pl.pallas_call(
         functools.partial(place_kv_kernel, n),
         grid=(1,),
         out_shape=[whole_kv] * 2,
-        in_specs=[SMEM, full(inv_k)] + [full(early)] * n + [full(own_kv)] * n,
+        in_specs=[SMEM, full(inv_k)]
+        + [full(early)] * n
+        + [full(own_k)] * n
+        + [full(own_v)] * n,
         out_specs=[HBM] * 2,
         scratch_shapes=[
             pltpu.VMEM((n, heads, ahead), bf16),
@@ -436,7 +476,7 @@
         ],
         cost_estimate=cost(moved * 4, 2 * moved),
         name="place_kv",
-    )(me, inv_k, *found_early, *found_kv)
+    )(me, inv_k, *found_early, *found_k, *found_v)
     for name, chunks, distances in (
         ("place_near", range(len(CUTS)), near),
         ("place1", (0, 1), far),

time: 182 us -> 186 us (1.022)
  Pallas kernels: 47.5 us -> 54.8 us
  waiting for transfers between devices: 98.2 us -> 92.6 us
  starting transfers between devices: 26.9 us -> 29.5 us
    pallas_call x3 -> x4, Pallas kernels: 17.5 us -> 24.5 us  [the longest x1 11.1 us: on_device(): pl.pallas_call(functools.partial(fourth_kernel, [c * unit for c in CUTS])...]
    ppermute x45 -> x48, waiting for transfers between devices: 98.2 us -> 92.6 us  [swap(): return lax.ppermute(array, axis, [(i, i ^ distance) for i in range(size)])]
    ppermute x45 -> x48, starting transfers between devices: 26.9 us -> 29.5 us  [swap(): return lax.ppermute(array, axis, [(i, i ^ distance) for i in range(size)])]
  transfers between devices with their start and end apart: 45 -> 48, of which waited for: 14 -> 15; matrix products, arithmetic and copies ran while one was open for 1% -> 2% of each run, Pallas kernels for 24% -> 27%
where the time goes in v2:
time: 186 us
  waiting for transfers between devices  92.6 us (50%)
  Pallas kernels  54.8 us (29%)
  starting transfers between devices  29.5 us (16%)
  local copies, waits for them, and re-layouts  5.69 us (3%)
  other arithmetic  2.31 us (1%)
    ppermute x48, waiting for transfers between devices, swap(): return lax.ppermute(array, axis, [(i, i ^ distance) for i in range(size)])  92.6 us
    ppermute x48, starting transfers between devices, swap(): return lax.ppermute(array, axis, [(i, i ^ distance) for i in range(size)])  29.5 us
    pallas_call x8, Pallas kernels, place(): pl.pallas_call(functools.partial(place_kernel, [job[1:] for job in jobs],...  20.9 us
    pallas_call x1, Pallas kernels, on_device(): pl.pallas_call(functools.partial(fourth_kernel, [c * unit for c in CUTS])...  11.1 us
    pallas_call x1, Pallas kernels, on_device(): pl.pallas_call(sizes_kernel, out_shape=shaped((1, width), f32), in_specs=...  6.87 us
    unnamed x63, local copies, waits for them, and re-layouts  5.68 us
    pallas_call x1, Pallas kernels, on_device(): pl.pallas_call(functools.partial(first_kernel, places, heads, gain, n * r...  4.06 us
    pallas_call x1, Pallas kernels, on_device(): pl.pallas_call(functools.partial(narrow_kernel, places), out_shape=(shape...  3.92 us
  transfers between devices with their start and end apart: 48, of which 15 were waited for; matrix products, arithmetic and copies ran while one was open for 2% of the time, Pallas kernels for 27%

profile of v2, /device:TPU:0, one launch (start us, length us, event | category | flops | bytes accessed | tf_op | source)
XLA Modules:
  0.0 186.0 jit_solution(8068304984450805868)
XLA Ops:
  0.6 3.9 %narrow.1 = (f32[64,2048]{1,0:T(8,128)}, f32[64,2048]{1,0:T(8,128)}, f32[64,1152]{1,0:T(8,128)}, f32[1,640]{1,0:T(1,128)}) custom-call(f32[2048,1024]{1,0:T(8,128)} %wq.11, f32[2048,1024]{1,0:T(8,128)} %sq.11, f32[64,2048]{1,0:T(8,128)} %bitcast.24, f32[64,2048]{1,0:T(8,128)} %bitcast.25, f32[64,2048]{1,0:T(8,128)} %bitcast.26, f32[64,2048]{1,0:T(8,128)} %bitcast.27, ...), custom_call_target="tpu_custom_call" | custom-call | flops 2097152 | bytes 4194304 | tf_op jit(solution)/shard_map/narrow/pallas_call | solution.py:309
  4.6 3.0 %collective-permute-start.28 = (f32[1,640]{1,0:T(1,128)}, f32[1,640]{1,0:T(1,128)S(1)}, u32[]{:S(2)}, u32[]{:S(2)}) collective-permute-start(f32[1,640]{1,0:T(1,128)} %get-tuple-element.42.refs_0_), channel_id=1, source_target_pairs={{0,16},{8,24},{16,0},{24,8},{1,17},{9,25},{17,1},{25,9},{2,18},{10... | collective-permute-start | bytes 7688 | tf_op jit(solution)/shard_map/ppermute | solution.py:291
  7.6 1.8 collective-permute-done.28.refs_2_
  9.4 6.9 %sizes.1.refs_0_ = f32[1,1024]{1,0:T(1,128)} custom-call(f32[2048,1024]{1,0:T(8,128)} %wq.11, f32[2048,1024]{1,0:T(8,128)} %sq.11), custom_call_target="tpu_custom_call" | custom-call | flops 16777216 | bytes 16777216 | tf_op jit(solution)/shard_map/sizes/pallas_call | solution.py:369
  16.3 2.1 %collective-permute-start.1 = (f32[1,1024]{1,0:T(1,128)}, f32[1,1024]{1,0:T(1,128)S(1)}, u32[]{:S(2)}, u32[]{:S(2)}) collective-permute-start(f32[1,1024]{1,0:T(1,128)} %sizes.1.refs_0_), channel_id=1, source_target_pairs={{0,16},{8,24},{16,0},{24,8},{1,17},{9,25},{17,1},{25,9},{2,18},{10... | collective-permute-start | bytes 12296 | tf_op jit(solution)/shard_map/ppermute | solution.py:291
  19.0 4.1 %first.1 = (bf16[64,896]{1,0:T(8,128)(2,1)}, bf16[768,256]{1,0:T(8,128)(2,1)}, bf16[1280,256]{1,0:T(8,128)(2,1)}, f32[64,128]{1,0:T(8,128)}, f32[1,64]{1,0:T(1,128)}, /*index=5*/f32[1,64]{1,0:T(1,128)}, f32[4,256]{1,0:T(4,128)}) custom-call(s32[1]{0:T(128)} %bitcast.me, f32[64,2048]{1,0:T(8,128)} %get-tuple-element.41.rk, f32[2048,1024]{1,0:T(8,128)} %wq.11, ...), custom_call_target="tpu_custom_call" | custom-call | flops 4194304 | bytes 6291456 | tf_op jit(solution)/shard_map/first/pallas_call | solution.py:340
  23.7 1.5 collective-permute-start.36
  25.8 1.5 collective-permute-done.36
  28.0 1.6 collective-permute-start.37
  31.4 2.4 %third.1 = (bf16[256,768]{1,0:T(8,128)(2,1)}, f32[1,768]{1,0:T(1,128)}, f32[1,1024]{1,0:T(1,128)}) custom-call(f32[2048,1024]{1,0:T(8,128)} %wq.11, f32[2048,1024]{1,0:T(8,128)} %sq.11, f32[1,1024]{1,0:T(1,128)} %sizes.1.refs_0_, f32[1,1024]{1,0:T(1,128)} %copy-done.26, f32[1,1024]{1,0:T(1,128)} %copy-done.25, f32[1,1024]{1,0:T(1,128)} %copy-done.27), custom_call_target="tpu_custom_call" | custom-call | flops 1572864 | bytes 1966080 | tf_op jit(solution)/shard_map/third/pallas_call | solution.py:389
  33.8 11.1 %fourth.1 = (f32[2048,1024]{1,0:T(8,128)}, bf16[512,768]{1,0:T(8,128)(2,1)}, bf16[512,768]{1,0:T(8,128)(2,1)}, bf16[256,768]{1,0:T(8,128)(2,1)}, bf16[128,768]{1...) custom-call(f32[2048,1024]{1,0:T(8,128)} %wq.11, f32[2048,1024]{1,0:T(8,128)} %sq.11, ...), custom_call_target="tpu_custom_call" | custom-call | flops 16777216 | bytes 29360128 | tf_op jit(solution)/shard_map/fourth/pallas_call | solution.py:407
  45.6 2.7 %collective-permute-start.38 = (bf16[4,4,256]{2,0,1:T(4,128)(2,1)S(1)}, bf16[4,4,256]{2,0,1:T(4,128)(2,1)S(1)}, u32[]{:S(2)}, u32[]{:S(2)}) collective-permute-start(bf16[4,4,256]{2,0,1:T(4,128)(2,1)S(1)} %pad_maximum_fusion.1), channel_id=1, source_target_pairs={{0,4},{1,5},{2,6},{3,7},{4,0},{5,1},{6,2},{7,3},{8,12},{9,13},{10,... | collective-permute-start | bytes 24584 | tf_op jit(solution)/shard_map/ppermute | solution.py:291
  48.3 0.8 multiply_bitcast_fusion
  49.1 1.2 collective-permute-done.38
  50.3 1.5 collective-permute-start.3
  52.4 3.2 %collective-permute-done.3.refs_0_ = bf16[64,768]{1,0:T(8,128)(2,1)S(1)} collective-permute-done((bf16[64,768]{1,0:T(8,128)(2,1)}, bf16[64,768]{1,0:T(8,128)(2,1)S(1)}, u32[]{:S(2)}, u32[]{:S(2)}) %collective-permute-start.3) | collective-permute-done | bytes 98336 | tf_op jit(solution)/shard_map/ppermute | solution.py:291
  55.7 1.3 collective-permute-start.46
  57.6 1.2 collective-permute-start.7
  58.8 0.9 collective-permute-start.40
  59.9 9.2 %collective-permute-done.7.refs_0_ = bf16[128,768]{1,0:T(8,128)(2,1)S(1)} collective-permute-done((bf16[128,768]{1,0:T(8,128)(2,1)}, bf16[128,768]{1,0:T(8,128)(2,1)S(1)}, u32[]{:S(2)}, u32[]{:S(2)}) %collective-permute-start.7) | collective-permute-done | bytes 196640 | tf_op jit(solution)/shard_map/ppermute | solution.py:291
  69.1 1.3 collective-permute-start.31
  72.3 2.4 %next.1.refs_2_ = bf16[256,768]{1,0:T(8,128)(2,1)} custom-call(f32[2048,1024]{1,0:T(8,128)} %wq.11, f32[2048,1024]{1,0:T(8,128)} %sq.11, f32[1,768]{1,0:T(1,128)} %get-tuple-element.33.inv), custom_call_target="tpu_custom_call" | custom-call | flops 1572864 | bytes 1966080 | tf_op jit(solution)/shard_map/next/pallas_call | solution.py:398
  74.7 0.7 collective-permute-done.40.refs_2_
  76.0 5.4 %collective-permute-done.31.refs_2_ = bf16[768,256]{1,0:T(8,128)(2,1)} collective-permute-done((bf16[768,256]{1,0:T(8,128)(2,1)}, bf16[768,256]{1,0:T(8,128)(2,1)}, u32[]{:S(2)}, u32[]{:S(2)}) %collective-permute-start.31) | collective-permute-done | bytes 393248 | tf_op jit(solution)/shard_map/ppermute | solution.py:291
  81.4 1.3 collective-permute-start.17
  83.4 1.3 collective-permute-start.34
  84.8 0.8 collective-permute-start.9
  85.5 8.1 %collective-permute-done.17.refs_2_ = bf16[256,768]{1,0:T(8,128)(2,1)S(1)} collective-permute-done((bf16[256,768]{1,0:T(8,128)(2,1)}, bf16[256,768]{1,0:T(8,128)(2,1)S(1)}, u32[]{:S(2)}, u32[]{:S(2)}) %collective-permute-start.17) | collective-permute-done | bytes 393248 | tf_op jit(solution)/shard_map/ppermute | solution.py:291
  93.6 8.5 %collective-permute-done.15.refs_0_ = bf16[256,768]{1,0:T(8,128)(2,1)} collective-permute-done((bf16[256,768]{1,0:T(8,128)(2,1)S(1)}, bf16[256,768]{1,0:T(8,128)(2,1)}, u32[]{:S(2)}, u32[]{:S(2)}) %collective-permute-start.15) | collective-permute-done | bytes 393248 | tf_op jit(solution)/shard_map/ppermute | solution.py:291
  102.1 19.6 %collective-permute-done.9.refs_0_ = bf16[256,768]{1,0:T(8,128)(2,1)} collective-permute-done((bf16[256,768]{1,0:T(8,128)(2,1)S(1)}, bf16[256,768]{1,0:T(8,128)(2,1)}, u32[]{:S(2)}, u32[]{:S(2)}) %collective-permute-start.9) | collective-permute-done | bytes 393248 | tf_op jit(solution)/shard_map/ppermute | solution.py:291
  121.8 1.3 collective-permute-start.13
  123.1 0.8 collective-permute-start.11
  124.5 17.7 %collective-permute-done.13.refs_0_ = bf16[512,768]{1,0:T(8,128)(2,1)S(1)} collective-permute-done((bf16[512,768]{1,0:T(8,128)(2,1)S(1)}, bf16[512,768]{1,0:T(8,128)(2,1)S(1)}, u32[]{:S(2)}, u32[]{:S(2)}) %collective-permute-start.13) | collective-permute-done | bytes 786464 | tf_op jit(solution)/shard_map/ppermute | solution.py:291
  142.2 12.7 %collective-permute-done.11.refs_0_ = bf16[512,768]{1,0:T(8,128)(2,1)} collective-permute-done((bf16[512,768]{1,0:T(8,128)(2,1)S(1)}, bf16[512,768]{1,0:T(8,128)(2,1)}, u32[]{:S(2)}, u32[]{:S(2)}) %collective-permute-start.11) | collective-permute-done | bytes 786464 | tf_op jit(solution)/shard_map/ppermute | solution.py:291
  155.6 0.8 copy-done.4
  156.5 0.8 copy-done.5
  157.2 0.8 collective-permute-done.18.refs_3_
  158.2 1.4 collective-permute-done.16.refs_1_
  161.0 3.1 %place_kv.1 = (bf16[64,8192]{1,0:T(8,128)(2,1)}, bf16[64,8192]{1,0:T(8,128)(2,1)}) custom-call(s32[1]{0:T(128)} %bitcast.me, f32[64,128]{1,0:T(8,128)} %get-tuple-element.46.inv, f32[64,1152]{1,0:T(8,128)} %get-tuple-element.47.refs_0_, f32[64,1152]{1,0:T(8,128)} %collective-permute-done.39.refs_1_, f32[64,1152]{1,0:T(8,128)} %collective-permute-done.40.refs_2_, ...), custom_call_target="tpu_custom_call" | custom-call | flops 8388608 | bytes 4194304 | tf_op jit(solution)/shard_map/place_kv/pallas_call | solution.py:464
  164.2 4.2 %shard_map.159.refs_16_ = bf16[8192,1024]{1,0:T(8,128)(2,1)} custom-call(s32[1]{0:T(128)} %bitcast.me, bf16[768,256]{1,0:T(8,128)(2,1)} %get-tuple-element.43.refs_0_, bf16[768,256]{1,0:T(8,128)(2,1)} %collective-permute-done.30.refs_1_, bf16[768,256]{1,0:T(8,128)(2,1)} %collective-permute-done.31.refs_2_, bf16[768,256]{1,0:T(8,128)(2,1)} %copy-done.17, ...), custom_call_target="tpu_custom_call" | custom-call | flops 16777216 | bytes 8388608 | tf_op jit(solution)/shard_map/pallas_call | solution.py:426
  168.4 5.5 %shard_map.160.refs_4_ = bf16[8192,1024]{1,0:T(8,128)(2,1)} custom-call(s32[1]{0:T(128)} %bitcast.me, bf16[256,768]{1,0:T(8,128)(2,1)} %get-tuple-element.40.refs_0_, bf16[256,768]{1,0:T(8,128)(2,1)} %copy-done.13, bf16[256,768]{1,0:T(8,128)(2,1)} %next.1.refs_2_, bf16[256,768]{1,0:T(8,128)(2,1)} %copy-done.12, ...), custom_call_target="tpu_custom_call", output_to_operand_aliasing={{}: (17, {})} | custom-call | flops 25165824 | bytes 12582912 | tf_op jit(solution)/shard_map/pallas_call | solution.py:426
  174.0 2.5 %shard_map.161.refs_2_ = bf16[8192,1024]{1,0:T(8,128)(2,1)} custom-call(s32[1]{0:T(128)} %bitcast.me, bf16[256,768]{1,0:T(8,128)(2,1)} %collective-permute-done.15.refs_0_, bf16[256,768]{1,0:T(8,128)(2,1)} %collective-permute-done.16.refs_1_, bf16[256,768]{1,0:T(8,128)(2,1)} %copy-done.14, ...), custom_call_target="tpu_custom_call", output_to_operand_aliasing={{}: (5, {})} | custom-call | flops 6291456 | bytes 3145728 | tf_op jit(solution)/shard_map/pallas_call | solution.py:426
  176.5 2.5 %shard_map.162.refs_2_ = bf16[8192,1024]{1,0:T(8,128)(2,1)} custom-call(s32[1]{0:T(128)} %bitcast.me, bf16[512,768]{1,0:T(8,128)(2,1)} %copy-done.3, bf16[512,768]{1,0:T(8,128)(2,1)} %collective-permute-done.14.refs_1_, bf16[8192,1024]{1,0:T(8,128)(2,1)} %shard_map.161.refs_2_), custom_call_target="tpu_custom_call", output_to_operand_aliasing={{}: (3, {})} | custom-call | flops 6291456 | bytes 3145728 | tf_op jit(solution)/shard_map/pallas_call | solution.py:426
  179.0 2.5 %shard_map.163.refs_2_ = bf16[8192,1024]{1,0:T(8,128)(2,1)} custom-call(s32[1]{0:T(128)} %bitcast.me, bf16[512,768]{1,0:T(8,128)(2,1)} %collective-permute-done.11.refs_0_, bf16[512,768]{1,0:T(8,128)(2,1)} %collective-permute-done.12.refs_1_, bf16[8192,1024]{1,0:T(8,128)(2,1)} %shard_map.162.refs_2_), custom_call_target="tpu_custom_call", output_to_operand_aliasing={{}: (3, {})} | custom-call | flops 6291456 | bytes 3145728 | tf_op jit(solution)/shard_map/pallas_call | solution.py:426
  181.6 0.8 copy-done.16
  182.4 2.0 %shard_map.164.refs_2_ = bf16[8192,1024]{1,0:T(8,128)(2,1)} custom-call(s32[1]{0:T(128)} %bitcast.me, bf16[256,768]{1,0:T(8,128)(2,1)} %collective-permute-done.9.refs_0_, bf16[256,768]{1,0:T(8,128)(2,1)} %copy-done.16, bf16[8192,1024]{1,0:T(8,128)(2,1)} %shard_map.163.refs_2_), custom_call_target="tpu_custom_call", output_to_operand_aliasing={{}: (3, {})} | custom-call | flops 3145728 | bytes 1572864 | tf_op jit(solution)/shard_map/pallas_call | solution.py:426
  184.4 0.8 shard_map.165.refs_4_
  185.2 0.8 shard_map.166
  (136 shorter events, 12.4 us)
Async XLA Ops:
  4.6 4.8 %collective-permute-start.28 = (f32[1,640]{1,0:T(1,128)}, f32[1,640]{1,0:T(1,128)S(1)}, u32[]{:S(2)}, u32[]{:S(2)}) collective-permute-start(f32[1,640]{1,0:T(1,128)} %get-tuple-element.42.refs_0_), channel_id=1, source_target_pairs={{0,16},{8,24},{16,0},{24,8},{1,17},{9,25},{17,1},{25,9},{2,18},{10... | collective-permute-start | bytes 7688 | tf_op jit(solution)/shard_map/ppermute | solution.py:291
  7.6 10.8 %collective-permute-start.27 = (f32[1,640]{1,0:T(1,128)}, f32[1,640]{1,0:T(1,128)S(1)}, u32[]{:S(2)}, u32[]{:S(2)}) collective-permute-start(f32[1,640]{1,0:T(1,128)} %get-tuple-element.42.refs_0_), channel_id=1, source_target_pairs={{0,8},{8,0},{16,24},{24,16},{1,9},{9,1},{17,25},{25,17},{2,10},{10... | collective-permute-start | bytes 7688 | tf_op jit(solution)/shard_map/ppermute | solution.py:291
  9.4 9.0 %collective-permute-start.29 = (f32[1,640]{1,0:T(1,128)S(1)}, f32[1,640]{1,0:T(1,128)S(1)}, u32[]{:S(2)}, u32[]{:S(2)}) collective-permute-start(f32[1,640]{1,0:T(1,128)S(1)} %collective-permute-done.28.refs_2_), channel_id=1, source_target_pairs={{0,8},{8,0},{16,24},{24,16},{1,9},{9,1},{17,25},{25,17},{2,10},{10... | collective-permute-start | bytes 7688 | tf_op jit(solution)/shard_map/ppermute | solution.py:291
  16.3 9.0 %collective-permute-start.1 = (f32[1,1024]{1,0:T(1,128)}, f32[1,1024]{1,0:T(1,128)S(1)}, u32[]{:S(2)}, u32[]{:S(2)}) collective-permute-start(f32[1,1024]{1,0:T(1,128)} %sizes.1.refs_0_), channel_id=1, source_target_pairs={{0,16},{8,24},{16,0},{24,8},{1,17},{9,25},{17,1},{25,9},{2,18},{10... | collective-permute-start | bytes 12296 | tf_op jit(solution)/shard_map/ppermute | solution.py:291
  23.7 3.6 %collective-permute-start.36 = (bf16[4,1,256]{2,0,1:T(4,128)(2,1)S(1)}, bf16[4,1,256]{2,0,1:T(4,128)(2,1)S(1)}, u32[]{:S(2)}, u32[]{:S(2)}) collective-permute-start(bf16[4,1,256]{2,0,1:T(4,128)(2,1)S(1)} %convert_bitcast_fusion), channel_id=1, source_target_pairs={{0,1},{1,0},{2,3},{3,2},{4,5},{5,4},{6,7},{7,6},{8,9},{9,8},{10,11... | collective-permute-start | bytes 6152 | tf_op jit(solution)/shard_map/ppermute | solution.py:291
  25.2 5.0 %collective-permute-start = (f32[1,1024]{1,0:T(1,128)S(1)}, f32[1,1024]{1,0:T(1,128)S(1)}, u32[]{:S(2)}, u32[]{:S(2)}) collective-permute-start(f32[1,1024]{1,0:T(1,128)S(1)} %copy-done.24), channel_id=1, source_target_pairs={{0,8},{8,0},{16,24},{24,16},{1,9},{9,1},{17,25},{25,17},{2,10},{10... | collective-permute-start | bytes 12296 | tf_op jit(solution)/shard_map/ppermute | solution.py:291
  25.3 4.9 %collective-permute-start.2 = (f32[1,1024]{1,0:T(1,128)S(1)}, f32[1,1024]{1,0:T(1,128)S(1)}, u32[]{:S(2)}, u32[]{:S(2)}) collective-permute-start(f32[1,1024]{1,0:T(1,128)S(1)} %collective-permute-done.1.refs_2_), channel_id=1, source_target_pairs={{0,8},{8,0},{16,24},{24,16},{1,9},{9,1},{17,25},{25,17},{2,10},{10... | collective-permute-start | bytes 12296 | tf_op jit(solution)/shard_map/ppermute | solution.py:291
  28.0 17.6 %collective-permute-start.37 = (bf16[4,2,256]{2,0,1:T(4,128)(2,1)S(1)}, bf16[4,2,256]{2,0,1:T(4,128)(2,1)S(1)}, u32[]{:S(2)}, u32[]{:S(2)}) collective-permute-start(bf16[4,2,256]{2,0,1:T(4,128)(2,1)S(1)} %pad_maximum_fusion.2), channel_id=1, source_target_pairs={{0,2},{1,3},{2,0},{3,1},{4,6},{5,7},{6,4},{7,5},{8,10},{9,11},{10,... | collective-permute-start | bytes 12296 | tf_op jit(solution)/shard_map/ppermute | solution.py:291
  29.7 29.1 %collective-permute-start.43 = (bf16[64,896]{1,0:T(8,128)(2,1)}, bf16[64,896]{1,0:T(8,128)(2,1)}, u32[]{:S(2)}, u32[]{:S(2)}) collective-permute-start(bf16[64,896]{1,0:T(8,128)(2,1)} %get-tuple-element.48.refs_4_), channel_id=1, source_target_pairs={{0,16},{8,24},{16,0},{24,8},{1,17},{9,25},{17,1},{25,9},{2,18},{10... | collective-permute-start | bytes 344072 | tf_op jit(solution)/shard_map/ppermute | solution.py:291
  30.2 28.6 %collective-permute-start.42 = (bf16[64,896]{1,0:T(8,128)(2,1)}, bf16[64,896]{1,0:T(8,128)(2,1)}, u32[]{:S(2)}, u32[]{:S(2)}) collective-permute-start(bf16[64,896]{1,0:T(8,128)(2,1)} %get-tuple-element.48.refs_4_), channel_id=1, source_target_pairs={{0,8},{8,0},{16,24},{24,16},{1,9},{9,1},{17,25},{25,17},{2,10},{10... | collective-permute-start | bytes 344072 | tf_op jit(solution)/shard_map/ppermute | solution.py:291
  45.0 6.8 %collective-permute-start.25 = (bf16[64,768]{1,0:T(8,128)(2,1)}, bf16[64,768]{1,0:T(8,128)(2,1)}, u32[]{:S(2)}, u32[]{:S(2)}) collective-permute-start(bf16[64,768]{1,0:T(8,128)(2,1)} %get-tuple-element.34.refs_12_), channel_id=1, source_target_pairs={{0,8},{8,0},{16,24},{24,16},{1,9},{9,1},{17,25},{25,17},{2,10},{10... | collective-permute-start | bytes 294920 | tf_op jit(solution)/shard_map/ppermute | solution.py:291
  45.5 6.8 %collective-permute-start.26 = (bf16[64,768]{1,0:T(8,128)(2,1)}, bf16[64,768]{1,0:T(8,128)(2,1)S(1)}, u32[]{:S(2)}, u32[]{:S(2)}) collective-permute-start(bf16[64,768]{1,0:T(8,128)(2,1)} %get-tuple-element.35.refs_14_), channel_id=1, source_target_pairs={{0,8},{8,0},{16,24},{24,16},{1,9},{9,1},{17,25},{25,17},{2,10},{10... | collective-permute-start | bytes 294920 | tf_op jit(solution)/shard_map/ppermute | solution.py:291
  45.6 4.6 %collective-permute-start.38 = (bf16[4,4,256]{2,0,1:T(4,128)(2,1)S(1)}, bf16[4,4,256]{2,0,1:T(4,128)(2,1)S(1)}, u32[]{:S(2)}, u32[]{:S(2)}) collective-permute-start(bf16[4,4,256]{2,0,1:T(4,128)(2,1)S(1)} %pad_maximum_fusion.1), channel_id=1, source_target_pairs={{0,4},{1,5},{2,6},{3,7},{4,0},{5,1},{6,2},{7,3},{8,12},{9,13},{10,... | collective-permute-start | bytes 24584 | tf_op jit(solution)/shard_map/ppermute | solution.py:291
  50.3 5.4 %collective-permute-start.3 = (bf16[64,768]{1,0:T(8,128)(2,1)}, bf16[64,768]{1,0:T(8,128)(2,1)S(1)}, u32[]{:S(2)}, u32[]{:S(2)}) collective-permute-start(bf16[64,768]{1,0:T(8,128)(2,1)} %get-tuple-element.34.refs_12_), channel_id=1, source_target_pairs={{0,16},{8,24},{16,0},{24,8},{1,17},{9,25},{17,1},{25,9},{2,18},{10... | collective-permute-start | bytes 294920 | tf_op jit(solution)/shard_map/ppermute | solution.py:291
  51.8 5.9 %collective-permute-start.5 = (bf16[64,768]{1,0:T(8,128)(2,1)}, bf16[64,768]{1,0:T(8,128)(2,1)S(1)}, u32[]{:S(2)}, u32[]{:S(2)}) collective-permute-start(bf16[64,768]{1,0:T(8,128)(2,1)} %get-tuple-element.35.refs_14_), channel_id=1, source_target_pairs={{0,16},{8,24},{16,0},{24,8},{1,17},{9,25},{17,1},{25,9},{2,18},{10... | collective-permute-start | bytes 294920 | tf_op jit(solution)/shard_map/ppermute | solution.py:291
  52.3 7.4 %collective-permute-start.24 = (bf16[128,768]{1,0:T(8,128)(2,1)}, bf16[128,768]{1,0:T(8,128)(2,1)S(1)}, u32[]{:S(2)}, u32[]{:S(2)}) collective-permute-start(bf16[128,768]{1,0:T(8,128)(2,1)} %get-tuple-element.36.refs_10_), channel_id=1, source_target_pairs={{0,8},{8,0},{16,24},{24,16},{1,9},{9,1},{17,25},{25,17},{2,10},{10... | collective-permute-start | bytes 589832 | tf_op jit(solution)/shard_map/ppermute | solution.py:291
  55.7 14.7 %collective-permute-start.46 = (bf16[64,2048]{1,0:T(8,128)(2,1)S(1)}, bf16[64,2048]{1,0:T(8,128)(2,1)S(1)}, u32[]{:S(2)}, u32[]{:S(2)}) collective-permute-start(bf16[64,2048]{1,0:T(8,128)(2,1)S(1)} %divide_convert_fusion.refs_8_), channel_id=1, source_target_pairs={{0,16},{8,24},{16,0},{24,8},{1,17},{9,25},{17,1},{25,9},{2,18},{10... | collective-permute-start | bytes 786440 | tf_op jit(solution)/shard_map/ppermute | solution.py:291
  57.6 11.4 %collective-permute-start.7 = (bf16[128,768]{1,0:T(8,128)(2,1)}, bf16[128,768]{1,0:T(8,128)(2,1)S(1)}, u32[]{:S(2)}, u32[]{:S(2)}) collective-permute-start(bf16[128,768]{1,0:T(8,128)(2,1)} %get-tuple-element.36.refs_10_), channel_id=1, source_target_pairs={{0,16},{8,24},{16,0},{24,8},{1,17},{9,25},{17,1},{25,9},{2,18},{10... | collective-permute-start | bytes 589832 | tf_op jit(solution)/shard_map/ppermute | solution.py:291
  58.8 12.1 %collective-permute-start.45 = (bf16[64,2048]{1,0:T(8,128)(2,1)S(1)}, bf16[64,2048]{1,0:T(8,128)(2,1)S(1)}, u32[]{:S(2)}, u32[]{:S(2)}) collective-permute-start(bf16[64,2048]{1,0:T(8,128)(2,1)S(1)} %divide_convert_fusion.refs_8_), channel_id=1, source_target_pairs={{0,8},{8,0},{16,24},{24,16},{1,9},{9,1},{17,25},{25,17},{2,10},{10... | collective-permute-start | bytes 786440 | tf_op jit(solution)/shard_map/ppermute | solution.py:291
  58.8 16.7 %collective-permute-start.40 = (f32[64,1152]{1,0:T(8,128)}, f32[64,1152]{1,0:T(8,128)}, u32[]{:S(2)}, u32[]{:S(2)}) collective-permute-start(f32[64,1152]{1,0:T(8,128)} %get-tuple-element.47.refs_0_), channel_id=1, source_target_pairs={{0,16},{8,24},{16,0},{24,8},{1,17},{9,25},{17,1},{25,9},{2,18},{10... | collective-permute-start | bytes 884744 | tf_op jit(solution)/shard_map/ppermute | solution.py:291
  59.7 10.7 %collective-permute-start.44 = (bf16[64,896]{1,0:T(8,128)(2,1)}, bf16[64,896]{1,0:T(8,128)(2,1)S(1)}, u32[]{:S(2)}, u32[]{:S(2)}) collective-permute-start(bf16[64,896]{1,0:T(8,128)(2,1)} %collective-permute-done.43.refs_6_), channel_id=1, source_target_pairs={{0,8},{8,0},{16,24},{24,16},{1,9},{9,1},{17,25},{25,17},{2,10},{10... | collective-permute-start | bytes 344072 | tf_op jit(solution)/shard_map/ppermute | solution.py:291
  69.1 12.3 %collective-permute-start.31 = (bf16[768,256]{1,0:T(8,128)(2,1)}, bf16[768,256]{1,0:T(8,128)(2,1)}, u32[]{:S(2)}, u32[]{:S(2)}) collective-permute-start(bf16[768,256]{1,0:T(8,128)(2,1)} %get-tuple-element.43.refs_0_), channel_id=1, source_target_pairs={{0,16},{8,24},{16,0},{24,8},{1,17},{9,25},{17,1},{25,9},{2,18},{10... | collective-permute-start | bytes 1179656 | tf_op jit(solution)/shard_map/ppermute | solution.py:291
  70.4 12.3 %collective-permute-start.30 = (bf16[768,256]{1,0:T(8,128)(2,1)}, bf16[768,256]{1,0:T(8,128)(2,1)}, u32[]{:S(2)}, u32[]{:S(2)}) collective-permute-start(bf16[768,256]{1,0:T(8,128)(2,1)} %get-tuple-element.43.refs_0_), channel_id=1, source_target_pairs={{0,8},{8,0},{16,24},{24,16},{1,9},{9,1},{17,25},{25,17},{2,10},{10... | collective-permute-start | bytes 1179656 | tf_op jit(solution)/shard_map/ppermute | solution.py:291
  70.4 13.0 %collective-permute-start.23 = (bf16[256,768]{1,0:T(8,128)(2,1)}, bf16[256,768]{1,0:T(8,128)(2,1)S(1)}, u32[]{:S(2)}, u32[]{:S(2)}) collective-permute-start(bf16[256,768]{1,0:T(8,128)(2,1)} %get-tuple-element.37.refs_8_), channel_id=1, source_target_pairs={{0,8},{8,0},{16,24},{24,16},{1,9},{9,1},{17,25},{25,17},{2,10},{10... | collective-permute-start | bytes 1179656 | tf_op jit(solution)/shard_map/ppermute | solution.py:291
  71.8 3.7 %collective-permute-start.39 = (f32[64,1152]{1,0:T(8,128)}, f32[64,1152]{1,0:T(8,128)}, u32[]{:S(2)}, u32[]{:S(2)}) collective-permute-start(f32[64,1152]{1,0:T(8,128)} %get-tuple-element.47.refs_0_), channel_id=1, source_target_pairs={{0,8},{8,0},{16,24},{24,16},{1,9},{9,1},{17,25},{25,17},{2,10},{10... | collective-permute-start | bytes 884744 | tf_op jit(solution)/shard_map/ppermute | solution.py:291
  75.5 9.3 %collective-permute-start.20 = (bf16[256,768]{1,0:T(8,128)(2,1)}, bf16[256,768]{1,0:T(8,128)(2,1)S(1)}, u32[]{:S(2)}, u32[]{:S(2)}) collective-permute-start(bf16[256,768]{1,0:T(8,128)(2,1)} %next.1.refs_2_), channel_id=1, source_target_pairs={{0,8},{8,0},{16,24},{24,16},{1,9},{9,1},{17,25},{25,17},{2,10},{10... | collective-permute-start | bytes 1179656 | tf_op jit(solution)/shard_map/ppermute | solution.py:291
  75.5 10.0 %collective-permute-start.19 = (bf16[256,768]{1,0:T(8,128)(2,1)S(1)}, bf16[256,768]{1,0:T(8,128)(2,1)S(1)}, u32[]{:S(2)}, u32[]{:S(2)}) collective-permute-start(bf16[256,768]{1,0:T(8,128)(2,1)S(1)} %copy-done.9), channel_id=1, source_target_pairs={{0,8},{8,0},{16,24},{24,16},{1,9},{9,1},{17,25},{25,17},{2,10},{10... | collective-permute-start | bytes 1179656 | tf_op jit(solution)/shard_map/ppermute | solution.py:291
  81.4 12.2 %collective-permute-start.17 = (bf16[256,768]{1,0:T(8,128)(2,1)}, bf16[256,768]{1,0:T(8,128)(2,1)S(1)}, u32[]{:S(2)}, u32[]{:S(2)}) collective-permute-start(bf16[256,768]{1,0:T(8,128)(2,1)} %next.1.refs_2_), channel_id=1, source_target_pairs={{0,16},{8,24},{16,0},{24,8},{1,17},{9,25},{17,1},{25,9},{2,18},{10... | collective-permute-start | bytes 1179656 | tf_op jit(solution)/shard_map/ppermute | solution.py:291
  82.7 19.4 %collective-permute-start.15 = (bf16[256,768]{1,0:T(8,128)(2,1)S(1)}, bf16[256,768]{1,0:T(8,128)(2,1)}, u32[]{:S(2)}, u32[]{:S(2)}) collective-permute-start(bf16[256,768]{1,0:T(8,128)(2,1)S(1)} %copy-done.9), channel_id=1, source_target_pairs={{0,16},{8,24},{16,0},{24,8},{1,17},{9,25},{17,1},{25,9},{2,18},{10... | collective-permute-start | bytes 1179656 | tf_op jit(solution)/shard_map/ppermute | solution.py:291
  83.4 40.5 %collective-permute-start.34 = (bf16[1280,256]{1,0:T(8,128)(2,1)}, bf16[1280,256]{1,0:T(8,128)(2,1)}, u32[]{:S(2)}, u32[]{:S(2)}) collective-permute-start(bf16[1280,256]{1,0:T(8,128)(2,1)} %get-tuple-element.44.refs_4_), channel_id=1, source_target_pairs={{0,16},{8,24},{16,0},{24,8},{1,17},{9,25},{17,1},{25,9},{2,18},{10... | collective-permute-start | bytes 1966088 | tf_op jit(solution)/shard_map/ppermute | solution.py:291
  84.8 37.0 %collective-permute-start.9 = (bf16[256,768]{1,0:T(8,128)(2,1)S(1)}, bf16[256,768]{1,0:T(8,128)(2,1)}, u32[]{:S(2)}, u32[]{:S(2)}) collective-permute-start(bf16[256,768]{1,0:T(8,128)(2,1)S(1)} %copy-done.10), channel_id=1, source_target_pairs={{0,16},{8,24},{16,0},{24,8},{1,17},{9,25},{17,1},{25,9},{2,18},{10... | collective-permute-start | bytes 1179656 | tf_op jit(solution)/shard_map/ppermute | solution.py:291
  85.5 38.4 %collective-permute-start.41 = (f32[64,1152]{1,0:T(8,128)}, f32[64,1152]{1,0:T(8,128)}, u32[]{:S(2)}, u32[]{:S(2)}) collective-permute-start(f32[64,1152]{1,0:T(8,128)} %collective-permute-done.40.refs_2_), channel_id=1, source_target_pairs={{0,8},{8,0},{16,24},{24,16},{1,9},{9,1},{17,25},{25,17},{2,10},{10... | collective-permute-start | bytes 884744 | tf_op jit(solution)/shard_map/ppermute | solution.py:291
  93.6 29.5 %collective-permute-start.47 = (bf16[64,2048]{1,0:T(8,128)(2,1)}, bf16[64,2048]{1,0:T(8,128)(2,1)S(1)}, u32[]{:S(2)}, u32[]{:S(2)}) collective-permute-start(bf16[64,2048]{1,0:T(8,128)(2,1)} %copy-done.18), channel_id=1, source_target_pairs={{0,8},{8,0},{16,24},{24,16},{1,9},{9,1},{17,25},{25,17},{2,10},{10... | collective-permute-start | bytes 786440 | tf_op jit(solution)/shard_map/ppermute | solution.py:291
  102.1 22.3 %collective-permute-start.33 = (bf16[1280,256]{1,0:T(8,128)(2,1)}, bf16[1280,256]{1,0:T(8,128)(2,1)S(1)}, u32[]{:S(2)}, u32[]{:S(2)}) collective-permute-start(bf16[1280,256]{1,0:T(8,128)(2,1)} %get-tuple-element.44.refs_4_), channel_id=1, source_target_pairs={{0,8},{8,0},{16,24},{24,16},{1,9},{9,1},{17,25},{25,17},{2,10},{10... | collective-permute-start | bytes 1966088 | tf_op jit(solution)/shard_map/ppermute | solution.py:291
  121.8 20.4 %collective-permute-start.13 = (bf16[512,768]{1,0:T(8,128)(2,1)S(1)}, bf16[512,768]{1,0:T(8,128)(2,1)S(1)}, u32[]{:S(2)}, u32[]{:S(2)}) collective-permute-start(bf16[512,768]{1,0:T(8,128)(2,1)S(1)} %copy-done.1), channel_id=1, source_target_pairs={{0,16},{8,24},{16,0},{24,8},{1,17},{9,25},{17,1},{25,9},{2,18},{10... | collective-permute-start | bytes 2359304 | tf_op jit(solution)/shard_map/ppermute | solution.py:291
  123.1 31.8 %collective-permute-start.11 = (bf16[512,768]{1,0:T(8,128)(2,1)S(1)}, bf16[512,768]{1,0:T(8,128)(2,1)}, u32[]{:S(2)}, u32[]{:S(2)}) collective-permute-start(bf16[512,768]{1,0:T(8,128)(2,1)S(1)} %copy-done.2), channel_id=1, source_target_pairs={{0,16},{8,24},{16,0},{24,8},{1,17},{9,25},{17,1},{25,9},{2,18},{10... | collective-permute-start | bytes 2359304 | tf_op jit(solution)/shard_map/ppermute | solution.py:291
  123.9 31.6 %collective-permute-start.21 = (bf16[512,768]{1,0:T(8,128)(2,1)S(1)}, bf16[512,768]{1,0:T(8,128)(2,1)S(1)}, u32[]{:S(2)}, u32[]{:S(2)}) collective-permute-start(bf16[512,768]{1,0:T(8,128)(2,1)S(1)} %copy-done.1), channel_id=1, source_target_pairs={{0,8},{8,0},{16,24},{24,16},{1,9},{9,1},{17,25},{25,17},{2,10},{10... | collective-permute-start | bytes 2359304 | tf_op jit(solution)/shard_map/ppermute | solution.py:291
  123.9 31.6 %collective-permute-start.22 = (bf16[512,768]{1,0:T(8,128)(2,1)S(1)}, bf16[512,768]{1,0:T(8,128)(2,1)S(1)}, u32[]{:S(2)}, u32[]{:S(2)}) collective-permute-start(bf16[512,768]{1,0:T(8,128)(2,1)S(1)} %copy-done.2), channel_id=1, source_target_pairs={{0,8},{8,0},{16,24},{24,16},{1,9},{9,1},{17,25},{25,17},{2,10},{10... | collective-permute-start | bytes 2359304 | tf_op jit(solution)/shard_map/ppermute | solution.py:291
  124.4 30.5 %collective-permute-start.32 = (bf16[768,256]{1,0:T(8,128)(2,1)}, bf16[768,256]{1,0:T(8,128)(2,1)S(1)}, u32[]{:S(2)}, u32[]{:S(2)}) collective-permute-start(bf16[768,256]{1,0:T(8,128)(2,1)} %collective-permute-done.31.refs_2_), channel_id=1, source_target_pairs={{0,8},{8,0},{16,24},{24,16},{1,9},{9,1},{17,25},{25,17},{2,10},{10... | collective-permute-start | bytes 1179656 | tf_op jit(solution)/shard_map/ppermute | solution.py:291
  142.2 18.0 %collective-permute-start.14 = (bf16[512,768]{1,0:T(8,128)(2,1)S(1)}, bf16[512,768]{1,0:T(8,128)(2,1)}, u32[]{:S(2)}, u32[]{:S(2)}) collective-permute-start(bf16[512,768]{1,0:T(8,128)(2,1)S(1)} %collective-permute-done.13.refs_0_), channel_id=1, source_target_pairs={{0,8},{8,0},{16,24},{24,16},{1,9},{9,1},{17,25},{25,17},{2,10},{10... | collective-permute-start | bytes 2359304 | tf_op jit(solution)/shard_map/ppermute | solution.py:291
  154.9 24.1 %collective-permute-start.12 = (bf16[512,768]{1,0:T(8,128)(2,1)}, bf16[512,768]{1,0:T(8,128)(2,1)}, u32[]{:S(2)}, u32[]{:S(2)}) collective-permute-start(bf16[512,768]{1,0:T(8,128)(2,1)} %collective-permute-done.11.refs_0_), channel_id=1, source_target_pairs={{0,8},{8,0},{16,24},{24,16},{1,9},{9,1},{17,25},{25,17},{2,10},{10... | collective-permute-start | bytes 2359304 | tf_op jit(solution)/shard_map/ppermute | solution.py:291
  155.0 3.0 %collective-permute-start.18 = (bf16[256,768]{1,0:T(8,128)(2,1)S(1)}, bf16[256,768]{1,0:T(8,128)(2,1)S(1)}, u32[]{:S(2)}, u32[]{:S(2)}) collective-permute-start(bf16[256,768]{1,0:T(8,128)(2,1)S(1)} %collective-permute-done.17.refs_2_), channel_id=1, source_target_pairs={{0,8},{8,0},{16,24},{24,16},{1,9},{9,1},{17,25},{25,17},{2,10},{10... | collective-permute-start | bytes 1179656 | tf_op jit(solution)/shard_map/ppermute | solution.py:291
  155.5 4.3 %collective-permute-start.35 = (bf16[1280,256]{1,0:T(8,128)(2,1)}, bf16[1280,256]{1,0:T(8,128)(2,1)S(1)}, u32[]{:S(2)}, u32[]{:S(2)}) collective-permute-start(bf16[1280,256]{1,0:T(8,128)(2,1)} %collective-permute-done.34.refs_6_), channel_id=1, source_target_pairs={{0,8},{8,0},{16,24},{24,16},{1,9},{9,1},{17,25},{25,17},{2,10},{10... | collective-permute-start | bytes 1966088 | tf_op jit(solution)/shard_map/ppermute | solution.py:291
  156.4 3.3 %collective-permute-start.16 = (bf16[256,768]{1,0:T(8,128)(2,1)}, bf16[256,768]{1,0:T(8,128)(2,1)}, u32[]{:S(2)}, u32[]{:S(2)}) collective-permute-start(bf16[256,768]{1,0:T(8,128)(2,1)} %collective-permute-done.15.refs_0_), channel_id=1, source_target_pairs={{0,8},{8,0},{16,24},{24,16},{1,9},{9,1},{17,25},{25,17},{2,10},{10... | collective-permute-start | bytes 1179656 | tf_op jit(solution)/shard_map/ppermute | solution.py:291
  158.0 23.6 %collective-permute-start.10 = (bf16[256,768]{1,0:T(8,128)(2,1)}, bf16[256,768]{1,0:T(8,128)(2,1)S(1)}, u32[]{:S(2)}, u32[]{:S(2)}) collective-permute-start(bf16[256,768]{1,0:T(8,128)(2,1)} %collective-permute-done.9.refs_0_), channel_id=1, source_target_pairs={{0,8},{8,0},{16,24},{24,16},{1,9},{9,1},{17,25},{25,17},{2,10},{10... | collective-permute-start | bytes 1179656 | tf_op jit(solution)/shard_map/ppermute | solution.py:291
  159.6 24.7 %collective-permute-start.8 = (bf16[128,768]{1,0:T(8,128)(2,1)S(1)}, bf16[128,768]{1,0:T(8,128)(2,1)S(1)}, u32[]{:S(2)}, u32[]{:S(2)}) collective-permute-start(bf16[128,768]{1,0:T(8,128)(2,1)S(1)} %collective-permute-done.7.refs_0_), channel_id=1, source_target_pairs={{0,8},{8,0},{16,24},{24,16},{1,9},{9,1},{17,25},{25,17},{2,10},{10... | collective-permute-start | bytes 589832 | tf_op jit(solution)/shard_map/ppermute | solution.py:291
  159.8 25.4 %collective-permute-start.4 = (bf16[64,768]{1,0:T(8,128)(2,1)S(1)}, bf16[64,768]{1,0:T(8,128)(2,1)S(1)}, u32[]{:S(2)}, u32[]{:S(2)}) collective-permute-start(bf16[64,768]{1,0:T(8,128)(2,1)S(1)} %collective-permute-done.3.refs_0_), channel_id=1, source_target_pairs={{0,8},{8,0},{16,24},{24,16},{1,9},{9,1},{17,25},{25,17},{2,10},{10... | collective-permute-start | bytes 294920 | tf_op jit(solution)/shard_map/ppermute | solution.py:291
  160.3 24.9 %collective-permute-start.6 = (bf16[64,768]{1,0:T(8,128)(2,1)S(1)}, bf16[64,768]{1,0:T(8,128)(2,1)S(1)}, u32[]{:S(2)}, u32[]{:S(2)}) collective-permute-start(bf16[64,768]{1,0:T(8,128)(2,1)S(1)} %collective-permute-done.5.refs_2_), channel_id=1, source_target_pairs={{0,8},{8,0},{16,24},{24,16},{1,9},{9,1},{17,25},{25,17},{2,10},{10... | collective-permute-start | bytes 294920 | tf_op jit(solution)/shard_map/ppermute | solution.py:291
  (31 other events, 712.8 us)

commit v3 on v2

--- a/solution.py
+++ b/solution.py
@@ -275,7 +275,14 @@
         copy.wait()
 
 
-CUTS = (4, 4, 8, 8, 4, 2, 1, 1)
+CHUNKS = 7
+
+
+def chunk_rows(rows):
+    part = rows // 8
+    return (part, part, 3 * part, 2 * part, part // 2, part // 2 - 16, 16)
+
+
 CUT_A = 6
 
 
@@ -290,10 +297,13 @@
     def swap(array, distance, axis="zero", size=n):
         return lax.ppermute(array, axis, [(i, i ^ distance) for i in range(size)])
 
-    def gather(piece):
+    def gather(piece, direct=False):
         found = [piece, swap(piece, 1)]
         for distance in range(2, n, 2):
             far = swap(piece, distance)
+            if direct:
+                found += [far, swap(piece, distance + 1)]
+                continue
             found += [far, swap(far, 1)]
         return found
 
@@ -379,13 +389,13 @@
     )(wq, sq)
     messages_q = gather(message_q)
 
-    unit = rows // sum(CUTS)
-    firsts = [sum(CUTS[:at]) for at in range(len(CUTS))]
+    sizes = chunk_rows(rows)
+    firsts = [sum(sizes[:at]) for at in range(CHUNKS)]
     rest = width - columns
     rows_of = lambda at: pl.BlockSpec(
-        (CUTS[at] * unit, width), lambda i: (firsts[at] // CUTS[at], 0)
+        (sizes[at], width), lambda i: (firsts[at] // sizes[at], 0)
     )
-    narrow = [shaped((c * unit, rest), bf16) for c in CUTS]
+    narrow = [shaped((c, rest), bf16) for c in sizes]
     own0, inv, factor_q = pl.pallas_call(
         functools.partial(third_kernel, columns, n * rows),
         grid=(1,),
@@ -405,17 +415,18 @@
         name="next",
     )(wq, sq, inv)
     rq, *owns = pl.pallas_call(
-        functools.partial(fourth_kernel, [c * unit for c in CUTS]),
+        functools.partial(fourth_kernel, sizes),
         out_shape=[shaped((rows, width), f32)] + narrow[2:],
         in_specs=[HBM] * 3,
-        out_specs=[HBM] * (len(CUTS) - 1),
+        out_specs=[HBM] * (CHUNKS - 1),
         scratch_shapes=[pltpu.VMEM((rows, width), f32)] * 2
         + [pltpu.VMEM((1, rest), f32), pltpu.VMEM((rows, rest), bf16)]
         + [pltpu.SemaphoreType.DMA((65,)), pltpu.SemaphoreType.DMA((64,))],
         cost_estimate=cost(rows * width * 8, rows * width * 14),
         name="fourth",
     )(wq, sq, inv)
-    found = [gather(piece) for piece in [own0, own1, *owns]]
+    found = [gather(piece) for piece in [own0, own1, *owns[:-1]]]
+    found.append(gather(owns[-1], direct=True))
 
     whole = shaped((n * rows, width), bf16)
     whole_kv = shaped((heads, n * rows), bf16)
@@ -443,7 +454,7 @@
 
     def jobs(chunks, distances):
         return [
-            (found[at][d], d, firsts[at] * unit, columns) for at in chunks for d in distances
+            (found[at][d], d, firsts[at], columns) for at in chunks for d in distances
         ]
 
     gains = norms.astype(jnp.bfloat16).reshape(n, 1, gain)
@@ -478,16 +489,15 @@
         name="place_kv",
     )(me, inv_k, *found_early, *found_k, *found_v)
     for name, chunks, distances in (
-        ("place_near", range(len(CUTS)), near),
+        ("place_near", range(CHUNKS), near),
         ("place1", (0, 1), far),
         ("place2", (2,), far),
         ("place3", (3,), far),
         ("place4", (4,), far),
-        ("place5", (5,), far),
-        ("place6", (6, 7), far),
+        ("place5", (5, 6), far),
     ):
         extra = (serve,) if name == "place1" else ()
-        spec = HBM if name in ("place5", "place6") else None
+        spec = HBM if name in ("place4", "place5") else None
         final_q = place(jobs(chunks, distances), final_q, extra, spec)
 
     return (

time: 186 us -> 185 us (level)
  waiting for transfers between devices: 92.6 us -> 89.5 us
  starting transfers between devices: 29.5 us -> 31.4 us
    ppermute x48 -> x45, waiting for transfers between devices: 92.6 us -> 89.5 us  [swap(): return lax.ppermute(array, axis, [(i, i ^ distance) for i in range(size)])]
    ppermute x48 -> x45, starting transfers between devices: 29.5 us -> 31.4 us  [swap(): return lax.ppermute(array, axis, [(i, i ^ distance) for i in range(size)])]
    pallas_call x8 -> x7, Pallas kernels: 20.9 us -> 19.4 us  [place(): pl.pallas_call(functools.partial(place_kernel, [job[1:] for job in jobs],...]
    unnamed x63 -> x59, local copies, waits for them, and re-layouts: 5.68 us -> 5.63 us
  transfers between devices with their start and end apart: 48 -> 45, of which waited for: 15 -> 15; matrix products, arithmetic and copies ran while one was open for 2% -> 2% of each run, Pallas kernels for 27% -> 26%
where the time goes in v3:
time: 185 us; the launch traced here: 184 us
  waiting for transfers between devices  89.5 us (48%)
  Pallas kernels  53.4 us (29%)
  starting transfers between devices  31.4 us (17%)
  local copies, waits for them, and re-layouts  5.63 us (3%)
  other arithmetic  2.99 us (2%)
    ppermute x45, waiting for transfers between devices, swap(): return lax.ppermute(array, axis, [(i, i ^ distance) for i in range(size)])  89.5 us
    ppermute x45, starting transfers between devices, swap(): return lax.ppermute(array, axis, [(i, i ^ distance) for i in range(size)])  31.4 us
    pallas_call x7, Pallas kernels, place(): pl.pallas_call(functools.partial(place_kernel, [job[1:] for job in jobs],...  19.4 us
    pallas_call x1, Pallas kernels, on_device(): pl.pallas_call(functools.partial(fourth_kernel, sizes), out_shape=[shaped...  11.1 us
    pallas_call x1, Pallas kernels, on_device(): pl.pallas_call(sizes_kernel, out_shape=shaped((1, width), f32), in_specs=...  6.87 us
    unnamed x59, local copies, waits for them, and re-layouts  5.63 us
    pallas_call x1, Pallas kernels, on_device(): pl.pallas_call(functools.partial(first_kernel, places, heads, gain, n * r...  4.07 us
    pallas_call x1, Pallas kernels, on_device(): pl.pallas_call(functools.partial(narrow_kernel, places), out_shape=(shape...  3.94 us
  transfers between devices with their start and end apart: 45, of which 15 were waited for; matrix products, arithmetic and copies ran while one was open for 2% of the time, Pallas kernels for 26%

profile of v3, /device:TPU:0, one launch (start us, length us, event | category | flops | bytes accessed | tf_op | source)
XLA Modules:
  0.0 184.0 jit_solution(15976858656878238488)
XLA Ops:
  0.6 3.9 %narrow.1 = (f32[64,2048]{1,0:T(8,128)}, f32[64,2048]{1,0:T(8,128)}, f32[64,1152]{1,0:T(8,128)}, f32[1,640]{1,0:T(1,128)}) custom-call(f32[2048,1024]{1,0:T(8,128)} %wq.11, f32[2048,1024]{1,0:T(8,128)} %sq.11, f32[64,2048]{1,0:T(8,128)} %bitcast.24, f32[64,2048]{1,0:T(8,128)} %bitcast.25, f32[64,2048]{1,0:T(8,128)} %bitcast.26, f32[64,2048]{1,0:T(8,128)} %bitcast.27, ...), custom_call_target="tpu_custom_call" | custom-call | flops 2097152 | bytes 4194304 | tf_op jit(solution)/shard_map/narrow/pallas_call | solution.py:319
  4.6 3.0 %collective-permute-start.25 = (f32[1,640]{1,0:T(1,128)}, f32[1,640]{1,0:T(1,128)S(1)}, u32[]{:S(2)}, u32[]{:S(2)}) collective-permute-start(f32[1,640]{1,0:T(1,128)} %get-tuple-element.40.refs_0_), channel_id=1, source_target_pairs={{0,16},{8,24},{16,0},{24,8},{1,17},{9,25},{17,1},{25,9},{2,18},{10... | collective-permute-start | bytes 7688 | tf_op jit(solution)/shard_map/ppermute | solution.py:298
  7.6 1.8 collective-permute-done.25.refs_2_
  9.4 6.9 %sizes.1.refs_0_ = f32[1,1024]{1,0:T(1,128)} custom-call(f32[2048,1024]{1,0:T(8,128)} %wq.11, f32[2048,1024]{1,0:T(8,128)} %sq.11), custom_call_target="tpu_custom_call" | custom-call | flops 16777216 | bytes 16777216 | tf_op jit(solution)/shard_map/sizes/pallas_call | solution.py:379
  16.3 2.1 %collective-permute-start.1 = (f32[1,1024]{1,0:T(1,128)}, f32[1,1024]{1,0:T(1,128)S(1)}, u32[]{:S(2)}, u32[]{:S(2)}) collective-permute-start(f32[1,1024]{1,0:T(1,128)} %sizes.1.refs_0_), channel_id=1, source_target_pairs={{0,16},{8,24},{16,0},{24,8},{1,17},{9,25},{17,1},{25,9},{2,18},{10... | collective-permute-start | bytes 12296 | tf_op jit(solution)/shard_map/ppermute | solution.py:298
  19.0 4.1 %first.1 = (bf16[64,896]{1,0:T(8,128)(2,1)}, bf16[768,256]{1,0:T(8,128)(2,1)}, bf16[1280,256]{1,0:T(8,128)(2,1)}, f32[64,128]{1,0:T(8,128)}, f32[1,64]{1,0:T(1,128)}, /*index=5*/f32[1,64]{1,0:T(1,128)}, f32[4,256]{1,0:T(4,128)}) custom-call(s32[1]{0:T(128)} %bitcast.me, f32[64,2048]{1,0:T(8,128)} %get-tuple-element.39.rk, f32[2048,1024]{1,0:T(8,128)} %wq.11, ...), custom_call_target="tpu_custom_call" | custom-call | flops 4194304 | bytes 6291456 | tf_op jit(solution)/shard_map/first/pallas_call | solution.py:350
  23.7 1.5 collective-permute-start.33
  25.8 1.5 collective-permute-done.33
  27.3 0.7 broadcast_select_fusion.5
  28.0 1.6 collective-permute-start.34
  31.4 2.4 %third.1 = (bf16[256,768]{1,0:T(8,128)(2,1)}, f32[1,768]{1,0:T(1,128)}, f32[1,1024]{1,0:T(1,128)}) custom-call(f32[2048,1024]{1,0:T(8,128)} %wq.11, f32[2048,1024]{1,0:T(8,128)} %sq.11, f32[1,1024]{1,0:T(1,128)} %sizes.1.refs_0_, f32[1,1024]{1,0:T(1,128)} %copy-done.24, f32[1,1024]{1,0:T(1,128)} %copy-done.23, f32[1,1024]{1,0:T(1,128)} %copy-done.25), custom_call_target="tpu_custom_call" | custom-call | flops 1572864 | bytes 1966080 | tf_op jit(solution)/shard_map/third/pallas_call | solution.py:399
  33.9 11.1 %fourth.1 = (f32[2048,1024]{1,0:T(8,128)}, bf16[768,768]{1,0:T(8,128)(2,1)}, bf16[512,768]{1,0:T(8,128)(2,1)}, bf16[128,768]{1,0:T(8,128)(2,1)}, bf16[112,768]{1,0:T(8,128)(2,1)}, /*index=5*/bf16[16,768]{1,0:T(8,128)(2,1)}) custom-call(f32[2048,1024]{1,0:T(8,128)} %wq.11, f32[2048,1024]{1,0:T(8,128)} %sq.11, f32[1,768]{1,0:T(1,128)} %get-tuple-element.32.inv), custom_call_target="tpu_custom_call" | custom-call | flops 16777216 | bytes 29360128 | tf_op jit(solution)/shard_map/fourth/pallas_call | solution.py:417
  45.6 2.7 %collective-permute-start.35 = (bf16[4,4,256]{2,0,1:T(4,128)(2,1)S(1)}, bf16[4,4,256]{2,0,1:T(4,128)(2,1)}, u32[]{:S(2)}, u32[]{:S(2)}) collective-permute-start(bf16[4,4,256]{2,0,1:T(4,128)(2,1)S(1)} %pad_maximum_fusion.1), channel_id=1, source_target_pairs={{0,4},{1,5},{2,6},{3,7},{4,0},{5,1},{6,2},{7,3},{8,12},{9,13},{10,... | collective-permute-start | bytes 24584 | tf_op jit(solution)/shard_map/ppermute | solution.py:298
  48.2 0.7 multiply_bitcast_fusion
  49.0 1.3 collective-permute-done.35
  50.3 1.5 collective-permute-start.7
  53.1 1.6 collective-permute-start.43
  55.2 6.3 %collective-permute-done.3.refs_0_ = bf16[112,768]{1,0:T(8,128)(2,1)S(1)} collective-permute-done((bf16[112,768]{1,0:T(8,128)(2,1)}, bf16[112,768]{1,0:T(8,128)(2,1)S(1)}, u32[]{:S(2)}, u32[]{:S(2)}) %collective-permute-start.3) | collective-permute-done | bytes 172064 | tf_op jit(solution)/shard_map/ppermute | solution.py:298
  62.2 1.4 collective-permute-done.41.refs_7_
  63.6 1.9 %collective-permute-start.28 = (bf16[768,256]{1,0:T(8,128)(2,1)}, bf16[768,256]{1,0:T(8,128)(2,1)}, u32[]{:S(2)}, u32[]{:S(2)}) collective-permute-start(bf16[768,256]{1,0:T(8,128)(2,1)} %get-tuple-element.41.refs_0_), channel_id=1, source_target_pairs={{0,16},{8,24},{16,0},{24,8},{1,17},{9,25},{17,1},{25,9},{2,18},{10... | collective-permute-start | bytes 1179656 | tf_op jit(solution)/shard_map/ppermute | solution.py:298
  65.6 1.6 collective-permute-done.43.refs_10_
  67.1 2.5 %next.1.refs_2_ = bf16[256,768]{1,0:T(8,128)(2,1)} custom-call(f32[2048,1024]{1,0:T(8,128)} %wq.11, f32[2048,1024]{1,0:T(8,128)} %sq.11, f32[1,768]{1,0:T(1,128)} %get-tuple-element.32.inv), custom_call_target="tpu_custom_call" | custom-call | flops 1572864 | bytes 1966080 | tf_op jit(solution)/shard_map/next/pallas_call | solution.py:408
  70.2 3.4 %collective-permute-done.37.refs_2_ = f32[64,1152]{1,0:T(8,128)} collective-permute-done((f32[64,1152]{1,0:T(8,128)S(1)}, f32[64,1152]{1,0:T(8,128)}, u32[]{:S(2)}, u32[]{:S(2)}) %collective-permute-start.37) | collective-permute-done | bytes 294944 | tf_op jit(solution)/shard_map/ppermute | solution.py:298
  73.6 0.7 copy-done.11
  74.3 1.9 %collective-permute-start.11 = (bf16[768,768]{1,0:T(8,128)(2,1)}, bf16[768,768]{1,0:T(8,128)(2,1)S(1)}, u32[]{:S(2)}, u32[]{:S(2)}) collective-permute-start(bf16[768,768]{1,0:T(8,128)(2,1)} %get-tuple-element.37.refs_4_), channel_id=1, source_target_pairs={{0,16},{8,24},{16,0},{24,8},{1,17},{9,25},{17,1},{25,9},{2,18},{10... | collective-permute-start | bytes 3538952 | tf_op jit(solution)/shard_map/ppermute | solution.py:298
  76.2 5.8 %collective-permute-done.28.refs_2_ = bf16[768,256]{1,0:T(8,128)(2,1)} collective-permute-done((bf16[768,256]{1,0:T(8,128)(2,1)}, bf16[768,256]{1,0:T(8,128)(2,1)}, u32[]{:S(2)}, u32[]{:S(2)}) %collective-permute-start.28) | collective-permute-done | bytes 393248 | tf_op jit(solution)/shard_map/ppermute | solution.py:298
  82.0 1.9 %collective-permute-start.15 = (bf16[256,768]{1,0:T(8,128)(2,1)}, bf16[256,768]{1,0:T(8,128)(2,1)S(1)}, u32[]{:S(2)}, u32[]{:S(2)}) collective-permute-start(bf16[256,768]{1,0:T(8,128)(2,1)} %next.1.refs_2_), channel_id=1, source_target_pairs={{0,16},{8,24},{16,0},{24,8},{1,17},{9,25},{17,1},{25,9},{2,18},{10... | collective-permute-start | bytes 1179656 | tf_op jit(solution)/shard_map/ppermute | solution.py:298
  84.0 2.0 %collective-permute-start.31 = (bf16[1280,256]{1,0:T(8,128)(2,1)S(1)}, bf16[1280,256]{1,0:T(8,128)(2,1)}, u32[]{:S(2)}, u32[]{:S(2)}) collective-permute-start(bf16[1280,256]{1,0:T(8,128)(2,1)S(1)} %copy-done.3), channel_id=1, source_target_pairs={{0,16},{8,24},{16,0},{24,8},{1,17},{9,25},{17,1},{25,9},{2,18},{10... | collective-permute-start | bytes 1966088 | tf_op jit(solution)/shard_map/ppermute | solution.py:298
  86.0 29.6 %collective-permute-done.15.refs_2_ = bf16[256,768]{1,0:T(8,128)(2,1)S(1)} collective-permute-done((bf16[256,768]{1,0:T(8,128)(2,1)}, bf16[256,768]{1,0:T(8,128)(2,1)S(1)}, u32[]{:S(2)}, u32[]{:S(2)}) %collective-permute-start.15) | collective-permute-done | bytes 393248 | tf_op jit(solution)/shard_map/ppermute | solution.py:298
  115.6 8.5 %collective-permute-done.13.refs_0_ = bf16[256,768]{1,0:T(8,128)(2,1)} collective-permute-done((bf16[256,768]{1,0:T(8,128)(2,1)}, bf16[256,768]{1,0:T(8,128)(2,1)}, u32[]{:S(2)}, u32[]{:S(2)}) %collective-permute-start.13) | collective-permute-done | bytes 393248 | tf_op jit(solution)/shard_map/ppermute | solution.py:298
  124.1 1.7 collective-permute-done.44.refs_11_
  125.9 1.9 %collective-permute-start.9 = (bf16[512,768]{1,0:T(8,128)(2,1)}, bf16[512,768]{1,0:T(8,128)(2,1)}, u32[]{:S(2)}, u32[]{:S(2)}) collective-permute-start(bf16[512,768]{1,0:T(8,128)(2,1)} %get-tuple-element.36.refs_6_), channel_id=1, source_target_pairs={{0,16},{8,24},{16,0},{24,8},{1,17},{9,25},{17,1},{25,9},{2,18},{10... | collective-permute-start | bytes 2359304 | tf_op jit(solution)/shard_map/ppermute | solution.py:298
  127.8 0.7 copy-done.12
  128.5 9.6 %collective-permute-done.31.refs_6_ = bf16[1280,256]{1,0:T(8,128)(2,1)} collective-permute-done((bf16[1280,256]{1,0:T(8,128)(2,1)S(1)}, bf16[1280,256]{1,0:T(8,128)(2,1)}, u32[]{:S(2)}, u32[]{:S(2)}) %collective-permute-start.31) | collective-permute-done | bytes 655392 | tf_op jit(solution)/shard_map/ppermute | solution.py:298
  140.2 13.4 %collective-permute-done.9.refs_0_ = bf16[512,768]{1,0:T(8,128)(2,1)} collective-permute-done((bf16[512,768]{1,0:T(8,128)(2,1)}, bf16[512,768]{1,0:T(8,128)(2,1)}, u32[]{:S(2)}, u32[]{:S(2)}) %collective-permute-start.9) | collective-permute-done | bytes 786464 | tf_op jit(solution)/shard_map/ppermute | solution.py:298
  154.2 0.7 copy-done.8
  155.0 2.9 %collective-permute-done.14.refs_1_ = bf16[256,768]{1,0:T(8,128)(2,1)} collective-permute-done((bf16[256,768]{1,0:T(8,128)(2,1)}, bf16[256,768]{1,0:T(8,128)(2,1)}, u32[]{:S(2)}, u32[]{:S(2)}) %collective-permute-start.14) | collective-permute-done | bytes 393248 | tf_op jit(solution)/shard_map/ppermute | solution.py:298
  158.3 0.7 broadcast_select_fusion.1
  159.1 1.6 collective-permute-start.5
  160.7 0.7 copy.25
  161.4 3.1 %place_kv.1 = (bf16[64,8192]{1,0:T(8,128)(2,1)}, bf16[64,8192]{1,0:T(8,128)(2,1)}) custom-call(s32[1]{0:T(128)} %bitcast.me, f32[64,128]{1,0:T(8,128)} %get-tuple-element.44.inv, f32[64,1152]{1,0:T(8,128)} %get-tuple-element.45.refs_0_, f32[64,1152]{1,0:T(8,128)} %copy-done.11, f32[64,1152]{1,0:T(8,128)} %collective-permute-done.37.refs_2_, ...), custom_call_target="tpu_custom_call" | custom-call | flops 8388608 | bytes 4194304 | tf_op jit(solution)/shard_map/place_kv/pallas_call | solution.py:475
  164.5 4.2 %shard_map.159.refs_14_ = bf16[8192,1024]{1,0:T(8,128)(2,1)} custom-call(s32[1]{0:T(128)} %bitcast.me, bf16[768,256]{1,0:T(8,128)(2,1)} %get-tuple-element.41.refs_0_, bf16[768,256]{1,0:T(8,128)(2,1)} %collective-permute-done.27.refs_1_, bf16[768,256]{1,0:T(8,128)(2,1)} %collective-permute-done.28.refs_2_, bf16[768,256]{1,0:T(8,128)(2,1)} %copy-done.9, ...), custom_call_target="tpu_custom_call" | custom-call | flops 16777216 | bytes 8388608 | tf_op jit(solution)/shard_map/pallas_call | solution.py:437
  168.7 5.5 %shard_map.160.refs_4_ = bf16[8192,1024]{1,0:T(8,128)(2,1)} custom-call(s32[1]{0:T(128)} %bitcast.me, bf16[256,768]{1,0:T(8,128)(2,1)} %get-tuple-element.38.refs_0_, bf16[256,768]{1,0:T(8,128)(2,1)} %collective-permute-done.17.refs_1_, bf16[256,768]{1,0:T(8,128)(2,1)} %next.1.refs_2_, bf16[256,768]{1,0:T(8,128)(2,1)} %copy-done.6, ...), custom_call_target="tpu_custom_call", output_to_operand_aliasing={{}: (15, {})} | custom-call | flops 25165824 | bytes 12582912 | tf_op jit(solution)/shard_map/pallas_call | solution.py:437
  174.3 2.5 %shard_map.161.refs_2_ = bf16[8192,1024]{1,0:T(8,128)(2,1)} custom-call(s32[1]{0:T(128)} %bitcast.me, bf16[256,768]{1,0:T(8,128)(2,1)} %collective-permute-done.13.refs_0_, bf16[256,768]{1,0:T(8,128)(2,1)} %collective-permute-done.14.refs_1_, bf16[256,768]{1,0:T(8,128)(2,1)} %copy-done.7, ...), custom_call_target="tpu_custom_call", output_to_operand_aliasing={{}: (5, {})} | custom-call | flops 6291456 | bytes 3145728 | tf_op jit(solution)/shard_map/pallas_call | solution.py:437
  176.8 3.0 %shard_map.162.refs_2_ = bf16[8192,1024]{1,0:T(8,128)(2,1)} custom-call(s32[1]{0:T(128)} %bitcast.me, bf16[768,768]{1,0:T(8,128)(2,1)} %copy-done, bf16[768,768]{1,0:T(8,128)(2,1)} %copy-done.1, bf16[8192,1024]{1,0:T(8,128)(2,1)} %shard_map.161.refs_2_), custom_call_target="tpu_custom_call", output_to_operand_aliasing={{}: (3, {})} | custom-call | flops 9437184 | bytes 4718592 | tf_op jit(solution)/shard_map/pallas_call | solution.py:437
  179.9 2.5 %shard_map.163.refs_2_ = bf16[8192,1024]{1,0:T(8,128)(2,1)} custom-call(s32[1]{0:T(128)} %bitcast.me, bf16[512,768]{1,0:T(8,128)(2,1)} %collective-permute-done.9.refs_0_, bf16[512,768]{1,0:T(8,128)(2,1)} %collective-permute-done.10.refs_1_, bf16[8192,1024]{1,0:T(8,128)(2,1)} %shard_map.162.refs_2_), custom_call_target="tpu_custom_call", output_to_operand_aliasing={{}: (3, {})} | custom-call | flops 6291456 | bytes 3145728 | tf_op jit(solution)/shard_map/pallas_call | solution.py:437
  182.4 0.8 shard_map.164.refs_4_
  183.2 0.8 shard_map.165
  (125 shorter events, 10.4 us)
Async XLA Ops:
  4.6 4.8 %collective-permute-start.25 = (f32[1,640]{1,0:T(1,128)}, f32[1,640]{1,0:T(1,128)S(1)}, u32[]{:S(2)}, u32[]{:S(2)}) collective-permute-start(f32[1,640]{1,0:T(1,128)} %get-tuple-element.40.refs_0_), channel_id=1, source_target_pairs={{0,16},{8,24},{16,0},{24,8},{1,17},{9,25},{17,1},{25,9},{2,18},{10... | collective-permute-start | bytes 7688 | tf_op jit(solution)/shard_map/ppermute | solution.py:298
  7.6 10.8 %collective-permute-start.24 = (f32[1,640]{1,0:T(1,128)}, f32[1,640]{1,0:T(1,128)S(1)}, u32[]{:S(2)}, u32[]{:S(2)}) collective-permute-start(f32[1,640]{1,0:T(1,128)} %get-tuple-element.40.refs_0_), channel_id=1, source_target_pairs={{0,8},{8,0},{16,24},{24,16},{1,9},{9,1},{17,25},{25,17},{2,10},{10... | collective-permute-start | bytes 7688 | tf_op jit(solution)/shard_map/ppermute | solution.py:298
  9.4 9.0 %collective-permute-start.26 = (f32[1,640]{1,0:T(1,128)S(1)}, f32[1,640]{1,0:T(1,128)S(1)}, u32[]{:S(2)}, u32[]{:S(2)}) collective-permute-start(f32[1,640]{1,0:T(1,128)S(1)} %collective-permute-done.25.refs_2_), channel_id=1, source_target_pairs={{0,8},{8,0},{16,24},{24,16},{1,9},{9,1},{17,25},{25,17},{2,10},{10... | collective-permute-start | bytes 7688 | tf_op jit(solution)/shard_map/ppermute | solution.py:298
  16.3 9.0 %collective-permute-start.1 = (f32[1,1024]{1,0:T(1,128)}, f32[1,1024]{1,0:T(1,128)S(1)}, u32[]{:S(2)}, u32[]{:S(2)}) collective-permute-start(f32[1,1024]{1,0:T(1,128)} %sizes.1.refs_0_), channel_id=1, source_target_pairs={{0,16},{8,24},{16,0},{24,8},{1,17},{9,25},{17,1},{25,9},{2,18},{10... | collective-permute-start | bytes 12296 | tf_op jit(solution)/shard_map/ppermute | solution.py:298
  23.7 3.6 %collective-permute-start.33 = (bf16[4,1,256]{2,0,1:T(4,128)(2,1)S(1)}, bf16[4,1,256]{2,0,1:T(4,128)(2,1)S(1)}, u32[]{:S(2)}, u32[]{:S(2)}) collective-permute-start(bf16[4,1,256]{2,0,1:T(4,128)(2,1)S(1)} %convert_bitcast_fusion), channel_id=1, source_target_pairs={{0,1},{1,0},{2,3},{3,2},{4,5},{5,4},{6,7},{7,6},{8,9},{9,8},{10,11... | collective-permute-start | bytes 6152 | tf_op jit(solution)/shard_map/ppermute | solution.py:298
  25.3 5.0 %collective-permute-start = (f32[1,1024]{1,0:T(1,128)S(1)}, f32[1,1024]{1,0:T(1,128)S(1)}, u32[]{:S(2)}, u32[]{:S(2)}) collective-permute-start(f32[1,1024]{1,0:T(1,128)S(1)} %copy-done.22), channel_id=1, source_target_pairs={{0,8},{8,0},{16,24},{24,16},{1,9},{9,1},{17,25},{25,17},{2,10},{10... | collective-permute-start | bytes 12296 | tf_op jit(solution)/shard_map/ppermute | solution.py:298
  25.3 4.9 %collective-permute-start.2 = (f32[1,1024]{1,0:T(1,128)S(1)}, f32[1,1024]{1,0:T(1,128)S(1)}, u32[]{:S(2)}, u32[]{:S(2)}) collective-permute-start(f32[1,1024]{1,0:T(1,128)S(1)} %collective-permute-done.1.refs_2_), channel_id=1, source_target_pairs={{0,8},{8,0},{16,24},{24,16},{1,9},{9,1},{17,25},{25,17},{2,10},{10... | collective-permute-start | bytes 12296 | tf_op jit(solution)/shard_map/ppermute | solution.py:298
  28.0 17.5 %collective-permute-start.34 = (bf16[4,2,256]{2,0,1:T(4,128)(2,1)S(1)}, bf16[4,2,256]{2,0,1:T(4,128)(2,1)S(1)}, u32[]{:S(2)}, u32[]{:S(2)}) collective-permute-start(bf16[4,2,256]{2,0,1:T(4,128)(2,1)S(1)} %pad_maximum_fusion.2), channel_id=1, source_target_pairs={{0,2},{1,3},{2,0},{3,1},{4,6},{5,7},{6,4},{7,5},{8,10},{9,11},{10,... | collective-permute-start | bytes 12296 | tf_op jit(solution)/shard_map/ppermute | solution.py:298
  29.7 22.7 %collective-permute-start.40 = (bf16[64,896]{1,0:T(8,128)(2,1)}, bf16[64,896]{1,0:T(8,128)(2,1)S(1)}, u32[]{:S(2)}, u32[]{:S(2)}) collective-permute-start(bf16[64,896]{1,0:T(8,128)(2,1)} %get-tuple-element.46.refs_4_), channel_id=1, source_target_pairs={{0,16},{8,24},{16,0},{24,8},{1,17},{9,25},{17,1},{25,9},{2,18},{10... | collective-permute-start | bytes 344072 | tf_op jit(solution)/shard_map/ppermute | solution.py:298
  30.2 22.8 %collective-permute-start.39 = (bf16[64,896]{1,0:T(8,128)(2,1)}, bf16[64,896]{1,0:T(8,128)(2,1)S(1)}, u32[]{:S(2)}, u32[]{:S(2)}) collective-permute-start(bf16[64,896]{1,0:T(8,128)(2,1)} %get-tuple-element.46.refs_4_), channel_id=1, source_target_pairs={{0,8},{8,0},{16,24},{24,16},{1,9},{9,1},{17,25},{25,17},{2,10},{10... | collective-permute-start | bytes 344072 | tf_op jit(solution)/shard_map/ppermute | solution.py:298
  44.9 114.1 %copy-start.20 = (bf16[16,768]{1,0:T(8,128)(2,1)S(1)}, bf16[16,768]{1,0:T(8,128)(2,1)}, u32[]{:S(2)}) copy-start(bf16[16,768]{1,0:T(8,128)(2,1)} %get-tuple-element.34.refs_12_) | copy-start | bytes 73732
  45.0 6.8 %collective-permute-start.23 = (bf16[16,768]{1,0:T(8,128)(2,1)}, bf16[16,768]{1,0:T(8,128)(2,1)S(1)}, u32[]{:S(2)}, u32[]{:S(2)}) collective-permute-start(bf16[16,768]{1,0:T(8,128)(2,1)} %get-tuple-element.34.refs_12_), channel_id=1, source_target_pairs={{0,8},{8,0},{16,24},{24,16},{1,9},{9,1},{17,25},{25,17},{2,10},{10... | collective-permute-start | bytes 73736 | tf_op jit(solution)/shard_map/ppermute | solution.py:298
  45.6 4.7 %collective-permute-start.35 = (bf16[4,4,256]{2,0,1:T(4,128)(2,1)S(1)}, bf16[4,4,256]{2,0,1:T(4,128)(2,1)}, u32[]{:S(2)}, u32[]{:S(2)}) collective-permute-start(bf16[4,4,256]{2,0,1:T(4,128)(2,1)S(1)} %pad_maximum_fusion.1), channel_id=1, source_target_pairs={{0,4},{1,5},{2,6},{3,7},{4,0},{5,1},{6,2},{7,3},{8,12},{9,13},{10,... | collective-permute-start | bytes 24584 | tf_op jit(solution)/shard_map/ppermute | solution.py:298
  49.0 12.6 %collective-permute-start.21 = (bf16[128,768]{1,0:T(8,128)(2,1)}, bf16[128,768]{1,0:T(8,128)(2,1)S(1)}, u32[]{:S(2)}, u32[]{:S(2)}) collective-permute-start(bf16[128,768]{1,0:T(8,128)(2,1)} %get-tuple-element.35.refs_8_), channel_id=1, source_target_pairs={{0,8},{8,0},{16,24},{24,16},{1,9},{9,1},{17,25},{25,17},{2,10},{10... | collective-permute-start | bytes 589832 | tf_op jit(solution)/shard_map/ppermute | solution.py:298
  50.3 11.8 %collective-permute-start.7 = (bf16[128,768]{1,0:T(8,128)(2,1)}, bf16[128,768]{1,0:T(8,128)(2,1)S(1)}, u32[]{:S(2)}, u32[]{:S(2)}) collective-permute-start(bf16[128,768]{1,0:T(8,128)(2,1)} %get-tuple-element.35.refs_8_), channel_id=1, source_target_pairs={{0,16},{8,24},{16,0},{24,8},{1,17},{9,25},{17,1},{25,9},{2,18},{10... | collective-permute-start | bytes 589832 | tf_op jit(solution)/shard_map/ppermute | solution.py:298
  51.8 2.8 %collective-permute-start.22 = (bf16[112,768]{1,0:T(8,128)(2,1)}, bf16[112,768]{1,0:T(8,128)(2,1)S(1)}, u32[]{:S(2)}, u32[]{:S(2)}) collective-permute-start(bf16[112,768]{1,0:T(8,128)(2,1)} %get-tuple-element.33.refs_10_), channel_id=1, source_target_pairs={{0,8},{8,0},{16,24},{24,16},{1,9},{9,1},{17,25},{25,17},{2,10},{10... | collective-permute-start | bytes 516104 | tf_op jit(solution)/shard_map/ppermute | solution.py:298
  52.4 109.0 %copy-start.17 = (bf16[64,896]{1,0:T(8,128)(2,1)}, bf16[64,896]{1,0:T(8,128)(2,1)S(1)}, u32[]{:S(2)}) copy-start(bf16[64,896]{1,0:T(8,128)(2,1)S(1)} %collective-permute-done.40.refs_6_) | copy-start | bytes 344068
  52.4 9.1 %collective-permute-start.3 = (bf16[112,768]{1,0:T(8,128)(2,1)}, bf16[112,768]{1,0:T(8,128)(2,1)S(1)}, u32[]{:S(2)}, u32[]{:S(2)}) collective-permute-start(bf16[112,768]{1,0:T(8,128)(2,1)} %get-tuple-element.33.refs_10_), channel_id=1, source_target_pairs={{0,16},{8,24},{16,0},{24,8},{1,17},{9,25},{17,1},{25,9},{2,18},{10... | collective-permute-start | bytes 516104 | tf_op jit(solution)/shard_map/ppermute | solution.py:298
  53.0 108.4 %copy-start.2 = (bf16[64,2048]{1,0:T(8,128)(2,1)}, bf16[64,2048]{1,0:T(8,128)(2,1)S(1)}, u32[]{:S(2)}) copy-start(bf16[64,2048]{1,0:T(8,128)(2,1)S(1)} %divide_convert_fusion.refs_8_) | copy-start | bytes 786436
  53.1 14.1 %collective-permute-start.43 = (bf16[64,2048]{1,0:T(8,128)(2,1)S(1)}, bf16[64,2048]{1,0:T(8,128)(2,1)S(1)}, u32[]{:S(2)}, u32[]{:S(2)}) collective-permute-start(bf16[64,2048]{1,0:T(8,128)(2,1)S(1)} %divide_convert_fusion.refs_8_), channel_id=1, source_target_pairs={{0,16},{8,24},{16,0},{24,8},{1,17},{9,25},{17,1},{25,9},{2,18},{10... | collective-permute-start | bytes 786440 | tf_op jit(solution)/shard_map/ppermute | solution.py:298
  54.6 18.9 %collective-permute-start.37 = (f32[64,1152]{1,0:T(8,128)S(1)}, f32[64,1152]{1,0:T(8,128)}, u32[]{:S(2)}, u32[]{:S(2)}) collective-permute-start(f32[64,1152]{1,0:T(8,128)S(1)} %copy-done.10), channel_id=1, source_target_pairs={{0,16},{8,24},{16,0},{24,8},{1,17},{9,25},{17,1},{25,9},{2,18},{10... | collective-permute-start | bytes 884744 | tf_op jit(solution)/shard_map/ppermute | solution.py:298
  61.5 8.2 %collective-permute-start.42 = (bf16[64,2048]{1,0:T(8,128)(2,1)S(1)}, bf16[64,2048]{1,0:T(8,128)(2,1)}, u32[]{:S(2)}, u32[]{:S(2)}) collective-permute-start(bf16[64,2048]{1,0:T(8,128)(2,1)S(1)} %divide_convert_fusion.refs_8_), channel_id=1, source_target_pairs={{0,8},{8,0},{16,24},{24,16},{1,9},{9,1},{17,25},{25,17},{2,10},{10... | collective-permute-start | bytes 786440 | tf_op jit(solution)/shard_map/ppermute | solution.py:298
  61.6 12.0 %collective-permute-start.36 = (f32[64,1152]{1,0:T(8,128)S(1)}, f32[64,1152]{1,0:T(8,128)S(1)}, u32[]{:S(2)}, u32[]{:S(2)}) collective-permute-start(f32[64,1152]{1,0:T(8,128)S(1)} %copy-done.10), channel_id=1, source_target_pairs={{0,8},{8,0},{16,24},{24,16},{1,9},{9,1},{17,25},{25,17},{2,10},{10... | collective-permute-start | bytes 884744 | tf_op jit(solution)/shard_map/ppermute | solution.py:298
  62.1 1.5 collective-permute-start.41
  63.6 18.3 %collective-permute-start.28 = (bf16[768,256]{1,0:T(8,128)(2,1)}, bf16[768,256]{1,0:T(8,128)(2,1)}, u32[]{:S(2)}, u32[]{:S(2)}) collective-permute-start(bf16[768,256]{1,0:T(8,128)(2,1)} %get-tuple-element.41.refs_0_), channel_id=1, source_target_pairs={{0,16},{8,24},{16,0},{24,8},{1,17},{9,25},{17,1},{25,9},{2,18},{10... | collective-permute-start | bytes 1179656 | tf_op jit(solution)/shard_map/ppermute | solution.py:298
  67.1 16.8 %collective-permute-start.27 = (bf16[768,256]{1,0:T(8,128)(2,1)}, bf16[768,256]{1,0:T(8,128)(2,1)}, u32[]{:S(2)}, u32[]{:S(2)}) collective-permute-start(bf16[768,256]{1,0:T(8,128)(2,1)} %get-tuple-element.41.refs_0_), channel_id=1, source_target_pairs={{0,8},{8,0},{16,24},{24,16},{1,9},{9,1},{17,25},{25,17},{2,10},{10... | collective-permute-start | bytes 1179656 | tf_op jit(solution)/shard_map/ppermute | solution.py:298
  69.7 14.3 %collective-permute-start.18 = (bf16[256,768]{1,0:T(8,128)(2,1)}, bf16[256,768]{1,0:T(8,128)(2,1)S(1)}, u32[]{:S(2)}, u32[]{:S(2)}) collective-permute-start(bf16[256,768]{1,0:T(8,128)(2,1)} %next.1.refs_2_), channel_id=1, source_target_pairs={{0,8},{8,0},{16,24},{24,16},{1,9},{9,1},{17,25},{25,17},{2,10},{10... | collective-permute-start | bytes 1179656 | tf_op jit(solution)/shard_map/ppermute | solution.py:298
  73.6 12.5 %collective-permute-start.17 = (bf16[256,768]{1,0:T(8,128)(2,1)}, bf16[256,768]{1,0:T(8,128)(2,1)}, u32[]{:S(2)}, u32[]{:S(2)}) collective-permute-start(bf16[256,768]{1,0:T(8,128)(2,1)} %get-tuple-element.38.refs_0_), channel_id=1, source_target_pairs={{0,8},{8,0},{16,24},{24,16},{1,9},{9,1},{17,25},{25,17},{2,10},{10... | collective-permute-start | bytes 1179656 | tf_op jit(solution)/shard_map/ppermute | solution.py:298
  74.3 64.4 %collective-permute-start.11 = (bf16[768,768]{1,0:T(8,128)(2,1)}, bf16[768,768]{1,0:T(8,128)(2,1)S(1)}, u32[]{:S(2)}, u32[]{:S(2)}) collective-permute-start(bf16[768,768]{1,0:T(8,128)(2,1)} %get-tuple-element.37.refs_4_), channel_id=1, source_target_pairs={{0,16},{8,24},{16,0},{24,8},{1,17},{9,25},{17,1},{25,9},{2,18},{10... | collective-permute-start | bytes 3538952 | tf_op jit(solution)/shard_map/ppermute | solution.py:298
  82.0 33.6 %collective-permute-start.15 = (bf16[256,768]{1,0:T(8,128)(2,1)}, bf16[256,768]{1,0:T(8,128)(2,1)S(1)}, u32[]{:S(2)}, u32[]{:S(2)}) collective-permute-start(bf16[256,768]{1,0:T(8,128)(2,1)} %next.1.refs_2_), channel_id=1, source_target_pairs={{0,16},{8,24},{16,0},{24,8},{1,17},{9,25},{17,1},{25,9},{2,18},{10... | collective-permute-start | bytes 1179656 | tf_op jit(solution)/shard_map/ppermute | solution.py:298
  83.9 40.2 %collective-permute-start.13 = (bf16[256,768]{1,0:T(8,128)(2,1)}, bf16[256,768]{1,0:T(8,128)(2,1)}, u32[]{:S(2)}, u32[]{:S(2)}) collective-permute-start(bf16[256,768]{1,0:T(8,128)(2,1)} %get-tuple-element.38.refs_0_), channel_id=1, source_target_pairs={{0,16},{8,24},{16,0},{24,8},{1,17},{9,25},{17,1},{25,9},{2,18},{10... | collective-permute-start | bytes 1179656 | tf_op jit(solution)/shard_map/ppermute | solution.py:298
  84.0 54.1 %collective-permute-start.31 = (bf16[1280,256]{1,0:T(8,128)(2,1)S(1)}, bf16[1280,256]{1,0:T(8,128)(2,1)}, u32[]{:S(2)}, u32[]{:S(2)}) collective-permute-start(bf16[1280,256]{1,0:T(8,128)(2,1)S(1)} %copy-done.3), channel_id=1, source_target_pairs={{0,16},{8,24},{16,0},{24,8},{1,17},{9,25},{17,1},{25,9},{2,18},{10... | collective-permute-start | bytes 1966088 | tf_op jit(solution)/shard_map/ppermute | solution.py:298
  86.0 52.1 %collective-permute-start.30 = (bf16[1280,256]{1,0:T(8,128)(2,1)S(1)}, bf16[1280,256]{1,0:T(8,128)(2,1)S(1)}, u32[]{:S(2)}, u32[]{:S(2)}) collective-permute-start(bf16[1280,256]{1,0:T(8,128)(2,1)S(1)} %copy-done.3), channel_id=1, source_target_pairs={{0,8},{8,0},{16,24},{24,16},{1,9},{9,1},{17,25},{25,17},{2,10},{10... | collective-permute-start | bytes 1966088 | tf_op jit(solution)/shard_map/ppermute | solution.py:298
  115.6 12.2 %collective-permute-start.38 = (f32[64,1152]{1,0:T(8,128)}, f32[64,1152]{1,0:T(8,128)S(1)}, u32[]{:S(2)}, u32[]{:S(2)}) collective-permute-start(f32[64,1152]{1,0:T(8,128)} %collective-permute-done.37.refs_2_), channel_id=1, source_target_pairs={{0,8},{8,0},{16,24},{24,16},{1,9},{9,1},{17,25},{25,17},{2,10},{10... | collective-permute-start | bytes 884744 | tf_op jit(solution)/shard_map/ppermute | solution.py:298
  124.1 1.7 collective-permute-start.44
  125.9 27.8 %collective-permute-start.9 = (bf16[512,768]{1,0:T(8,128)(2,1)}, bf16[512,768]{1,0:T(8,128)(2,1)}, u32[]{:S(2)}, u32[]{:S(2)}) collective-permute-start(bf16[512,768]{1,0:T(8,128)(2,1)} %get-tuple-element.36.refs_6_), channel_id=1, source_target_pairs={{0,16},{8,24},{16,0},{24,8},{1,17},{9,25},{17,1},{25,9},{2,18},{10... | collective-permute-start | bytes 2359304 | tf_op jit(solution)/shard_map/ppermute | solution.py:298
  127.8 25.9 %collective-permute-start.20 = (bf16[512,768]{1,0:T(8,128)(2,1)}, bf16[512,768]{1,0:T(8,128)(2,1)}, u32[]{:S(2)}, u32[]{:S(2)}) collective-permute-start(bf16[512,768]{1,0:T(8,128)(2,1)} %get-tuple-element.36.refs_6_), channel_id=1, source_target_pairs={{0,8},{8,0},{16,24},{24,16},{1,9},{9,1},{17,25},{25,17},{2,10},{10... | collective-permute-start | bytes 2359304 | tf_op jit(solution)/shard_map/ppermute | solution.py:298
  138.2 1.9 %collective-permute-start.29 = (bf16[768,256]{1,0:T(8,128)(2,1)}, bf16[768,256]{1,0:T(8,128)(2,1)S(1)}, u32[]{:S(2)}, u32[]{:S(2)}) collective-permute-start(bf16[768,256]{1,0:T(8,128)(2,1)} %collective-permute-done.28.refs_2_), channel_id=1, source_target_pairs={{0,8},{8,0},{16,24},{24,16},{1,9},{9,1},{17,25},{25,17},{2,10},{10... | collective-permute-start | bytes 1179656 | tf_op jit(solution)/shard_map/ppermute | solution.py:298
  138.2 19.8 %collective-permute-start.19 = (bf16[768,768]{1,0:T(8,128)(2,1)}, bf16[768,768]{1,0:T(8,128)(2,1)}, u32[]{:S(2)}, u32[]{:S(2)}) collective-permute-start(bf16[768,768]{1,0:T(8,128)(2,1)} %get-tuple-element.37.refs_4_), channel_id=1, source_target_pairs={{0,8},{8,0},{16,24},{24,16},{1,9},{9,1},{17,25},{25,17},{2,10},{10... | collective-permute-start | bytes 3538952 | tf_op jit(solution)/shard_map/ppermute | solution.py:298
  139.0 21.6 %collective-permute-start.12 = (bf16[768,768]{1,0:T(8,128)(2,1)S(1)}, bf16[768,768]{1,0:T(8,128)(2,1)S(1)}, u32[]{:S(2)}, u32[]{:S(2)}) collective-permute-start(bf16[768,768]{1,0:T(8,128)(2,1)S(1)} %collective-permute-done.11.refs_0_), channel_id=1, source_target_pairs={{0,8},{8,0},{16,24},{24,16},{1,9},{9,1},{17,25},{25,17},{2,10},{10... | collective-permute-start | bytes 3538952 | tf_op jit(solution)/shard_map/ppermute | solution.py:298
  140.1 14.1 %collective-permute-start.16 = (bf16[256,768]{1,0:T(8,128)(2,1)S(1)}, bf16[256,768]{1,0:T(8,128)(2,1)S(1)}, u32[]{:S(2)}, u32[]{:S(2)}) collective-permute-start(bf16[256,768]{1,0:T(8,128)(2,1)S(1)} %collective-permute-done.15.refs_2_), channel_id=1, source_target_pairs={{0,8},{8,0},{16,24},{24,16},{1,9},{9,1},{17,25},{25,17},{2,10},{10... | collective-permute-start | bytes 1179656 | tf_op jit(solution)/shard_map/ppermute | solution.py:298
  153.7 26.2 %collective-permute-start.10 = (bf16[512,768]{1,0:T(8,128)(2,1)}, bf16[512,768]{1,0:T(8,128)(2,1)}, u32[]{:S(2)}, u32[]{:S(2)}) collective-permute-start(bf16[512,768]{1,0:T(8,128)(2,1)} %collective-permute-done.9.refs_0_), channel_id=1, source_target_pairs={{0,8},{8,0},{16,24},{24,16},{1,9},{9,1},{17,25},{25,17},{2,10},{10... | collective-permute-start | bytes 2359304 | tf_op jit(solution)/shard_map/ppermute | solution.py:298
  153.7 5.4 %collective-permute-start.32 = (bf16[1280,256]{1,0:T(8,128)(2,1)}, bf16[1280,256]{1,0:T(8,128)(2,1)}, u32[]{:S(2)}, u32[]{:S(2)}) collective-permute-start(bf16[1280,256]{1,0:T(8,128)(2,1)} %collective-permute-done.31.refs_6_), channel_id=1, source_target_pairs={{0,8},{8,0},{16,24},{24,16},{1,9},{9,1},{17,25},{25,17},{2,10},{10... | collective-permute-start | bytes 1966088 | tf_op jit(solution)/shard_map/ppermute | solution.py:298
  154.9 2.9 %collective-permute-start.14 = (bf16[256,768]{1,0:T(8,128)(2,1)}, bf16[256,768]{1,0:T(8,128)(2,1)}, u32[]{:S(2)}, u32[]{:S(2)}) collective-permute-start(bf16[256,768]{1,0:T(8,128)(2,1)} %collective-permute-done.13.refs_0_), channel_id=1, source_target_pairs={{0,8},{8,0},{16,24},{24,16},{1,9},{9,1},{17,25},{25,17},{2,10},{10... | collective-permute-start | bytes 1179656 | tf_op jit(solution)/shard_map/ppermute | solution.py:298
  157.8 25.4 %collective-permute-start.4 = (bf16[112,768]{1,0:T(8,128)(2,1)S(1)}, bf16[112,768]{1,0:T(8,128)(2,1)S(1)}, u32[]{:S(2)}, u32[]{:S(2)}) collective-permute-start(bf16[112,768]{1,0:T(8,128)(2,1)S(1)} %collective-permute-done.3.refs_0_), channel_id=1, source_target_pairs={{0,8},{8,0},{16,24},{24,16},{1,9},{9,1},{17,25},{25,17},{2,10},{10... | collective-permute-start | bytes 516104 | tf_op jit(solution)/shard_map/ppermute | solution.py:298
  158.0 24.4 %collective-permute-start.8 = (bf16[128,768]{1,0:T(8,128)(2,1)S(1)}, bf16[128,768]{1,0:T(8,128)(2,1)S(1)}, u32[]{:S(2)}, u32[]{:S(2)}) collective-permute-start(bf16[128,768]{1,0:T(8,128)(2,1)S(1)} %collective-permute-done.7.refs_0_), channel_id=1, source_target_pairs={{0,8},{8,0},{16,24},{24,16},{1,9},{9,1},{17,25},{25,17},{2,10},{10... | collective-permute-start | bytes 589832 | tf_op jit(solution)/shard_map/ppermute | solution.py:298
  159.1 24.1 %collective-permute-start.5 = (bf16[16,768]{1,0:T(8,128)(2,1)S(1)}, bf16[16,768]{1,0:T(8,128)(2,1)S(1)}, u32[]{:S(2)}, u32[]{:S(2)}) collective-permute-start(bf16[16,768]{1,0:T(8,128)(2,1)S(1)} %copy-done.20), channel_id=1, source_target_pairs={{0,16},{8,24},{16,0},{24,8},{1,17},{9,25},{17,1},{25,9},{2,18},{10... | collective-permute-start | bytes 73736 | tf_op jit(solution)/shard_map/ppermute | solution.py:298
  160.6 22.6 %collective-permute-start.6 = (bf16[16,768]{1,0:T(8,128)(2,1)S(1)}, bf16[16,768]{1,0:T(8,128)(2,1)S(1)}, u32[]{:S(2)}, u32[]{:S(2)}) collective-permute-start(bf16[16,768]{1,0:T(8,128)(2,1)S(1)} %copy-done.20), channel_id=1, source_target_pairs={{0,24},{8,16},{16,8},{24,0},{1,25},{9,17},{17,9},{25,1},{2,26},{10... | collective-permute-start | bytes 73736 | tf_op jit(solution)/shard_map/ppermute | solution.py:298
  (26 other events, 391.8 us)

commit v4 on v3

--- a/solution.py
+++ b/solution.py
@@ -70,7 +70,7 @@
 PARTS_Q = 2
 
 
-def narrow_kernel(places, wq, sq, wk, sk, wv, sv, nt, ns, rk, rv, early, message, *refs):
+def narrow_kernel(places, wq, sq, wk, sk, wv, sv, nt, ns, early, message, *refs):
     *buffers, gain_a, gain_b, note, sum_kv, in_kv, in_q, in_gain, outs = refs
     of_kv, of_q = buffers[:4], buffers[4:]
     place_kv, place_norm = places
@@ -88,14 +88,13 @@
     for part in range(PARTS):
         wait_kv(part)
         at = pl.ds(part * step, step)
-        for which, (w, s, r) in enumerate(((of_kv[0], of_kv[1], rk), (of_kv[2], of_kv[3], rv))):
+        for which, (w, s) in enumerate((of_kv[:2], of_kv[2:])):
             new = average(s[at, :], w[at, :])
             sum_kv[which * heads + part * step : which * heads + (part + 1) * step, :] = (
                 lane_sum(jnp.abs(new))
             )
-            s[at, :] = new
-            write(s.at[at, :], r.at[at, :])
             if which == 0:
+                s[at, pl.ds(0, early.shape[1])] = new[:, : early.shape[1]]
                 write(s.at[at, pl.ds(0, early.shape[1])], early.at[at, :])
     total = jnp.zeros((8, of_q[0].shape[1]), jnp.float32)
     step = rows // PARTS_Q
@@ -122,9 +121,12 @@
     return pieces[0]
 
 
-def first_kernel(places, heads, gain, count, me, rk, wq, sq, *refs):
-    n = len(refs) - 7
-    messages, (own_k, own_a, own_b, inv_k, factor_k, factor_v, norms) = refs[:n], refs[n:]
+def first_kernel(places, heads, gain, count, me, wk, sk, wv, sv, wq, sq, *refs):
+    n = len(refs) - 9
+    messages, outs = refs[:n], refs[n:]
+    rk, rv, own_k, own_a, own_b, inv_k, factor_k, factor_v, norms = outs
+    rk[...] = average(sk[...], wk[...])
+    rv[...] = average(sv[...], wv[...])
     place_kv, place_norm = places
     pieces = [m[...] for m in messages]
     for distance, piece in enumerate(pieces):
@@ -315,17 +317,15 @@
     place_norm = place_kv + round_up(2 * heads, LANES)
     places = (place_kv, place_norm)
     length = place_norm + round_up(gain, LANES)
-    ahead = rows * 9 // 16 // LANES * LANES
-    rk, rv, early, message = pl.pallas_call(
+    ahead = rows * 8 // 16 // LANES * LANES
+    early, message = pl.pallas_call(
         functools.partial(narrow_kernel, places),
         out_shape=(
-            shaped((heads, rows), f32),
-            shaped((heads, rows), f32),
             shaped((heads, ahead), f32),
             shaped((1, length), f32),
         ),
         in_specs=[HBM] * 8,
-        out_specs=[HBM] * 4,
+        out_specs=[HBM] * 2,
         scratch_shapes=[pltpu.VMEM((heads, rows), f32)] * 4
         + [pltpu.VMEM((rows, columns), f32)] * 2
         + [
@@ -345,12 +345,14 @@
     found_early = gather(early)
     total = tree(list(messages)) / (n * rows)
     of_v = total[0, place_kv + heads : place_kv + 2 * heads, None]
-    own_v = (rv / of_v).astype(bf16)
+    own_v = (average(sv.T, wv.T) / of_v).astype(bf16)
     cut_a = rows * CUT_A // 16
-    own_k, *own_a, inv_k, factor_k, factor_v, norms = pl.pallas_call(
+    rk, rv, own_k, *own_a, inv_k, factor_k, factor_v, norms = pl.pallas_call(
         functools.partial(first_kernel, places, heads, gain, n * rows),
         grid=(1,),
         out_shape=(
+            shaped((heads, rows), f32),
+            shaped((heads, rows), f32),
             shaped((heads, rows - ahead), bf16),
             shaped((cut_a, columns), bf16),
             shaped((rows - cut_a, columns), bf16),
@@ -359,8 +361,13 @@
             shaped((1, heads), f32),
             shaped((n, gain), f32),
         ),
-        in_specs=[SMEM, full(rk)] + [once((rows, columns))] * 2 + [full(message)] * n,
+        in_specs=[SMEM]
+        + [once((heads, rows))] * 4
+        + [once((rows, columns))] * 2
+        + [full(message)] * n,
         out_specs=[
+            once((heads, rows)),
+            once((heads, rows)),
             once((heads, rows - ahead)),
             once((cut_a, columns)),
             once((rows - cut_a, columns)),
@@ -371,7 +378,7 @@
         ],
         cost_estimate=cost(rows * columns * 8, rows * columns * 12),
         name="first",
-    )(me, rk, wq, sq, *messages)
+    )(me, wk.T, sk.T, wv.T, sv.T, wq, sq, *messages)
     found_v, found_k = gather(own_v), gather(own_k)
     found_a = [gather(piece) for piece in own_a]
 

time: 185 us -> 182 us (0.984)
  starting transfers between devices: 31.4 us -> 25.5 us
  waiting for transfers between devices: 89.5 us -> 94.1 us
    ppermute x45, starting transfers between devices: 31.4 us -> 25.5 us  [swap(): return lax.ppermute(array, axis, [(i, i ^ distance) for i in range(size)])]
    ppermute x45, waiting for transfers between devices: 89.5 us -> 94.1 us  [swap(): return lax.ppermute(array, axis, [(i, i ^ distance) for i in range(size)])]
    unnamed x59 -> x61, local copies, waits for them, and re-layouts: 5.63 us -> 4.96 us
  transfers between devices with their start and end apart: 45 -> 45, of which waited for: 15 -> 14; matrix products, arithmetic and copies ran while one was open for 2% -> 2% of each run, Pallas kernels for 26% -> 27%
where the time goes in v4:
time: 182 us
  waiting for transfers between devices  94.1 us (52%)
  Pallas kernels  54 us (30%)
  starting transfers between devices  25.5 us (14%)
  local copies, waits for them, and re-layouts  4.97 us (3%)
  other arithmetic  2.35 us (1%)
    ppermute x45, waiting for transfers between devices, swap(): return lax.ppermute(array, axis, [(i, i ^ distance) for i in range(size)])  94.1 us
    ppermute x45, starting transfers between devices, swap(): return lax.ppermute(array, axis, [(i, i ^ distance) for i in range(size)])  25.5 us
    pallas_call x7, Pallas kernels, place(): pl.pallas_call(functools.partial(place_kernel, [job[1:] for job in jobs],...  19.4 us
    pallas_call x1, Pallas kernels, on_device(): pl.pallas_call(functools.partial(fourth_kernel, sizes), out_shape=[shaped...  11.1 us
    pallas_call x1, Pallas kernels, on_device(): pl.pallas_call(sizes_kernel, out_shape=shaped((1, width), f32), in_specs=...  6.87 us
    unnamed x61, local copies, waits for them, and re-layouts  4.96 us
    pallas_call x1, Pallas kernels, on_device(): pl.pallas_call(functools.partial(first_kernel, places, heads, gain, n * r...  4.71 us
    pallas_call x1, Pallas kernels, on_device(): pl.pallas_call(functools.partial(narrow_kernel, places), out_shape=(shape...  3.98 us
  transfers between devices with their start and end apart: 45, of which 14 were waited for; matrix products, arithmetic and copies ran while one was open for 2% of the time, Pallas kernels for 27%

profile of v4, /device:TPU:0, one launch (start us, length us, event | category | flops | bytes accessed | tf_op | source)
XLA Modules:
  0.0 181.9 jit_solution(13651393793970450068)
XLA Ops:
  0.6 4.0 %narrow.1 = (f32[64,1024]{1,0:T(8,128)}, f32[1,640]{1,0:T(1,128)}) custom-call(f32[2048,1024]{1,0:T(8,128)} %wq.11, f32[2048,1024]{1,0:T(8,128)} %sq.11, f32[64,2048]{1,0:T(8,128)} %bitcast.30, f32[64,2048]{1,0:T(8,128)} %bitcast.32, f32[64,2048]{1,0:T(8,128)} %bitcast.26, f32[64,2048]{1,0:T(8,128)} %bitcast.28, f32[1,256]{1,0:T(1,128)} %bitcast.37, ...), custom_call_target="tpu_custom_call" | custom-call | flops 2097152 | bytes 4194304 | tf_op jit(solution)/shard_map/narrow/pallas_call | solution.py:321
  4.6 3.0 %collective-permute-start.25 = (f32[1,640]{1,0:T(1,128)}, f32[1,640]{1,0:T(1,128)S(1)}, u32[]{:S(2)}, u32[]{:S(2)}) collective-permute-start(f32[1,640]{1,0:T(1,128)} %get-tuple-element.39.refs_0_), channel_id=1, source_target_pairs={{0,16},{8,24},{16,0},{24,8},{1,17},{9,25},{17,1},{25,9},{2,18},{10... | collective-permute-start | bytes 7688 | tf_op jit(solution)/shard_map/ppermute | solution.py:300
  7.7 1.8 collective-permute-done.25.refs_2_
  9.5 6.9 %sizes.1.refs_0_ = f32[1,1024]{1,0:T(1,128)} custom-call(f32[2048,1024]{1,0:T(8,128)} %wq.11, f32[2048,1024]{1,0:T(8,128)} %sq.11), custom_call_target="tpu_custom_call" | custom-call | flops 16777216 | bytes 16777216 | tf_op jit(solution)/shard_map/sizes/pallas_call | solution.py:386
  16.3 2.1 %collective-permute-start.1 = (f32[1,1024]{1,0:T(1,128)}, f32[1,1024]{1,0:T(1,128)S(1)}, u32[]{:S(2)}, u32[]{:S(2)}) collective-permute-start(f32[1,1024]{1,0:T(1,128)} %sizes.1.refs_0_), channel_id=1, source_target_pairs={{0,16},{8,24},{16,0},{24,8},{1,17},{9,25},{17,1},{25,9},{2,18},{10... | collective-permute-start | bytes 12296 | tf_op jit(solution)/shard_map/ppermute | solution.py:300
  19.0 4.7 %first.1 = (f32[64,2048]{1,0:T(8,128)}, f32[64,2048]{1,0:T(8,128)}, bf16[64,1024]{1,0:T(8,128)(2,1)}, bf16[768,256]{1,0:T(8,128)(2,1)}, bf16[1280,256]{1,0:T(8,1...) custom-call(s32[1]{0:T(128)} %bitcast.me, f32[64,2048]{1,0:T(8,128)} %bitcast.31, ...), custom_call_target="tpu_custom_call" | custom-call | flops 4194304 | bytes 6291456 | tf_op jit(solution)/shard_map/first/pallas_call | solution.py:350
  23.8 0.7 convert_bitcast_fusion
  24.5 1.5 collective-permute-start.33
  26.5 1.5 collective-permute-done.33
  28.0 0.7 broadcast_select_fusion.5
  28.7 1.6 collective-permute-start.34
  30.9 1.5 collective-permute-start.40
  32.4 0.6 copy-done.25
  33.0 0.6 copy-done.26
  33.6 2.4 %third.1 = (bf16[256,768]{1,0:T(8,128)(2,1)}, f32[1,768]{1,0:T(1,128)}, f32[1,1024]{1,0:T(1,128)}) custom-call(f32[2048,1024]{1,0:T(8,128)} %wq.11, f32[2048,1024]{1,0:T(8,128)} %sq.11, f32[1,1024]{1,0:T(1,128)} %sizes.1.refs_0_, f32[1,1024]{1,0:T(1,128)} %copy-done.25, f32[1,1024]{1,0:T(1,128)} %copy-done.24, f32[1,1024]{1,0:T(1,128)} %copy-done.26), custom_call_target="tpu_custom_call" | custom-call | flops 1572864 | bytes 1966080 | tf_op jit(solution)/shard_map/third/pallas_call | solution.py:406
  36.0 11.1 %fourth.1 = (f32[2048,1024]{1,0:T(8,128)}, bf16[768,768]{1,0:T(8,128)(2,1)}, bf16[512,768]{1,0:T(8,128)(2,1)}, bf16[128,768]{1,0:T(8,128)(2,1)}, bf16[112,768]{1,0:T(8,128)(2,1)}, /*index=5*/bf16[16,768]{1,0:T(8,128)(2,1)}) custom-call(f32[2048,1024]{1,0:T(8,128)} %wq.11, f32[2048,1024]{1,0:T(8,128)} %sq.11, f32[1,768]{1,0:T(1,128)} %get-tuple-element.32.inv), custom_call_target="tpu_custom_call" | custom-call | flops 16777216 | bytes 29360128 | tf_op jit(solution)/shard_map/fourth/pallas_call | solution.py:424
  47.3 2.7 %collective-permute-start.35 = (bf16[4,4,256]{2,0,1:T(4,128)(2,1)S(1)}, bf16[4,4,256]{2,0,1:T(4,128)(2,1)S(1)}, u32[]{:S(2)}, u32[]{:S(2)}) collective-permute-start(bf16[4,4,256]{2,0,1:T(4,128)(2,1)S(1)} %pad_maximum_fusion.1), channel_id=1, source_target_pairs={{0,4},{1,5},{2,6},{3,7},{4,0},{5,1},{6,2},{7,3},{8,12},{9,13},{10,... | collective-permute-start | bytes 24584 | tf_op jit(solution)/shard_map/ppermute | solution.py:300
  49.9 0.8 multiply_bitcast_fusion
  50.7 1.2 collective-permute-done.35
  53.7 1.0 collective-permute-start.43
  54.7 5.2 %collective-permute-done.3.refs_0_ = bf16[112,768]{1,0:T(8,128)(2,1)S(1)} collective-permute-done((bf16[112,768]{1,0:T(8,128)(2,1)}, bf16[112,768]{1,0:T(8,128)(2,1)S(1)}, u32[]{:S(2)}, u32[]{:S(2)}) %collective-permute-start.3) | collective-permute-done | bytes 172064 | tf_op jit(solution)/shard_map/ppermute | solution.py:300
  59.9 0.6 collective-permute-start.7
  60.5 8.3 %collective-permute-done.7.refs_0_ = bf16[128,768]{1,0:T(8,128)(2,1)S(1)} collective-permute-done((bf16[128,768]{1,0:T(8,128)(2,1)}, bf16[128,768]{1,0:T(8,128)(2,1)S(1)}, u32[]{:S(2)}, u32[]{:S(2)}) %collective-permute-start.7) | collective-permute-done | bytes 196640 | tf_op jit(solution)/shard_map/ppermute | solution.py:300
  69.4 0.7 copy-done.13
  70.6 2.4 %next.1.refs_2_ = bf16[256,768]{1,0:T(8,128)(2,1)} custom-call(f32[2048,1024]{1,0:T(8,128)} %wq.11, f32[2048,1024]{1,0:T(8,128)} %sq.11, f32[1,768]{1,0:T(1,128)} %get-tuple-element.32.inv), custom_call_target="tpu_custom_call" | custom-call | flops 1572864 | bytes 1966080 | tf_op jit(solution)/shard_map/next/pallas_call | solution.py:415
  73.8 1.5 collective-permute-start.11
  75.3 5.9 %collective-permute-done.28.refs_2_ = bf16[768,256]{1,0:T(8,128)(2,1)} collective-permute-done((bf16[768,256]{1,0:T(8,128)(2,1)}, bf16[768,256]{1,0:T(8,128)(2,1)}, u32[]{:S(2)}, u32[]{:S(2)}) %collective-permute-start.28) | collective-permute-done | bytes 393248 | tf_op jit(solution)/shard_map/ppermute | solution.py:300
  81.2 2.0 %collective-permute-start.13 = (bf16[256,768]{1,0:T(8,128)(2,1)S(1)}, bf16[256,768]{1,0:T(8,128)(2,1)}, u32[]{:S(2)}, u32[]{:S(2)}) collective-permute-start(bf16[256,768]{1,0:T(8,128)(2,1)S(1)} %copy-done.7), channel_id=1, source_target_pairs={{0,16},{8,24},{16,0},{24,8},{1,17},{9,25},{17,1},{25,9},{2,18},{10... | collective-permute-start | bytes 1179656 | tf_op jit(solution)/shard_map/ppermute | solution.py:300
  83.3 0.6 copy-done.8
  83.9 30.8 %collective-permute-done.15.refs_2_ = bf16[256,768]{1,0:T(8,128)(2,1)S(1)} collective-permute-done((bf16[256,768]{1,0:T(8,128)(2,1)}, bf16[256,768]{1,0:T(8,128)(2,1)S(1)}, u32[]{:S(2)}, u32[]{:S(2)}) %collective-permute-start.15) | collective-permute-done | bytes 393248 | tf_op jit(solution)/shard_map/ppermute | solution.py:300
  114.7 8.5 %collective-permute-done.13.refs_0_ = bf16[256,768]{1,0:T(8,128)(2,1)} collective-permute-done((bf16[256,768]{1,0:T(8,128)(2,1)S(1)}, bf16[256,768]{1,0:T(8,128)(2,1)}, u32[]{:S(2)}, u32[]{:S(2)}) %collective-permute-start.13) | collective-permute-done | bytes 393248 | tf_op jit(solution)/shard_map/ppermute | solution.py:300
  123.4 1.6 collective-permute-done.44.refs_11_
  125.2 12.2 %collective-permute-done.31.refs_6_ = bf16[1280,256]{1,0:T(8,128)(2,1)} collective-permute-done((bf16[1280,256]{1,0:T(8,128)(2,1)S(1)}, bf16[1280,256]{1,0:T(8,128)(2,1)}, u32[]{:S(2)}, u32[]{:S(2)}) %collective-permute-start.31) | collective-permute-done | bytes 655392 | tf_op jit(solution)/shard_map/ppermute | solution.py:300
  138.7 0.6 collective-permute-done.29.refs_3_
  139.4 13.0 %collective-permute-done.9.refs_0_ = bf16[512,768]{1,0:T(8,128)(2,1)} collective-permute-done((bf16[512,768]{1,0:T(8,128)(2,1)}, bf16[512,768]{1,0:T(8,128)(2,1)}, u32[]{:S(2)}, u32[]{:S(2)}) %collective-permute-start.9) | collective-permute-done | bytes 786464 | tf_op jit(solution)/shard_map/ppermute | solution.py:300
  153.0 0.8 copy-done.10
  153.7 2.8 %collective-permute-done.14.refs_1_ = bf16[256,768]{1,0:T(8,128)(2,1)} collective-permute-done((bf16[256,768]{1,0:T(8,128)(2,1)}, bf16[256,768]{1,0:T(8,128)(2,1)}, u32[]{:S(2)}, u32[]{:S(2)}) %collective-permute-start.14) | collective-permute-done | bytes 393248 | tf_op jit(solution)/shard_map/ppermute | solution.py:300
  157.1 0.6 collective-permute-start.5
  157.7 1.0 collective-permute-start.6
  158.7 0.6 copy.25
  159.3 3.1 %place_kv.1 = (bf16[64,8192]{1,0:T(8,128)(2,1)}, bf16[64,8192]{1,0:T(8,128)(2,1)}) custom-call(s32[1]{0:T(128)} %bitcast.me, f32[64,128]{1,0:T(8,128)} %get-tuple-element.43.inv, f32[64,1024]{1,0:T(8,128)} %get-tuple-element.44.refs_0_, f32[64,1024]{1,0:T(8,128)} %copy-done.13, f32[64,1024]{1,0:T(8,128)} %collective-permute-done.37.refs_2_, ...), custom_call_target="tpu_custom_call" | custom-call | flops 8388608 | bytes 4194304 | tf_op jit(solution)/shard_map/place_kv/pallas_call | solution.py:482
  162.4 4.2 %shard_map.159.refs_14_ = bf16[8192,1024]{1,0:T(8,128)(2,1)} custom-call(s32[1]{0:T(128)} %bitcast.me, bf16[768,256]{1,0:T(8,128)(2,1)} %get-tuple-element.40.refs_0_, bf16[768,256]{1,0:T(8,128)(2,1)} %collective-permute-done.27.refs_1_, bf16[768,256]{1,0:T(8,128)(2,1)} %collective-permute-done.28.refs_2_, bf16[768,256]{1,0:T(8,128)(2,1)} %copy-done.11, ...), custom_call_target="tpu_custom_call" | custom-call | flops 16777216 | bytes 8388608 | tf_op jit(solution)/shard_map/pallas_call | solution.py:444
  166.6 5.5 %shard_map.160.refs_4_ = bf16[8192,1024]{1,0:T(8,128)(2,1)} custom-call(s32[1]{0:T(128)} %bitcast.me, bf16[256,768]{1,0:T(8,128)(2,1)} %get-tuple-element.38.refs_0_, bf16[256,768]{1,0:T(8,128)(2,1)} %collective-permute-done.17.refs_1_, bf16[256,768]{1,0:T(8,128)(2,1)} %next.1.refs_2_, bf16[256,768]{1,0:T(8,128)(2,1)} %copy-done.8, ...), custom_call_target="tpu_custom_call", output_to_operand_aliasing={{}: (15, {})} | custom-call | flops 25165824 | bytes 12582912 | tf_op jit(solution)/shard_map/pallas_call | solution.py:444
  172.2 2.5 %shard_map.161.refs_2_ = bf16[8192,1024]{1,0:T(8,128)(2,1)} custom-call(s32[1]{0:T(128)} %bitcast.me, bf16[256,768]{1,0:T(8,128)(2,1)} %collective-permute-done.13.refs_0_, bf16[256,768]{1,0:T(8,128)(2,1)} %collective-permute-done.14.refs_1_, bf16[256,768]{1,0:T(8,128)(2,1)} %copy-done.9, ...), custom_call_target="tpu_custom_call", output_to_operand_aliasing={{}: (5, {})} | custom-call | flops 6291456 | bytes 3145728 | tf_op jit(solution)/shard_map/pallas_call | solution.py:444
  174.8 3.0 %shard_map.162.refs_2_ = bf16[8192,1024]{1,0:T(8,128)(2,1)} custom-call(s32[1]{0:T(128)} %bitcast.me, bf16[768,768]{1,0:T(8,128)(2,1)} %copy-done.2, bf16[768,768]{1,0:T(8,128)(2,1)} %copy-done.3, bf16[8192,1024]{1,0:T(8,128)(2,1)} %shard_map.161.refs_2_), custom_call_target="tpu_custom_call", output_to_operand_aliasing={{}: (3, {})} | custom-call | flops 9437184 | bytes 4718592 | tf_op jit(solution)/shard_map/pallas_call | solution.py:444
  177.8 2.5 %shard_map.163.refs_2_ = bf16[8192,1024]{1,0:T(8,128)(2,1)} custom-call(s32[1]{0:T(128)} %bitcast.me, bf16[512,768]{1,0:T(8,128)(2,1)} %collective-permute-done.9.refs_0_, bf16[512,768]{1,0:T(8,128)(2,1)} %collective-permute-done.10.refs_1_, bf16[8192,1024]{1,0:T(8,128)(2,1)} %shard_map.162.refs_2_), custom_call_target="tpu_custom_call", output_to_operand_aliasing={{}: (3, {})} | custom-call | flops 6291456 | bytes 3145728 | tf_op jit(solution)/shard_map/pallas_call | solution.py:444
  180.4 0.8 shard_map.164.refs_4_
  181.2 0.8 shard_map.165
  (127 shorter events, 8.4 us)
Async XLA Ops:
  4.6 4.8 %collective-permute-start.25 = (f32[1,640]{1,0:T(1,128)}, f32[1,640]{1,0:T(1,128)S(1)}, u32[]{:S(2)}, u32[]{:S(2)}) collective-permute-start(f32[1,640]{1,0:T(1,128)} %get-tuple-element.39.refs_0_), channel_id=1, source_target_pairs={{0,16},{8,24},{16,0},{24,8},{1,17},{9,25},{17,1},{25,9},{2,18},{10... | collective-permute-start | bytes 7688 | tf_op jit(solution)/shard_map/ppermute | solution.py:300
  7.7 10.8 %collective-permute-start.24 = (f32[1,640]{1,0:T(1,128)}, f32[1,640]{1,0:T(1,128)S(1)}, u32[]{:S(2)}, u32[]{:S(2)}) collective-permute-start(f32[1,640]{1,0:T(1,128)} %get-tuple-element.39.refs_0_), channel_id=1, source_target_pairs={{0,8},{8,0},{16,24},{24,16},{1,9},{9,1},{17,25},{25,17},{2,10},{10... | collective-permute-start | bytes 7688 | tf_op jit(solution)/shard_map/ppermute | solution.py:300
  9.5 9.0 %collective-permute-start.26 = (f32[1,640]{1,0:T(1,128)S(1)}, f32[1,640]{1,0:T(1,128)S(1)}, u32[]{:S(2)}, u32[]{:S(2)}) collective-permute-start(f32[1,640]{1,0:T(1,128)S(1)} %collective-permute-done.25.refs_2_), channel_id=1, source_target_pairs={{0,8},{8,0},{16,24},{24,16},{1,9},{9,1},{17,25},{25,17},{2,10},{10... | collective-permute-start | bytes 7688 | tf_op jit(solution)/shard_map/ppermute | solution.py:300
  16.3 9.6 %collective-permute-start.1 = (f32[1,1024]{1,0:T(1,128)}, f32[1,1024]{1,0:T(1,128)S(1)}, u32[]{:S(2)}, u32[]{:S(2)}) collective-permute-start(f32[1,1024]{1,0:T(1,128)} %sizes.1.refs_0_), channel_id=1, source_target_pairs={{0,16},{8,24},{16,0},{24,8},{1,17},{9,25},{17,1},{25,9},{2,18},{10... | collective-permute-start | bytes 12296 | tf_op jit(solution)/shard_map/ppermute | solution.py:300
  24.5 3.6 %collective-permute-start.33 = (bf16[4,1,256]{2,0,1:T(4,128)(2,1)S(1)}, bf16[4,1,256]{2,0,1:T(4,128)(2,1)S(1)}, u32[]{:S(2)}, u32[]{:S(2)}) collective-permute-start(bf16[4,1,256]{2,0,1:T(4,128)(2,1)S(1)} %convert_bitcast_fusion), channel_id=1, source_target_pairs={{0,1},{1,0},{2,3},{3,2},{4,5},{5,4},{6,7},{7,6},{8,9},{9,8},{10,11... | collective-permute-start | bytes 6152 | tf_op jit(solution)/shard_map/ppermute | solution.py:300
  26.0 6.4 %collective-permute-start = (f32[1,1024]{1,0:T(1,128)S(1)}, f32[1,1024]{1,0:T(1,128)S(1)}, u32[]{:S(2)}, u32[]{:S(2)}) collective-permute-start(f32[1,1024]{1,0:T(1,128)S(1)} %copy-done.23), channel_id=1, source_target_pairs={{0,8},{8,0},{16,24},{24,16},{1,9},{9,1},{17,25},{25,17},{2,10},{10... | collective-permute-start | bytes 12296 | tf_op jit(solution)/shard_map/ppermute | solution.py:300
  26.0 6.4 %collective-permute-start.2 = (f32[1,1024]{1,0:T(1,128)S(1)}, f32[1,1024]{1,0:T(1,128)S(1)}, u32[]{:S(2)}, u32[]{:S(2)}) collective-permute-start(f32[1,1024]{1,0:T(1,128)S(1)} %collective-permute-done.1.refs_2_), channel_id=1, source_target_pairs={{0,8},{8,0},{16,24},{24,16},{1,9},{9,1},{17,25},{25,17},{2,10},{10... | collective-permute-start | bytes 12296 | tf_op jit(solution)/shard_map/ppermute | solution.py:300
  28.7 18.5 %collective-permute-start.34 = (bf16[4,2,256]{2,0,1:T(4,128)(2,1)S(1)}, bf16[4,2,256]{2,0,1:T(4,128)(2,1)S(1)}, u32[]{:S(2)}, u32[]{:S(2)}) collective-permute-start(bf16[4,2,256]{2,0,1:T(4,128)(2,1)S(1)} %pad_maximum_fusion.2), channel_id=1, source_target_pairs={{0,2},{1,3},{2,0},{3,1},{4,6},{5,7},{6,4},{7,5},{8,10},{9,11},{10,... | collective-permute-start | bytes 12296 | tf_op jit(solution)/shard_map/ppermute | solution.py:300
  30.4 39.0 %collective-permute-start.37 = (f32[64,1024]{1,0:T(8,128)S(1)}, f32[64,1024]{1,0:T(8,128)}, u32[]{:S(2)}, u32[]{:S(2)}) collective-permute-start(f32[64,1024]{1,0:T(8,128)S(1)} %copy-done.12), channel_id=1, source_target_pairs={{0,16},{8,24},{16,0},{24,8},{1,17},{9,25},{17,1},{25,9},{2,18},{10... | collective-permute-start | bytes 786440 | tf_op jit(solution)/shard_map/ppermute | solution.py:300
  30.9 21.5 %collective-permute-start.40 = (bf16[64,1024]{1,0:T(8,128)(2,1)}, bf16[64,1024]{1,0:T(8,128)(2,1)S(1)}, u32[]{:S(2)}, u32[]{:S(2)}) collective-permute-start(bf16[64,1024]{1,0:T(8,128)(2,1)} %get-tuple-element.45.refs_4_), channel_id=1, source_target_pairs={{0,16},{8,24},{16,0},{24,8},{1,17},{9,25},{17,1},{25,9},{2,18},{10... | collective-permute-start | bytes 393224 | tf_op jit(solution)/shard_map/ppermute | solution.py:300
  32.4 20.5 %collective-permute-start.39 = (bf16[64,1024]{1,0:T(8,128)(2,1)}, bf16[64,1024]{1,0:T(8,128)(2,1)S(1)}, u32[]{:S(2)}, u32[]{:S(2)}) collective-permute-start(bf16[64,1024]{1,0:T(8,128)(2,1)} %get-tuple-element.45.refs_4_), channel_id=1, source_target_pairs={{0,8},{8,0},{16,24},{24,16},{1,9},{9,1},{17,25},{25,17},{2,10},{10... | collective-permute-start | bytes 393224 | tf_op jit(solution)/shard_map/ppermute | solution.py:300
  47.2 4.8 %collective-permute-start.23 = (bf16[16,768]{1,0:T(8,128)(2,1)}, bf16[16,768]{1,0:T(8,128)(2,1)S(1)}, u32[]{:S(2)}, u32[]{:S(2)}) collective-permute-start(bf16[16,768]{1,0:T(8,128)(2,1)} %get-tuple-element.34.refs_12_), channel_id=1, source_target_pairs={{0,8},{8,0},{16,24},{24,16},{1,9},{9,1},{17,25},{25,17},{2,10},{10... | collective-permute-start | bytes 73736 | tf_op jit(solution)/shard_map/ppermute | solution.py:300
  47.3 4.6 %collective-permute-start.35 = (bf16[4,4,256]{2,0,1:T(4,128)(2,1)S(1)}, bf16[4,4,256]{2,0,1:T(4,128)(2,1)S(1)}, u32[]{:S(2)}, u32[]{:S(2)}) collective-permute-start(bf16[4,4,256]{2,0,1:T(4,128)(2,1)S(1)} %pad_maximum_fusion.1), channel_id=1, source_target_pairs={{0,4},{1,5},{2,6},{3,7},{4,0},{5,1},{6,2},{7,3},{8,12},{9,13},{10,... | collective-permute-start | bytes 24584 | tf_op jit(solution)/shard_map/ppermute | solution.py:300
  51.9 17.5 %collective-permute-start.36 = (f32[64,1024]{1,0:T(8,128)S(1)}, f32[64,1024]{1,0:T(8,128)S(1)}, u32[]{:S(2)}, u32[]{:S(2)}) collective-permute-start(f32[64,1024]{1,0:T(8,128)S(1)} %copy-done.12), channel_id=1, source_target_pairs={{0,8},{8,0},{16,24},{24,16},{1,9},{9,1},{17,25},{25,17},{2,10},{10... | collective-permute-start | bytes 786440 | tf_op jit(solution)/shard_map/ppermute | solution.py:300
  51.9 1.8 collective-permute-start.22
  52.4 106.9 %copy-start.19 = (bf16[64,1024]{1,0:T(8,128)(2,1)}, bf16[64,1024]{1,0:T(8,128)(2,1)S(1)}, u32[]{:S(2)}) copy-start(bf16[64,1024]{1,0:T(8,128)(2,1)S(1)} %collective-permute-done.40.refs_6_) | copy-start | bytes 393220
  52.4 7.5 %collective-permute-start.3 = (bf16[112,768]{1,0:T(8,128)(2,1)}, bf16[112,768]{1,0:T(8,128)(2,1)S(1)}, u32[]{:S(2)}, u32[]{:S(2)}) collective-permute-start(bf16[112,768]{1,0:T(8,128)(2,1)} %get-tuple-element.33.refs_10_), channel_id=1, source_target_pairs={{0,16},{8,24},{16,0},{24,8},{1,17},{9,25},{17,1},{25,9},{2,18},{10... | collective-permute-start | bytes 516104 | tf_op jit(solution)/shard_map/ppermute | solution.py:300
  53.0 6.9 %collective-permute-start.21 = (bf16[128,768]{1,0:T(8,128)(2,1)}, bf16[128,768]{1,0:T(8,128)(2,1)S(1)}, u32[]{:S(2)}, u32[]{:S(2)}) collective-permute-start(bf16[128,768]{1,0:T(8,128)(2,1)} %get-tuple-element.35.refs_8_), channel_id=1, source_target_pairs={{0,8},{8,0},{16,24},{24,16},{1,9},{9,1},{17,25},{25,17},{2,10},{10... | collective-permute-start | bytes 589832 | tf_op jit(solution)/shard_map/ppermute | solution.py:300
  53.1 106.2 %copy-start.4 = (bf16[64,2048]{1,0:T(8,128)(2,1)}, bf16[64,2048]{1,0:T(8,128)(2,1)S(1)}, u32[]{:S(2)}) copy-start(bf16[64,2048]{1,0:T(8,128)(2,1)S(1)} %divide_convert_fusion.refs_8_) | copy-start | bytes 786436
  53.7 19.3 %collective-permute-start.43 = (bf16[64,2048]{1,0:T(8,128)(2,1)S(1)}, bf16[64,2048]{1,0:T(8,128)(2,1)}, u32[]{:S(2)}, u32[]{:S(2)}) collective-permute-start(bf16[64,2048]{1,0:T(8,128)(2,1)S(1)} %divide_convert_fusion.refs_8_), channel_id=1, source_target_pairs={{0,16},{8,24},{16,0},{24,8},{1,17},{9,25},{17,1},{25,9},{2,18},{10... | collective-permute-start | bytes 786440 | tf_op jit(solution)/shard_map/ppermute | solution.py:300
  59.9 13.2 %collective-permute-start.42 = (bf16[64,2048]{1,0:T(8,128)(2,1)S(1)}, bf16[64,2048]{1,0:T(8,128)(2,1)S(1)}, u32[]{:S(2)}, u32[]{:S(2)}) collective-permute-start(bf16[64,2048]{1,0:T(8,128)(2,1)S(1)} %divide_convert_fusion.refs_8_), channel_id=1, source_target_pairs={{0,8},{8,0},{16,24},{24,16},{1,9},{9,1},{17,25},{25,17},{2,10},{10... | collective-permute-start | bytes 786440 | tf_op jit(solution)/shard_map/ppermute | solution.py:300
  59.9 8.9 %collective-permute-start.7 = (bf16[128,768]{1,0:T(8,128)(2,1)}, bf16[128,768]{1,0:T(8,128)(2,1)S(1)}, u32[]{:S(2)}, u32[]{:S(2)}) collective-permute-start(bf16[128,768]{1,0:T(8,128)(2,1)} %get-tuple-element.35.refs_8_), channel_id=1, source_target_pairs={{0,16},{8,24},{16,0},{24,8},{1,17},{9,25},{17,1},{25,9},{2,18},{10... | collective-permute-start | bytes 589832 | tf_op jit(solution)/shard_map/ppermute | solution.py:300
  68.8 12.3 %collective-permute-start.28 = (bf16[768,256]{1,0:T(8,128)(2,1)}, bf16[768,256]{1,0:T(8,128)(2,1)}, u32[]{:S(2)}, u32[]{:S(2)}) collective-permute-start(bf16[768,256]{1,0:T(8,128)(2,1)} %get-tuple-element.40.refs_0_), channel_id=1, source_target_pairs={{0,16},{8,24},{16,0},{24,8},{1,17},{9,25},{17,1},{25,9},{2,18},{10... | collective-permute-start | bytes 1179656 | tf_op jit(solution)/shard_map/ppermute | solution.py:300
  69.4 11.8 %collective-permute-start.27 = (bf16[768,256]{1,0:T(8,128)(2,1)}, bf16[768,256]{1,0:T(8,128)(2,1)}, u32[]{:S(2)}, u32[]{:S(2)}) collective-permute-start(bf16[768,256]{1,0:T(8,128)(2,1)} %get-tuple-element.40.refs_0_), channel_id=1, source_target_pairs={{0,8},{8,0},{16,24},{24,16},{1,9},{9,1},{17,25},{25,17},{2,10},{10... | collective-permute-start | bytes 1179656 | tf_op jit(solution)/shard_map/ppermute | solution.py:300
  70.1 3.5 %collective-permute-start.41 = (bf16[64,1024]{1,0:T(8,128)(2,1)S(1)}, bf16[64,1024]{1,0:T(8,128)(2,1)S(1)}, u32[]{:S(2)}, u32[]{:S(2)}) collective-permute-start(bf16[64,1024]{1,0:T(8,128)(2,1)S(1)} %collective-permute-done.40.refs_6_), channel_id=1, source_target_pairs={{0,8},{8,0},{16,24},{24,16},{1,9},{9,1},{17,25},{25,17},{2,10},{10... | collective-permute-start | bytes 393224 | tf_op jit(solution)/shard_map/ppermute | solution.py:300
  73.0 10.1 %collective-permute-start.18 = (bf16[256,768]{1,0:T(8,128)(2,1)}, bf16[256,768]{1,0:T(8,128)(2,1)S(1)}, u32[]{:S(2)}, u32[]{:S(2)}) collective-permute-start(bf16[256,768]{1,0:T(8,128)(2,1)} %next.1.refs_2_), channel_id=1, source_target_pairs={{0,8},{8,0},{16,24},{24,16},{1,9},{9,1},{17,25},{25,17},{2,10},{10... | collective-permute-start | bytes 1179656 | tf_op jit(solution)/shard_map/ppermute | solution.py:300
  73.1 10.8 %collective-permute-start.17 = (bf16[256,768]{1,0:T(8,128)(2,1)S(1)}, bf16[256,768]{1,0:T(8,128)(2,1)}, u32[]{:S(2)}, u32[]{:S(2)}) collective-permute-start(bf16[256,768]{1,0:T(8,128)(2,1)S(1)} %copy-done.7), channel_id=1, source_target_pairs={{0,8},{8,0},{16,24},{24,16},{1,9},{9,1},{17,25},{25,17},{2,10},{10... | collective-permute-start | bytes 1179656 | tf_op jit(solution)/shard_map/ppermute | solution.py:300
  73.8 64.1 %copy-start.21 = (bf16[64,1024]{1,0:T(8,128)(2,1)}, bf16[64,1024]{1,0:T(8,128)(2,1)S(1)}, u32[]{:S(2)}) copy-start(bf16[64,1024]{1,0:T(8,128)(2,1)S(1)} %collective-permute-done.41.refs_7_) | copy-start | bytes 393220
  73.8 64.1 %collective-permute-start.11 = (bf16[768,768]{1,0:T(8,128)(2,1)}, bf16[768,768]{1,0:T(8,128)(2,1)S(1)}, u32[]{:S(2)}, u32[]{:S(2)}) collective-permute-start(bf16[768,768]{1,0:T(8,128)(2,1)} %get-tuple-element.37.refs_4_), channel_id=1, source_target_pairs={{0,16},{8,24},{16,0},{24,8},{1,17},{9,25},{17,1},{25,9},{2,18},{10... | collective-permute-start | bytes 3538952 | tf_op jit(solution)/shard_map/ppermute | solution.py:300
  81.1 33.6 %collective-permute-start.15 = (bf16[256,768]{1,0:T(8,128)(2,1)}, bf16[256,768]{1,0:T(8,128)(2,1)S(1)}, u32[]{:S(2)}, u32[]{:S(2)}) collective-permute-start(bf16[256,768]{1,0:T(8,128)(2,1)} %next.1.refs_2_), channel_id=1, source_target_pairs={{0,16},{8,24},{16,0},{24,8},{1,17},{9,25},{17,1},{25,9},{2,18},{10... | collective-permute-start | bytes 1179656 | tf_op jit(solution)/shard_map/ppermute | solution.py:300
  81.2 42.1 %collective-permute-start.13 = (bf16[256,768]{1,0:T(8,128)(2,1)S(1)}, bf16[256,768]{1,0:T(8,128)(2,1)}, u32[]{:S(2)}, u32[]{:S(2)}) collective-permute-start(bf16[256,768]{1,0:T(8,128)(2,1)S(1)} %copy-done.7), channel_id=1, source_target_pairs={{0,16},{8,24},{16,0},{24,8},{1,17},{9,25},{17,1},{25,9},{2,18},{10... | collective-permute-start | bytes 1179656 | tf_op jit(solution)/shard_map/ppermute | solution.py:300
  83.2 54.1 %collective-permute-start.31 = (bf16[1280,256]{1,0:T(8,128)(2,1)S(1)}, bf16[1280,256]{1,0:T(8,128)(2,1)}, u32[]{:S(2)}, u32[]{:S(2)}) collective-permute-start(bf16[1280,256]{1,0:T(8,128)(2,1)S(1)} %copy-done.5), channel_id=1, source_target_pairs={{0,16},{8,24},{16,0},{24,8},{1,17},{9,25},{17,1},{25,9},{2,18},{10... | collective-permute-start | bytes 1966088 | tf_op jit(solution)/shard_map/ppermute | solution.py:300
  83.9 53.4 %collective-permute-start.30 = (bf16[1280,256]{1,0:T(8,128)(2,1)S(1)}, bf16[1280,256]{1,0:T(8,128)(2,1)S(1)}, u32[]{:S(2)}, u32[]{:S(2)}) collective-permute-start(bf16[1280,256]{1,0:T(8,128)(2,1)S(1)} %copy-done.5), channel_id=1, source_target_pairs={{0,8},{8,0},{16,24},{24,16},{1,9},{9,1},{17,25},{25,17},{2,10},{10... | collective-permute-start | bytes 1966088 | tf_op jit(solution)/shard_map/ppermute | solution.py:300
  114.7 8.5 %collective-permute-start.38 = (f32[64,1024]{1,0:T(8,128)}, f32[64,1024]{1,0:T(8,128)S(1)}, u32[]{:S(2)}, u32[]{:S(2)}) collective-permute-start(f32[64,1024]{1,0:T(8,128)} %collective-permute-done.37.refs_2_), channel_id=1, source_target_pairs={{0,8},{8,0},{16,24},{24,16},{1,9},{9,1},{17,25},{25,17},{2,10},{10... | collective-permute-start | bytes 786440 | tf_op jit(solution)/shard_map/ppermute | solution.py:300
  123.3 1.7 collective-permute-start.44
  123.3 29.1 %collective-permute-start.9 = (bf16[512,768]{1,0:T(8,128)(2,1)}, bf16[512,768]{1,0:T(8,128)(2,1)}, u32[]{:S(2)}, u32[]{:S(2)}) collective-permute-start(bf16[512,768]{1,0:T(8,128)(2,1)} %get-tuple-element.36.refs_6_), channel_id=1, source_target_pairs={{0,16},{8,24},{16,0},{24,8},{1,17},{9,25},{17,1},{25,9},{2,18},{10... | collective-permute-start | bytes 2359304 | tf_op jit(solution)/shard_map/ppermute | solution.py:300
  125.0 27.4 %collective-permute-start.20 = (bf16[512,768]{1,0:T(8,128)(2,1)}, bf16[512,768]{1,0:T(8,128)(2,1)}, u32[]{:S(2)}, u32[]{:S(2)}) collective-permute-start(bf16[512,768]{1,0:T(8,128)(2,1)} %get-tuple-element.36.refs_6_), channel_id=1, source_target_pairs={{0,8},{8,0},{16,24},{24,16},{1,9},{9,1},{17,25},{25,17},{2,10},{10... | collective-permute-start | bytes 2359304 | tf_op jit(solution)/shard_map/ppermute | solution.py:300
  137.3 1.9 %collective-permute-start.29 = (bf16[768,256]{1,0:T(8,128)(2,1)}, bf16[768,256]{1,0:T(8,128)(2,1)S(1)}, u32[]{:S(2)}, u32[]{:S(2)}) collective-permute-start(bf16[768,256]{1,0:T(8,128)(2,1)} %collective-permute-done.28.refs_2_), channel_id=1, source_target_pairs={{0,8},{8,0},{16,24},{24,16},{1,9},{9,1},{17,25},{25,17},{2,10},{10... | collective-permute-start | bytes 1179656 | tf_op jit(solution)/shard_map/ppermute | solution.py:300
  137.3 19.4 %collective-permute-start.19 = (bf16[768,768]{1,0:T(8,128)(2,1)}, bf16[768,768]{1,0:T(8,128)(2,1)}, u32[]{:S(2)}, u32[]{:S(2)}) collective-permute-start(bf16[768,768]{1,0:T(8,128)(2,1)} %get-tuple-element.37.refs_4_), channel_id=1, source_target_pairs={{0,8},{8,0},{16,24},{24,16},{1,9},{9,1},{17,25},{25,17},{2,10},{10... | collective-permute-start | bytes 3538952 | tf_op jit(solution)/shard_map/ppermute | solution.py:300
  138.2 19.5 %collective-permute-start.12 = (bf16[768,768]{1,0:T(8,128)(2,1)S(1)}, bf16[768,768]{1,0:T(8,128)(2,1)S(1)}, u32[]{:S(2)}, u32[]{:S(2)}) collective-permute-start(bf16[768,768]{1,0:T(8,128)(2,1)S(1)} %collective-permute-done.11.refs_0_), channel_id=1, source_target_pairs={{0,8},{8,0},{16,24},{24,16},{1,9},{9,1},{17,25},{25,17},{2,10},{10... | collective-permute-start | bytes 3538952 | tf_op jit(solution)/shard_map/ppermute | solution.py:300
  139.3 13.7 %collective-permute-start.16 = (bf16[256,768]{1,0:T(8,128)(2,1)S(1)}, bf16[256,768]{1,0:T(8,128)(2,1)S(1)}, u32[]{:S(2)}, u32[]{:S(2)}) collective-permute-start(bf16[256,768]{1,0:T(8,128)(2,1)S(1)} %collective-permute-done.15.refs_2_), channel_id=1, source_target_pairs={{0,8},{8,0},{16,24},{24,16},{1,9},{9,1},{17,25},{25,17},{2,10},{10... | collective-permute-start | bytes 1179656 | tf_op jit(solution)/shard_map/ppermute | solution.py:300
  152.4 25.4 %collective-permute-start.10 = (bf16[512,768]{1,0:T(8,128)(2,1)}, bf16[512,768]{1,0:T(8,128)(2,1)}, u32[]{:S(2)}, u32[]{:S(2)}) collective-permute-start(bf16[512,768]{1,0:T(8,128)(2,1)} %collective-permute-done.9.refs_0_), channel_id=1, source_target_pairs={{0,8},{8,0},{16,24},{24,16},{1,9},{9,1},{17,25},{25,17},{2,10},{10... | collective-permute-start | bytes 2359304 | tf_op jit(solution)/shard_map/ppermute | solution.py:300
  152.4 4.7 %collective-permute-start.32 = (bf16[1280,256]{1,0:T(8,128)(2,1)}, bf16[1280,256]{1,0:T(8,128)(2,1)}, u32[]{:S(2)}, u32[]{:S(2)}) collective-permute-start(bf16[1280,256]{1,0:T(8,128)(2,1)} %collective-permute-done.31.refs_6_), channel_id=1, source_target_pairs={{0,8},{8,0},{16,24},{24,16},{1,9},{9,1},{17,25},{25,17},{2,10},{10... | collective-permute-start | bytes 1966088 | tf_op jit(solution)/shard_map/ppermute | solution.py:300
  153.7 2.9 %collective-permute-start.14 = (bf16[256,768]{1,0:T(8,128)(2,1)}, bf16[256,768]{1,0:T(8,128)(2,1)}, u32[]{:S(2)}, u32[]{:S(2)}) collective-permute-start(bf16[256,768]{1,0:T(8,128)(2,1)} %collective-permute-done.13.refs_0_), channel_id=1, source_target_pairs={{0,8},{8,0},{16,24},{24,16},{1,9},{9,1},{17,25},{25,17},{2,10},{10... | collective-permute-start | bytes 1179656 | tf_op jit(solution)/shard_map/ppermute | solution.py:300
  156.6 24.6 %collective-permute-start.4 = (bf16[112,768]{1,0:T(8,128)(2,1)S(1)}, bf16[112,768]{1,0:T(8,128)(2,1)S(1)}, u32[]{:S(2)}, u32[]{:S(2)}) collective-permute-start(bf16[112,768]{1,0:T(8,128)(2,1)S(1)} %collective-permute-done.3.refs_0_), channel_id=1, source_target_pairs={{0,8},{8,0},{16,24},{24,16},{1,9},{9,1},{17,25},{25,17},{2,10},{10... | collective-permute-start | bytes 516104 | tf_op jit(solution)/shard_map/ppermute | solution.py:300
  156.7 23.7 %collective-permute-start.8 = (bf16[128,768]{1,0:T(8,128)(2,1)S(1)}, bf16[128,768]{1,0:T(8,128)(2,1)S(1)}, u32[]{:S(2)}, u32[]{:S(2)}) collective-permute-start(bf16[128,768]{1,0:T(8,128)(2,1)S(1)} %collective-permute-done.7.refs_0_), channel_id=1, source_target_pairs={{0,8},{8,0},{16,24},{24,16},{1,9},{9,1},{17,25},{25,17},{2,10},{10... | collective-permute-start | bytes 589832 | tf_op jit(solution)/shard_map/ppermute | solution.py:300
  157.1 24.0 %collective-permute-start.5 = (bf16[16,768]{1,0:T(8,128)(2,1)}, bf16[16,768]{1,0:T(8,128)(2,1)S(1)}, u32[]{:S(2)}, u32[]{:S(2)}) collective-permute-start(bf16[16,768]{1,0:T(8,128)(2,1)} %get-tuple-element.34.refs_12_), channel_id=1, source_target_pairs={{0,16},{8,24},{16,0},{24,8},{1,17},{9,25},{17,1},{25,9},{2,18},{10... | collective-permute-start | bytes 73736 | tf_op jit(solution)/shard_map/ppermute | solution.py:300
  157.7 23.4 %collective-permute-start.6 = (bf16[16,768]{1,0:T(8,128)(2,1)}, bf16[16,768]{1,0:T(8,128)(2,1)S(1)}, u32[]{:S(2)}, u32[]{:S(2)}) collective-permute-start(bf16[16,768]{1,0:T(8,128)(2,1)} %get-tuple-element.34.refs_12_), channel_id=1, source_target_pairs={{0,24},{8,16},{16,8},{24,0},{1,25},{9,17},{17,9},{25,1},{2,26},{10... | collective-permute-start | bytes 73736 | tf_op jit(solution)/shard_map/ppermute | solution.py:300
  (27 other events, 340.5 us)
